TPU v7x, 8 devices: a whole 2x2x1 slice. The times are simulated.
8 devices in a mesh: dp: 2 (over z, y), tp: 4 (over x, core).
Axes of the slice: x: 2, y: 2, z: 1, core: 2. Of those that a mesh axis runs over, the one named last changes fastest.
Arguments:
- x_in: bfloat16 [256, 4096], P('dp'), parts along dimension 0
- tok_pos: int32 [256], P('dp'), parts along dimension 0
- self_k: bfloat16 [256, 64, 64, 64], P('dp', None, 'tp'), parts along dimension 0
- self_v: bfloat16 [256, 64, 64, 64], P('dp', None, 'tp'), parts along dimension 0
- cross_k: bfloat16 [256, 128, 64, 64], P('dp', None, 'tp'), parts along dimension 0
- cross_v: bfloat16 [256, 128, 64, 64], P('dp', None, 'tp'), parts along dimension 0
- enc_mask: int32 [256, 128], P('dp'), parts along dimension 0
- rel_bias: float32 [32, 64], P(None, 'tp')
- w_q: bfloat16 [4096, 4096], P(None, 'tp')
- w_k: bfloat16 [4096, 4096], P(None, 'tp')
- w_v: bfloat16 [4096, 4096], P(None, 'tp')
- w_o: bfloat16 [4096, 4096], P('tp')
- cross_q: bfloat16 [4096, 4096], P(None, 'tp')
- cross_o: bfloat16 [4096, 4096], P('tp')
- w_gate: bfloat16 [4096, 10240], P(None, 'tp')
- w_up: bfloat16 [4096, 10240], P(None, 'tp')
- w_down: bfloat16 [10240, 4096], P('tp')
- norm_self: bfloat16 [4096], replicated
- norm_cross: bfloat16 [4096], replicated
- norm_mlp: bfloat16 [4096], replicated
Outputs:
- output 1: bfloat16 [256, 4096], P('dp'), parts along dimension 0
- output 2: bfloat16 [256, 64, 64, 64], P('dp', None, 'tp'), parts along dimension 0
- output 3: bfloat16 [256, 64, 64, 64], P('dp', None, 'tp'), parts along dimension 0
There are 2 independent parts. A program takes and returns all parts, laid end to end along the dimension named above; an argument that names none is the same for every part.
All inputs are finite; a program needn't handle non-finite values.
Results may differ from a plain program's by a relative error of at most 0.0181668.
Values are sent between devices in bfloat16 or wider.
A program may use at most 1 GiB of HBM per device.

v0:
```python
import math
import jax
import jax.numpy as jnp
from jax import lax
from jax.sharding import PartitionSpec as P

BUCKET_EDGES = tuple(int(math.ceil(16.0 * 8.0 ** (bucket_step / 16.0))) for bucket_step in range(1, 16))
NEG_FILL = -1e30


def rms_norm(values, norm_scale):
    inv_rms = lax.rsqrt(jnp.mean(values * values, axis=-1, keepdims=True) + 1e-6)
    return (values * inv_rms * norm_scale.astype(jnp.float32)).astype(jnp.bfloat16)


def project(normed, weight):
    return jnp.dot(normed, weight, preferred_element_type=jnp.float32).astype(jnp.bfloat16)


def rel_bucket(distance):
    bucket_edges = jnp.array(BUCKET_EDGES, dtype=jnp.int32)
    far_bucket = 16 + jnp.sum((distance[..., None] >= bucket_edges).astype(jnp.int32), axis=-1)
    return jnp.where(distance < 16, distance, far_bucket)


def attend(queries, keys_all, values_all, extra):
    scores = jnp.einsum('bhk,bthk->bht', queries, keys_all, preferred_element_type=jnp.float32) + extra
    probs_bf = jax.nn.softmax(scores, axis=-1).astype(jnp.bfloat16)
    mixed_out = jnp.einsum('bht,bthk->bhk', probs_bf, values_all, preferred_element_type=jnp.float32)
    return mixed_out.astype(jnp.bfloat16)


def self_terms(tok_pos, rel_bias, t_len):
    key_index = jnp.arange(t_len)
    at_pos = (key_index[None, :] == tok_pos[:, None])[:, :, None, None]
    distance = jnp.maximum(tok_pos[:, None] - key_index[None, :], 0)
    bias_rows = jnp.swapaxes(jnp.take(rel_bias, rel_bucket(distance), axis=0), 1, 2)
    causal = (key_index[None, :] <= tok_pos[:, None])[:, None, :]
    return at_pos, jnp.where(causal, bias_rows, NEG_FILL)


def solution(mesh):
    def tp_sum(partial_out):
        return lax.psum(partial_out.astype(jnp.bfloat16), 'tp').astype(jnp.float32)

    def local_layer(x_in, tok_pos, self_k, self_v, cross_k, cross_v, enc_mask, rel_bias, w_q, w_k, w_v, w_o, cross_q, cross_o, w_gate, w_up, w_down, norm_self, norm_cross, norm_mlp):
        row_count, t_len, head_count, head_dim = self_k.shape
        head_shape = (row_count, head_count, head_dim)
        flat_dim = head_count * head_dim
        residual = x_in.astype(jnp.float32)
        normed = rms_norm(residual, norm_self)
        queries = project(normed, w_q).reshape(head_shape)
        new_keys = project(normed, w_k).reshape(head_shape)
        new_values = project(normed, w_v).reshape(head_shape)
        at_pos, self_extra = self_terms(tok_pos, rel_bias, t_len)
        new_self_k = jnp.where(at_pos, new_keys[:, None], self_k)
        new_self_v = jnp.where(at_pos, new_values[:, None], self_v)
        mixed_self = attend(queries, new_self_k, new_self_v, self_extra)
        residual = residual + tp_sum(jnp.dot(mixed_self.reshape(row_count, flat_dim), w_o, preferred_element_type=jnp.float32))
        normed = rms_norm(residual, norm_cross)
        cross_queries = project(normed, cross_q).reshape(head_shape)
        cross_extra = jnp.where(enc_mask[:, None, :] != 0, 0.0, NEG_FILL)
        mixed_cross = attend(cross_queries, cross_k, cross_v, cross_extra)
        residual = residual + tp_sum(jnp.dot(mixed_cross.reshape(row_count, flat_dim), cross_o, preferred_element_type=jnp.float32))
        normed = rms_norm(residual, norm_mlp)
        gate_pre = jnp.dot(normed, w_gate, preferred_element_type=jnp.float32)
        up_pre = jnp.dot(normed, w_up, preferred_element_type=jnp.float32)
        hidden = (jax.nn.gelu(gate_pre, approximate=True) * up_pre).astype(jnp.bfloat16)
        residual = residual + tp_sum(jnp.dot(hidden, w_down, preferred_element_type=jnp.float32))
        return residual.astype(jnp.bfloat16), new_self_k, new_self_v

    cache_spec = P('dp', None, 'tp', None)
    split_cols = P(None, 'tp')
    split_rows = P('tp', None)
    in_specs = (P('dp', None), P('dp'), cache_spec, cache_spec, cache_spec, cache_spec, P('dp', None), split_cols, split_cols, split_cols, split_cols, split_rows, split_cols, split_rows, split_cols, split_cols, split_rows, P(None), P(None), P(None))
    out_specs = (P('dp', None), cache_spec, cache_spec)
    return jax.shard_map(local_layer, mesh=mesh, in_specs=in_specs, out_specs=out_specs, check_vma=False)
```

profile of v0, /device:TPU:0, one launch (start us, length us, event | category | flops | bytes accessed | tf_op | source)
XLA Modules:
  0.0 304.1 jit_solution(5647253601376462065)
XLA Ops:
  7.9 0.8 convert_reduce_fusion
  8.7 0.7 iota_compare_fusion
  9.3 0.7 compare_select_fusion
  10.0 1.5 fusion.5
  11.5 0.7 convert_element_type.73
  12.3 0.8 copy.41
  13.5 5.1 %convolution_convert_fusion.5 = bf16[128,1024]{1,0:T(8,128)(2,1)S(1)} fusion(bf16[4096,1024]{1,0:T(8,128)(2,1)} %param.30, bf16[128,4096]{1,0:T(8,128)(2,1)} %param.21, f32[4096]{0:T(1024)S(1)} %convert_element_type.73, f32[128]{0:T(128)S(1)} %add_rsqrt_fusion.2), kind=kOutput, calls=%fused_computation.46 | convolution fusion | flops 1075970048 | bytes 9716224 | tf_op jit(solution)/shard_map/dot_general | solution.py:17
  18.8 4.7 %convolution_convert_fusion.4 = bf16[128,1024]{1,0:T(8,128)(2,1)S(1)} fusion(bf16[4096,1024]{1,0:T(8,128)(2,1)} %param.31, bf16[128,4096]{1,0:T(8,128)(2,1)S(1)} %copy-done, f32[4096]{0:T(1024)S(1)} %convert_element_type.73, f32[128]{0:T(128)S(1)} %add_rsqrt_fusion.2), kind=kOutput, calls=%fused_computation.45 | convolution fusion | flops 1075970048 | bytes 9716224 | tf_op jit(solution)/shard_map/dot_general | solution.py:17
  23.6 4.7 %convolution_convert_fusion.6 = bf16[128,1024]{1,0:T(8,128)(2,1)S(1)} fusion(bf16[4096,1024]{1,0:T(8,128)(2,1)} %param.29, bf16[128,4096]{1,0:T(8,128)(2,1)S(1)} %copy-done, f32[4096]{0:T(1024)S(1)} %convert_element_type.73, f32[128]{0:T(128)S(1)} %add_rsqrt_fusion.2), kind=kOutput, calls=%fused_computation.47 | convolution fusion | flops 1075970048 | bytes 9716224 | tf_op jit(solution)/shard_map/dot_general | solution.py:17
  28.5 18.8 %multiply_reduce_fusion.1 = (f32[128,16,64]{0,1,2:T(8,128)S(1)}, bf16[128,64,16,64]{0,3,2,1:T(8,128)(2,1)}) fusion(f32[128,16,64]{0,2,1:T(8,128)S(1)} %bitcast_convert_fusion.1, bf16[128,64,16,64]{0,3,2,1:T(8,128)(2,1)} %param.23, bf16[128,16,64]{0,2,1:T(8,128)(2,1)S(1)} %bitcast.61, pred[128,64]{0,1:T(8,128)(4,1)S(1)} %get-tuple-element.9), kind=kLoop, calls=%fused_computation.6 | loop fusion | flops 33423360 | bytes 34873344
  47.4 4.4 %copy.50 = f32[128,16,64]{1,2,0:T(8,128)} copy(f32[128,16,64]{0,1,2:T(8,128)S(1)} %get-tuple-element.5) | data formatting | bytes 1048576 | tf_op jit(solution)/shard_map/bhk,bthk->bht/dot_general | solution.py:27
  51.7 27.7 %gather_fusion = f32[8192,16]{1,0:T(8,128)} fusion(f32[32,16]{1,0:T(8,128)S(1)} %copy.41, s32[8192]{0:T(1024)S(1)} %broadcast_clamp_fusion), kind=kCustom, calls=%fused_computation | custom fusion | bytes 1081344 | tf_op jit(solution)/shard_map/jit(_take)/gather | solution.py:37
  79.4 6.9 %fusion.8 = f32[128,16,64]{1,2,0:T(8,128)} fusion(f32[128,16,64]{1,2,0:T(8,128)} %copy.50, f32[128,64,16]{2,1,0:T(8,128)} %bitcast.57, pred[128,64]{1,0:T(8,128)(4,1)S(1)} %copy.39, pred[128,64]{1,0:T(8,128)(4,1)S(1)} %copy.38), kind=kOutput, calls=%fused_computation.30 | output fusion | flops 921726 | bytes 1589248 | tf_op jit(solution)/shard_map/div | solution.py:28
  86.3 3.7 %copy.62 = f32[128,16,64]{0,1,2:T(8,128)S(1)} copy(f32[128,16,64]{1,2,0:T(8,128)} %fusion.8) | data formatting | bytes 1048576
  90.0 17.1 %multiply_reduce_fusion = (bf16[128,16,64]{0,2,1:T(8,128)(2,1)S(1)}, bf16[128,64,16,64]{0,3,2,1:T(8,128)(2,1)}) fusion(f32[128,16,64]{0,1,2:T(8,128)S(1)} %copy.62, bf16[128,64,16,64]{0,3,2,1:T(8,128)(2,1)} %param.24, bf16[128,16,64]{0,2,1:T(8,128)(2,1)S(1)} %bitcast.60, pred[128,64]{0,1:T(8,128)(4,1)S(1)} %get-tuple-element.9), kind=kLoop, calls=%fused_computation.5 | loop fusion | flops 33423360 | bytes 34611200 | tf_op jit(solution)/shard_map/bht,bthk->bhk/dot_general | solution.py:29
  107.1 5.7 %convolution_convert_fusion.1 = bf16[128,4096]{1,0:T(8,128)(2,1)} fusion(bf16[128,1024]{0,1:T(8,128)(2,1)S(1)} %bitcast.58, bf16[1024,4096]{1,0:T(8,128)(2,1)} %param.32), kind=kOutput, calls=%fused_computation.10 | convolution fusion | flops 1074266112 | bytes 9699328 | tf_op jit(solution)/shard_map/dot_general | solution.py:59
  113.1 33.6 %all-reduce.4.cloned.1.call-done = bf16[128,4096]{1,0:T(8,128)(2,1)} async-done(((bf16[128,4096]{1,0:T(8,128)(2,1)}), bf16[128,4096]{1,0:T(8,128)(2,1)}) %all-reduce.4.cloned.1.call-update) | async-done | bytes 1048592 | tf_op jit(solution)/shard_map/psum | solution.py:44
  146.7 1.6 multiply_reduce_fusion.3
  148.3 5.5 %convolution_convert_fusion.3 = bf16[128,1024]{1,0:T(8,128)(2,1)S(1)} fusion(bf16[4096,1024]{1,0:T(8,128)(2,1)} %param.33, bf16[128,4096]{1,0:T(8,128)(2,1)} %all-reduce.4.cloned.1.call-done, bf16[128,4096]{1,0:T(8,128)(2,1)S(1)} %copy-done, f32[4096]{0:T(1024)S(1)} %convert_element_type.83, f32[128]{0:T(128)S(1)} %add_rsqrt_fusion.1), kind=kOutput, calls=%fused_computation.44 | convolution fusion | flops 1077018624 | bytes 10764800 | tf_op jit(solution)/shard_map/dot_general | solution.py:17
  154.0 0.9 copy.57
  154.9 14.4 %fusion.35 = f32[128,16,1,128]{3,2,1,0:T(1,128)S(1)} fusion(bf16[128,16,64,1]{2,3,1,0:T(2,128)(2,1)S(1)} %copy.57, bf16[128,128,16,64]{1,3,2,0:T(8,128)(2,1)} %param.25), kind=kOutput, calls=%fused_computation.73 | convolution fusion | flops 33554432 | bytes 34865152 | tf_op jit(solution)/shard_map/bhk,bthk->bht/dot_general | solution.py:27
  169.3 1.4 fusion.21
  170.8 22.0 %fusion.22 = bf16[128,16,1,64]{3,2,1,0:T(2,128)(2,1)S(1)} fusion(bf16[128,128,16,64]{1,3,2,0:T(8,128)(2,1)} %param.26, bf16[128,16,128,1]{2,1,0,3:T(8,128)(2,1)} %fusion.21), kind=kOutput, calls=%fused_computation.48 | convolution fusion | flops 33554432 | bytes 34340864 | tf_op jit(solution)/shard_map/bht,bthk->bhk/dot_general | solution.py:29
  192.8 0.8 copy.60
  193.6 5.7 %convolution_convert_fusion = bf16[128,4096]{1,0:T(8,128)(2,1)} fusion(bf16[128,1024]{0,1:T(8,128)(2,1)S(1)} %bitcast.59, bf16[1024,4096]{1,0:T(8,128)(2,1)} %param.34), kind=kOutput, calls=%fused_computation.9 | convolution fusion | flops 1074266112 | bytes 9699328 | tf_op jit(solution)/shard_map/dot_general | solution.py:64
  199.6 31.0 %all-reduce.6.cloned.1.call-done = bf16[128,4096]{1,0:T(8,128)(2,1)} async-done(((bf16[128,4096]{1,0:T(8,128)(2,1)}), bf16[128,4096]{1,0:T(8,128)(2,1)}) %all-reduce.6.cloned.1.call-update) | async-done | bytes 1048592 | tf_op jit(solution)/shard_map/psum | solution.py:44
  230.6 1.8 multiply_reduce_fusion.2
  232.4 1.8 multiply_convert_fusion
  234.2 10.9 %fusion.36 = f32[128,2560]{1,0:T(8,128)} fusion(bf16[128,4096]{1,0:T(8,128)(2,1)S(1)} %multiply_convert_fusion, bf16[4096,2560]{1,0:T(8,128)(2,1)} %param.35), kind=kOutput, calls=%fused_computation.74 | convolution fusion | flops 2684354560 | bytes 23330816 | tf_op jit(solution)/shard_map/dot_general | solution.py:66
  245.1 18.0 %convolution_convert_fusion.2 = bf16[128,4096]{1,0:T(8,128)(2,1)} fusion(bf16[2560,4096]{1,0:T(8,128)(2,1)} %param.37, bf16[128,4096]{1,0:T(8,128)(2,1)S(1)} %multiply_convert_fusion, bf16[4096,2560]{1,0:T(8,128)(2,1)} %param.36, f32[128,2560]{1,0:T(8,128)} %fusion.36), kind=kOutput, calls=%fused_computation.11 | convolution fusion | flops 5372510208 | bytes 45350912 | tf_op jit(solution)/shard_map/dot_general | solution.py:69
  263.1 31.3 %all-reduce.8.cloned.1.call-done = bf16[128,4096]{1,0:T(8,128)(2,1)} async-done(((bf16[128,4096]{1,0:T(8,128)(2,1)}), bf16[128,4096]{1,0:T(8,128)(2,1)}) %all-reduce.8.cloned.1.call-update) | async-done | bytes 1048592 | tf_op jit(solution)/shard_map/psum | solution.py:44
  294.4 3.2 %add_convert_fusion = bf16[128,4096]{1,0:T(8,128)(2,1)} fusion(bf16[128,4096]{1,0:T(8,128)(2,1)} %all-reduce.8.cloned.1.call-done, bf16[128,4096]{1,0:T(8,128)(2,1)} %all-reduce.6.cloned.1.call-done, bf16[128,4096]{1,0:T(8,128)(2,1)S(1)} %copy-done.1, bf16[128,4096]{1,0:T(8,128)(2,1)S(1)} %copy-done), kind=kLoop, calls=%fused_computation.23 | loop fusion | flops 4194304 | bytes 5242880 | tf_op jit(solution)/shard_map/convert_element_type | solution.py:70
  (33 shorter events, 2.4 us)
Async XLA Ops:
  7.2 139.5 %all-reduce.4.cloned.1.call-start = ((), (), s32[]{:S(2)}) async-start(), calls=%async_computation | async-start | bytes 2097152 | tf_op jit(solution)/shard_map/psum | solution.py:44
  13.5 5.3 %copy-start = (bf16[128,4096]{1,0:T(8,128)(2,1)S(1)}, bf16[128,4096]{1,0:T(8,128)(2,1)}, u32[]{:S(2)}) copy-start(bf16[128,4096]{1,0:T(8,128)(2,1)} %param.21) | copy-start | bytes 3145732
  107.1 6.0 %copy-start.3 = (bf16[4096]{0:T(1024)(128)(2,1)S(1)}, bf16[4096]{0:T(1024)(128)(2,1)}, u32[]{:S(2)}) copy-start(bf16[4096]{0:T(1024)(128)(2,1)} %param.39) | copy-start | bytes 24580
  107.1 6.0 %copy-start.2 = (s32[128,128]{1,0:T(8,128)S(1)}, s32[128,128]{1,0:T(8,128)}, u32[]{:S(2)}) copy-start(s32[128,128]{1,0:T(8,128)} %param.27) | copy-start | bytes 196612
  112.9 117.7 %all-reduce.6.cloned.1.call-start = ((), (), s32[]{:S(2)}) async-start(), calls=%async_computation.1 | async-start | bytes 2097152 | tf_op jit(solution)/shard_map/psum | solution.py:44
  193.6 6.0 %copy-start.4 = (bf16[4096]{0:T(1024)(128)(2,1)S(1)}, bf16[4096]{0:T(1024)(128)(2,1)}, u32[]{:S(2)}) copy-start(bf16[4096]{0:T(1024)(128)(2,1)} %param.40) | copy-start | bytes 24580
  193.6 37.0 %copy-start.1 = (bf16[128,4096]{1,0:T(8,128)(2,1)S(1)}, bf16[128,4096]{1,0:T(8,128)(2,1)}, u32[]{:S(2)}) copy-start(bf16[128,4096]{1,0:T(8,128)(2,1)} %all-reduce.4.cloned.1.call-done) | copy-start | bytes 3145732
  199.3 95.0 %all-reduce.8.cloned.1.call-start = ((), (), s32[]{:S(2)}) async-start(), calls=%async_computation.2 | async-start | bytes 2097152 | tf_op jit(solution)/shard_map/psum | solution.py:44
Sparse Core Ops, SparseCore 0:
  113.0 33.6 all-reduce.3
  199.5 31.0 all-reduce.5
  263.2 31.0 all-reduce.7
where the time goes:
time: 305 us; the launch traced here: 304 us
  matrix products  96.7 us (32%)
  waiting for transfers between devices  95.8 us (31%)
  other arithmetic  57.7 us (19%)
  local copies, waits for them, and re-layouts  39.3 us (13%)
  between operations  14 us (5%)
    psum x3, waiting for transfers between devices, tp_sum(): return lax.psum(partial_out.astype(jnp.bfloat16), 'tp').astype(jnp.float32)  95.8 us
    gather x1, local copies, waits for them, and re-layouts, self_terms(): jnp.take(rel_bias, rel_bucket(distance), axis=0)  27.7 us
    dot_general x1, matrix products, attend(): jnp.einsum('bht,bthk->bhk', probs_bf, values_all, preferred_element_type=...  22 us
    dot_general x4, matrix products, project(): jnp.dot(normed, weight, preferred_element_type=jnp.float32)  19.9 us
    unnamed x2, other arithmetic  18.9 us
    dot_general x1, matrix products, local_layer(): jnp.dot(hidden, w_down, preferred_element_type=jnp.float32)  18 us
    dot_general x1, other arithmetic, attend(): jnp.einsum('bht,bthk->bhk', probs_bf, values_all, preferred_element_type=...  17.1 us
    dot_general x1, matrix products, attend(): jnp.einsum('bhk,bthk->bht', queries, keys_all, preferred_element_type=jnp...  14.4 us
  transfers between devices with their start and end apart: 3, of which 3 were waited for; matrix products, arithmetic and copies ran while one was open for 0% of the time, Pallas kernels for 0%

commit v1 on v0

--- a/solution.py
+++ b/solution.py
@@ -2,10 +2,228 @@
 import jax
 import jax.numpy as jnp
 from jax import lax
+from jax.experimental import pallas as pl
+from jax.experimental.pallas import tpu as pltpu
 from jax.sharding import PartitionSpec as P
 
 BUCKET_EDGES = tuple(int(math.ceil(16.0 * 8.0 ** (bucket_step / 16.0))) for bucket_step in range(1, 16))
 NEG_FILL = -1e30
+F32 = jnp.float32
+BF16 = jnp.bfloat16
+ANY = pl.BlockSpec(memory_space=pl.ANY)
+VMEM = pl.BlockSpec(memory_space=pltpu.VMEM)
+COLS = 256
+T_BLOCK = 8
+
+
+def self_kernel(x_hbm, norm_ref, pos_ref, rel_ref, wq_hbm, wk_hbm, wv_hbm, wo_hbm, k_hbm, v_hbm,
+                part_hbm, newk_hbm, newv_hbm,
+                xbuf, hbuf, wbuf, kvbuf, q_ref, kn_ref, hit_ref, score_ref, acc_ref,
+                x_sem, w_sem, kv_sem, out_sem, part_sem, window):
+    rows, d_model = xbuf.shape
+    n_w = wbuf.shape[0]
+    per_mat = n_w // 3
+    n_chunk = kvbuf.shape[0] // 2
+    n_head, t_len = score_ref.shape[0], score_ref.shape[1]
+    inner = acc_ref.shape[0]
+    d_head = inner // n_head
+    chunk_rows = kvbuf.shape[1]
+    sub = d_head // 16
+    wo_per_slot = wbuf.shape[1] // inner
+    n_wo = wo_hbm.shape[1] // COLS // wo_per_slot
+
+    def w_copy(c):
+        src = (wq_hbm, wk_hbm, wv_hbm)[c // per_mat]
+        return pltpu.make_async_copy(src.at[:, pl.ds((c % per_mat) * COLS, COLS)], wbuf.at[c], w_sem.at[c])
+
+    def kv_copy(i):
+        src = k_hbm if i < n_chunk else v_hbm
+        return pltpu.make_async_copy(src.at[pl.ds((i % n_chunk) * chunk_rows, chunk_rows)], kvbuf.at[i], kv_sem.at[i])
+
+    def wo_copies(i):
+        return [pltpu.make_async_copy(wo_hbm.at[:, pl.ds((i * wo_per_slot + r) * COLS, COLS)],
+                                      wbuf.at[i, pl.ds(r * inner, inner)], w_sem.at[i]) for r in range(wo_per_slot)]
+
+    loads = [[w_copy(c)] for c in range(n_w)] + [[kv_copy(i)] for i in range(2 * n_chunk)] + [wo_copies(i) for i in range(n_wo)]
+    issued = [0]
+
+    def issue(upto):
+        while issued[0] < min(upto, len(loads)):
+            for copy in loads[issued[0]]:
+                copy.start()
+            issued[0] += 1
+
+    x_copy = pltpu.make_async_copy(x_hbm, xbuf, x_sem)
+    x_copy.start()
+    issue(window)
+
+    pos = pos_ref[...]
+    pos16 = jnp.broadcast_to(pos, (16, rows))
+
+    def set_hit(t, carry):
+        hit_ref[t] = jnp.where(pos16 == t, 1.0, 0.0).astype(BF16)
+        return carry
+    lax.fori_loop(0, t_len, set_hit, 0)
+
+    lane = lax.broadcasted_iota(jnp.int32, (n_head, 128), 1)
+    bucket = jnp.full((n_head, 128), 16, jnp.int32)
+    for edge in BUCKET_EDGES:
+        bucket = bucket + (lane >= edge).astype(jnp.int32)
+    bucket = jnp.where(lane < 16, lane, bucket)
+    rel = rel_ref[...]
+    table = jnp.zeros((n_head, 128), F32)
+    for b in range(rel.shape[1]):
+        table = jnp.where(bucket == b, rel[:, b:b + 1], table)
+    acc_ref[0:n_head, :] = table
+
+    x_copy.wait()
+    block = 16
+    norm = norm_ref[0:1, :]
+
+    def norm_rows(i, carry):
+        at = pl.ds(pl.multiple_of(i * block, block), block)
+        r = xbuf[at, :].astype(F32)
+        inv = lax.rsqrt(jnp.mean(r * r, axis=-1, keepdims=True) + 1e-6)
+        hbuf[at, :] = (r * inv * norm).astype(BF16)
+        return carry
+    lax.fori_loop(0, rows // block, norm_rows, 0)
+
+    for c in range(n_w):
+        w_copy(c).wait()
+        issue(c + 1 + window)
+        y = jnp.dot(hbuf[...], wbuf[c], preferred_element_type=F32).astype(BF16).astype(F32).T
+        at = (c % per_mat) * COLS
+        if c < per_mat:
+            q_ref[at:at + COLS, :] = y
+        else:
+            kn_ref[c // per_mat - 1, at:at + COLS, :] = y.astype(BF16)
+
+    def chunk_out(i):
+        dst = newk_hbm if i < n_chunk else newv_hbm
+        return pltpu.make_async_copy(kvbuf.at[i], dst.at[pl.ds((i % n_chunk) * chunk_rows, chunk_rows)], out_sem.at[i])
+
+    for j in range(n_chunk):
+        kv_copy(j).wait()
+        issue(n_w + j + 1 + window)
+
+        def k_head(h, carry):
+            at = pl.multiple_of(h * d_head, d_head)
+            q = q_ref[pl.ds(at, d_head), :]
+            kn = kn_ref[0, pl.ds(at, d_head), :].reshape(sub, 16, rows)
+            rows_out = []
+            for tt in range(T_BLOCK):
+                here = pl.ds(pl.multiple_of(tt * inner + at, d_head), d_head)
+                old = kvbuf[j, here, :].reshape(sub, 16, rows)
+                hit = hit_ref[j * T_BLOCK + tt] != 0
+                new = jnp.where(hit[None], kn, old)
+                kvbuf[j, here, :] = new.reshape(d_head, rows)
+                prod = new.reshape(d_head, rows).astype(F32) * q
+                rows_out.append(jnp.sum(prod, axis=0, keepdims=True))
+            score_ref[h, j * T_BLOCK:(j + 1) * T_BLOCK, :] = jnp.concatenate(rows_out, axis=0)
+            return carry
+        lax.fori_loop(0, n_head, k_head, 0)
+        chunk_out(j).start()
+
+    t_iota = lax.broadcasted_iota(jnp.int32, (t_len, rows), 0)
+    causal = t_iota <= pos
+    back = jnp.maximum(pos - t_iota, 0)
+
+    def soft_head(h, carry):
+        line = jnp.broadcast_to(acc_ref[pl.ds(h, 1), :], (t_len, 128))
+        s = score_ref[h] + jnp.take_along_axis(line, back, axis=1)
+        s = jnp.where(causal, s, NEG_FILL)
+        e = jnp.exp(s - jnp.max(s, axis=0, keepdims=True))
+        p = e / jnp.sum(e, axis=0, keepdims=True)
+        score_ref[h] = p.astype(BF16).astype(F32)
+        return carry
+    lax.fori_loop(0, n_head, soft_head, 0)
+
+    acc_ref[...] = jnp.zeros_like(acc_ref)
+    for j in range(n_chunk):
+        kv_copy(n_chunk + j).wait()
+        issue(n_w + n_chunk + j + 1 + window)
+
+        def v_head(h, carry):
+            at = pl.multiple_of(h * d_head, d_head)
+            vn = kn_ref[1, pl.ds(at, d_head), :].reshape(sub, 16, rows)
+            p = score_ref[h, j * T_BLOCK:(j + 1) * T_BLOCK, :]
+            acc = acc_ref[pl.ds(at, d_head), :]
+            for tt in range(T_BLOCK):
+                here = pl.ds(pl.multiple_of(tt * inner + at, d_head), d_head)
+                old = kvbuf[n_chunk + j, here, :].reshape(sub, 16, rows)
+                hit = hit_ref[j * T_BLOCK + tt] != 0
+                new = jnp.where(hit[None], vn, old)
+                kvbuf[n_chunk + j, here, :] = new.reshape(d_head, rows)
+                acc = acc + new.reshape(d_head, rows).astype(F32) * p[tt:tt + 1, :]
+            acc_ref[pl.ds(at, d_head), :] = acc
+            return carry
+        lax.fori_loop(0, n_head, v_head, 0)
+        chunk_out(n_chunk + j).start()
+
+    issue(len(loads))
+    hbuf[:, 0:inner] = acc_ref[...].T.astype(BF16)
+    width = wo_per_slot * COLS
+    part_copies = []
+    for i in range(n_wo):
+        for copy in wo_copies(i):
+            copy.wait()
+        for r in range(wo_per_slot):
+            at = (i * wo_per_slot + r) * COLS
+            y = jnp.dot(hbuf[:, 0:inner], wbuf[i, r * inner:(r + 1) * inner, :], preferred_element_type=F32)
+            xbuf[:, at:at + COLS] = y.astype(BF16)
+        copy = pltpu.make_async_copy(xbuf.at[:, pl.ds(i * width, width)], part_hbm.at[:, pl.ds(i * width, width)], part_sem.at[i])
+        copy.start()
+        part_copies.append(copy)
+    for i in range(2 * n_chunk):
+        chunk_out(i).wait()
+    for copy in part_copies:
+        copy.wait()
+
+
+def self_attention(x_in, norms, tok_pos, rel_bias, w_q, w_k, w_v, w_o, self_k, self_v):
+    rows, t_len, n_head, d_head = self_k.shape
+    d_model = x_in.shape[1]
+    inner = n_head * d_head
+    flat = (t_len * inner, rows)
+    k_flat = self_k.transpose(1, 2, 3, 0).reshape(flat)
+    v_flat = self_v.transpose(1, 2, 3, 0).reshape(flat)
+    n_w = 3 * (inner // COLS)
+    n_chunk = t_len // T_BLOCK
+    n_wo = w_o.shape[1] // COLS // (d_model // inner)
+
+    def body(*refs):
+        self_kernel(*refs, window=6)
+
+    part, new_k, new_v = pl.pallas_call(
+        body,
+        out_shape=(jax.ShapeDtypeStruct((rows, w_o.shape[1]), BF16),
+                   jax.ShapeDtypeStruct(flat, BF16), jax.ShapeDtypeStruct(flat, BF16)),
+        in_specs=[ANY, VMEM, VMEM, VMEM] + [ANY] * 6,
+        out_specs=(ANY, ANY, ANY),
+        scratch_shapes=[
+            pltpu.VMEM((rows, d_model), BF16),
+            pltpu.VMEM((rows, d_model), BF16),
+            pltpu.VMEM((n_w, d_model, COLS), BF16),
+            pltpu.VMEM((2 * n_chunk, T_BLOCK * inner, rows), BF16),
+            pltpu.VMEM((inner, rows), F32),
+            pltpu.VMEM((2, inner, rows), BF16),
+            pltpu.VMEM((t_len, 16, rows), BF16),
+            pltpu.VMEM((n_head, t_len, rows), F32),
+            pltpu.VMEM((inner, rows), F32),
+            pltpu.SemaphoreType.DMA,
+            pltpu.SemaphoreType.DMA((n_w,)),
+            pltpu.SemaphoreType.DMA((2 * n_chunk,)),
+            pltpu.SemaphoreType.DMA((2 * n_chunk,)),
+            pltpu.SemaphoreType.DMA((n_wo,)),
+        ],
+        compiler_params=pltpu.CompilerParams(vmem_limit_bytes=66_900_000),
+        cost_estimate=pl.CostEstimate(flops=4_400_000_000, bytes_accessed=104_000_000, transcendentals=131_072),
+        name="self_part",
+    )(x_in, norms, tok_pos.reshape(1, rows), rel_bias.T, w_q, w_k, w_v, w_o, k_flat, v_flat)
+
+    def unflat(cache):
+        return cache.reshape(t_len, n_head, d_head, rows).transpose(3, 0, 1, 2)
+    return part, unflat(new_k), unflat(new_v)
 
 
 def rms_norm(values, norm_scale):
@@ -15,12 +233,6 @@
 
 def project(normed, weight):
     return jnp.dot(normed, weight, preferred_element_type=jnp.float32).astype(jnp.bfloat16)
-
-
-def rel_bucket(distance):
-    bucket_edges = jnp.array(BUCKET_EDGES, dtype=jnp.int32)
-    far_bucket = 16 + jnp.sum((distance[..., None] >= bucket_edges).astype(jnp.int32), axis=-1)
-    return jnp.where(distance < 16, distance, far_bucket)
 
 
 def attend(queries, keys_all, values_all, extra):
@@ -30,15 +242,6 @@
     return mixed_out.astype(jnp.bfloat16)
 
 
-def self_terms(tok_pos, rel_bias, t_len):
-    key_index = jnp.arange(t_len)
-    at_pos = (key_index[None, :] == tok_pos[:, None])[:, :, None, None]
-    distance = jnp.maximum(tok_pos[:, None] - key_index[None, :], 0)
-    bias_rows = jnp.swapaxes(jnp.take(rel_bias, rel_bucket(distance), axis=0), 1, 2)
-    causal = (key_index[None, :] <= tok_pos[:, None])[:, None, :]
-    return at_pos, jnp.where(causal, bias_rows, NEG_FILL)
-
-
 def solution(mesh):
     def tp_sum(partial_out):
         return lax.psum(partial_out.astype(jnp.bfloat16), 'tp').astype(jnp.float32)
@@ -47,16 +250,9 @@
         row_count, t_len, head_count, head_dim = self_k.shape
         head_shape = (row_count, head_count, head_dim)
         flat_dim = head_count * head_dim
-        residual = x_in.astype(jnp.float32)
-        normed = rms_norm(residual, norm_self)
-        queries = project(normed, w_q).reshape(head_shape)
-        new_keys = project(normed, w_k).reshape(head_shape)
-        new_values = project(normed, w_v).reshape(head_shape)
-        at_pos, self_extra = self_terms(tok_pos, rel_bias, t_len)
-        new_self_k = jnp.where(at_pos, new_keys[:, None], self_k)
-        new_self_v = jnp.where(at_pos, new_values[:, None], self_v)
-        mixed_self = attend(queries, new_self_k, new_self_v, self_extra)
-        residual = residual + tp_sum(jnp.dot(mixed_self.reshape(row_count, flat_dim), w_o, preferred_element_type=jnp.float32))
+        norms = jnp.stack([norm_self, norm_cross, norm_mlp]).astype(F32)
+        part, new_self_k, new_self_v = self_attention(x_in, norms, tok_pos, rel_bias, w_q, w_k, w_v, w_o, self_k, self_v)
+        residual = x_in.astype(jnp.float32) + tp_sum(part)
         normed = rms_norm(residual, norm_cross)
         cross_queries = project(normed, cross_q).reshape(head_shape)
         cross_extra = jnp.where(enc_mask[:, None, :] != 0, 0.0, NEG_FILL)

time: 305 us -> 244 us (0.80)
  other arithmetic: 57.7 us -> 10.2 us
  Pallas kernels: 0 us -> 39.5 us
  local copies, waits for them, and re-layouts: 39.3 us -> 5.59 us
  matrix products: 96.7 us -> 77.7 us
    pallas_call x0 -> x1, Pallas kernels: none -> 39.5 us  [self_attention(): pl.pallas_call(body, out_shape=(jax.ShapeDtypeStruct((rows, w_o.shape[1])...]
    gather x1 -> x0, local copies, waits for them, and re-layouts: 27.7 us -> none  [self_terms(): jnp.take(rel_bias, rel_bucket(distance), axis=0)]
    unnamed x2 -> x0, other arithmetic: 18.9 us -> none
    dot_general x1 -> x0, other arithmetic: 17.1 us -> none  [attend(): jnp.einsum('bht,bthk->bhk', probs_bf, values_all, preferred_element_type=...]
    dot_general x4 -> x1, matrix products: 19.9 us -> 5.11 us  [project(): jnp.dot(normed, weight, preferred_element_type=jnp.float32)]
    div x2 -> x1, other arithmetic: 8.32 us -> 1.87 us  [attend(): probs_bf = jax.nn.softmax(scores, axis=-1).astype(jnp.bfloat16)]
    dot_general x1 -> x0, matrix products: 5.68 us -> none  [local_layer(): jnp.dot(mixed_self.reshape(row_count, flat_dim), w_o, preferred_element_t...]
    unnamed x12, local copies, waits for them, and re-layouts: 4.53 us -> 0.03 us
where the time goes in v1:
time: 244 us; the launch traced here: 243 us
  waiting for transfers between devices  95.8 us (39%)
  matrix products  77.7 us (32%)
  Pallas kernels  39.5 us (16%)
  between operations  13.9 us (6%)
  other arithmetic  10.2 us (4%)
  local copies, waits for them, and re-layouts  5.59 us (2%)
    psum x3, waiting for transfers between devices, tp_sum(): return lax.psum(partial_out.astype(jnp.bfloat16), 'tp').astype(jnp.float32)  95.7 us
    pallas_call x1, Pallas kernels, self_attention(): pl.pallas_call(body, out_shape=(jax.ShapeDtypeStruct((rows, w_o.shape[1])...  39.5 us
    dot_general x1, matrix products, attend(): jnp.einsum('bht,bthk->bhk', probs_bf, values_all, preferred_element_type=...  22.7 us
    dot_general x1, matrix products, local_layer(): jnp.dot(hidden, w_down, preferred_element_type=jnp.float32)  18 us
    dot_general x1, matrix products, attend(): jnp.einsum('bhk,bthk->bht', queries, keys_all, preferred_element_type=jnp...  15.3 us
    dot_general x1, matrix products, local_layer(): gate_pre = jnp.dot(normed, w_gate, preferred_element_type=jnp.float32)  10.9 us
    dot_general x1, matrix products, local_layer(): jnp.dot(mixed_cross.reshape(row_count, flat_dim), cross_o, preferred_elem...  5.64 us
    dot_general x1, matrix products, project(): jnp.dot(normed, weight, preferred_element_type=jnp.float32)  5.11 us
  transfers between devices with their start and end apart: 3, of which 3 were waited for; matrix products, arithmetic and copies ran while one was open for 0% of the time, Pallas kernels for 0%

profile of v1, /device:TPU:0, one launch (start us, length us, event | category | flops | bytes accessed | tf_op | source)
XLA Modules:
  0.0 243.2 jit_solution(12114008352414604365)
XLA Ops:
  7.2 0.0 all-reduce.4.cloned.1.call-start
  7.2 0.7 stack.12
  7.9 0.7 stack.13
  8.6 0.7 stack.14
  9.3 0.7 maximum_convert_fusion.refs_1_
  10.0 39.5 %self_part.1 = (bf16[128,4096]{1,0:T(8,128)(2,1)}, bf16[65536,128]{1,0:T(8,128)(2,1)}, bf16[65536,128]{1,0:T(8,128)(2,1)}) custom-call(bf16[128,4096]{1,0:T(8,128)(2,1)} %refs_0_.1, f32[3,4096]{1,0:T(4,128)} %maximum_convert_fusion.refs_1_, s32[1,128]{1,0:T(1,128)} %bitcast.50, f32[16,32]{1,0:T(8,128)} %bitcast.49, bf16[4096,1024]{1,0:T(8,128)(2,1)} %refs_4_.1, ...), custom_call_target="tpu_custom_call" | custom-call | flops 4400000000 | bytes 104000000 | tf_op jit(solution)/shard_map/self_part/pallas_call | solution.py:197
  49.5 0.0 copy-start
  49.6 0.0 all-reduce.4.cloned.1.call-update
  49.6 0.2 all-reduce.6.cloned.1.call-start
  49.8 0.0 copy-done.4
  49.9 33.5 %all-reduce.4.cloned.1.call-done = bf16[128,4096]{1,0:T(8,128)(2,1)} async-done(((bf16[128,4096]{1,0:T(8,128)(2,1)}), bf16[128,4096]{1,0:T(8,128)(2,1)}) %all-reduce.4.cloned.1.call-update) | async-done | bytes 1048592 | tf_op jit(solution)/shard_map/psum | solution.py:247
  83.4 2.1 multiply_reduce_fusion.1
  85.5 5.1 %convolution_convert_fusion.2 = bf16[128,1024]{1,0:T(8,128)(2,1)S(1)} fusion(bf16[4096,1024]{1,0:T(8,128)(2,1)} %param.32, bf16[128,4096]{1,0:T(8,128)(2,1)S(1)} %copy-done.1, bf16[128,4096]{1,0:T(8,128)(2,1)S(1)} %copy-done, f32[4096]{0:T(1024)S(1)} %convert_element_type.51, f32[128]{0:T(128)S(1)} %add_rsqrt_fusion.1), kind=kOutput, calls=%fused_computation.26 | convolution fusion | flops 1077018624 | bytes 10764800 | tf_op jit(solution)/shard_map/dot_general | solution.py:235
  90.6 0.2 copy.24
  90.8 0.9 copy.25
  91.7 15.3 %fusion.23 = f32[128,16,1,128]{3,2,1,0:T(1,128)} fusion(bf16[128,16,64,1]{2,3,1,0:T(2,128)(2,1)S(1)} %copy.25, bf16[128,128,16,64]{1,3,2,0:T(8,128)(2,1)} %param.24), kind=kOutput, calls=%fused_computation.39 | convolution fusion | flops 33554432 | bytes 34865152 | tf_op jit(solution)/shard_map/bhk,bthk->bht/dot_general | solution.py:239
  107.0 1.9 fusion.14
  108.9 22.7 %fusion.15 = bf16[128,16,1,64]{3,2,1,0:T(2,128)(2,1)} fusion(bf16[128,128,16,64]{1,3,2,0:T(8,128)(2,1)} %param.25, bf16[128,16,128,1]{2,1,0,3:T(8,128)(2,1)S(1)} %fusion.14), kind=kOutput, calls=%fused_computation.27 | convolution fusion | flops 33554432 | bytes 34340864 | tf_op jit(solution)/shard_map/bht,bthk->bhk/dot_general | solution.py:241
  131.6 2.3 copy.28
  133.9 0.0 copy-start.5
  134.0 5.6 %convolution_convert_fusion = bf16[128,4096]{1,0:T(8,128)(2,1)} fusion(bf16[128,1024]{0,1:T(8,128)(2,1)S(1)} %bitcast.47, bf16[1024,4096]{1,0:T(8,128)(2,1)} %param.33), kind=kOutput, calls=%fused_computation.2 | convolution fusion | flops 1074266112 | bytes 9699328 | tf_op jit(solution)/shard_map/dot_general | solution.py:260
  139.6 0.0 all-reduce.6.cloned.1.call-update
  139.6 0.3 all-reduce.8.cloned.1.call-start
  139.9 0.0 copy-done.5
  139.9 30.9 %all-reduce.6.cloned.1.call-done = bf16[128,4096]{1,0:T(8,128)(2,1)} async-done(((bf16[128,4096]{1,0:T(8,128)(2,1)}), bf16[128,4096]{1,0:T(8,128)(2,1)}) %all-reduce.6.cloned.1.call-update) | async-done | bytes 1048592 | tf_op jit(solution)/shard_map/psum | solution.py:247
  170.9 1.9 multiply_reduce_fusion
  172.8 0.6 multiply_convert_fusion
  173.3 10.9 %fusion.24 = f32[128,2560]{1,0:T(8,128)} fusion(bf16[128,4096]{1,0:T(8,128)(2,1)S(1)} %multiply_convert_fusion, bf16[4096,2560]{1,0:T(8,128)(2,1)} %param.34), kind=kOutput, calls=%fused_computation.40 | convolution fusion | flops 2684354560 | bytes 23330816 | tf_op jit(solution)/shard_map/dot_general | solution.py:262
  184.2 18.0 %convolution_convert_fusion.1 = bf16[128,4096]{1,0:T(8,128)(2,1)} fusion(bf16[2560,4096]{1,0:T(8,128)(2,1)} %param.36, bf16[128,4096]{1,0:T(8,128)(2,1)S(1)} %multiply_convert_fusion, bf16[4096,2560]{1,0:T(8,128)(2,1)} %param.35, f32[128,2560]{1,0:T(8,128)} %fusion.24), kind=kOutput, calls=%fused_computation.3 | convolution fusion | flops 5372510208 | bytes 45350912 | tf_op jit(solution)/shard_map/dot_general | solution.py:265
  202.2 0.0 all-reduce.8.cloned.1.call-update
  202.2 31.3 %all-reduce.8.cloned.1.call-done = bf16[128,4096]{1,0:T(8,128)(2,1)} async-done(((bf16[128,4096]{1,0:T(8,128)(2,1)}), bf16[128,4096]{1,0:T(8,128)(2,1)}) %all-reduce.8.cloned.1.call-update) | async-done | bytes 1048592 | tf_op jit(solution)/shard_map/psum | solution.py:247
  233.5 3.2 %add_convert_fusion = bf16[128,4096]{1,0:T(8,128)(2,1)} fusion(bf16[128,4096]{1,0:T(8,128)(2,1)} %all-reduce.8.cloned.1.call-done, bf16[128,4096]{1,0:T(8,128)(2,1)} %all-reduce.6.cloned.1.call-done, bf16[128,4096]{1,0:T(8,128)(2,1)S(1)} %copy-done.1, bf16[128,4096]{1,0:T(8,128)(2,1)S(1)} %copy-done), kind=kLoop, calls=%fused_computation.6 | loop fusion | flops 4194304 | bytes 5242880 | tf_op jit(solution)/shard_map/convert_element_type | solution.py:266
  (13 shorter events, 0.0 us)
Async XLA Ops:
  7.2 76.2 %all-reduce.4.cloned.1.call-start = ((), (), s32[]{:S(2)}) async-start(), calls=%async_computation | async-start | bytes 2097152 | tf_op jit(solution)/shard_map/psum | solution.py:247
  10.0 39.8 %copy-start.4 = (bf16[4096]{0:T(1024)(128)(2,1)S(1)}, bf16[4096]{0:T(1024)(128)(2,1)}, u32[]{:S(2)}) copy-start(bf16[4096]{0:T(1024)(128)(2,1)} %param.38) | copy-start | bytes 24580
  10.0 39.8 %copy-start.3 = (s32[128,128]{1,0:T(8,128)S(1)}, s32[128,128]{1,0:T(8,128)}, u32[]{:S(2)}) copy-start(s32[128,128]{1,0:T(8,128)} %param.26) | copy-start | bytes 196612
  49.5 35.9 %copy-start = (bf16[128,4096]{1,0:T(8,128)(2,1)S(1)}, bf16[128,4096]{1,0:T(8,128)(2,1)}, u32[]{:S(2)}) copy-start(bf16[128,4096]{1,0:T(8,128)(2,1)} %refs_0_.1) | copy-start | bytes 3145732
  49.6 121.3 %all-reduce.6.cloned.1.call-start = ((), (), s32[]{:S(2)}) async-start(), calls=%async_computation.1 | async-start | bytes 2097152 | tf_op jit(solution)/shard_map/psum | solution.py:247
  83.4 2.1 copy-start.1
  133.9 5.9 %copy-start.5 = (bf16[4096]{0:T(1024)(128)(2,1)S(1)}, bf16[4096]{0:T(1024)(128)(2,1)}, u32[]{:S(2)}) copy-start(bf16[4096]{0:T(1024)(128)(2,1)} %param.39) | copy-start | bytes 24580
  139.6 93.9 %all-reduce.8.cloned.1.call-start = ((), (), s32[]{:S(2)}) async-start(), calls=%async_computation.2 | async-start | bytes 2097152 | tf_op jit(solution)/shard_map/psum | solution.py:247
  170.9 1.9 copy-start.2
Sparse Core Ops, SparseCore 0:
  49.7 33.6 all-reduce.3
  139.7 31.0 all-reduce.5
  202.4 31.0 all-reduce.7

commit v2 on v1

--- a/solution.py
+++ b/solution.py
@@ -1,3 +1,4 @@
+import functools
 import math
 import jax
 import jax.numpy as jnp
@@ -226,44 +227,399 @@
     return part, unflat(new_k), unflat(new_v)
 
 
-def rms_norm(values, norm_scale):
-    inv_rms = lax.rsqrt(jnp.mean(values * values, axis=-1, keepdims=True) + 1e-6)
-    return (values * inv_rms * norm_scale.astype(jnp.float32)).astype(jnp.bfloat16)
-
-
-def project(normed, weight):
-    return jnp.dot(normed, weight, preferred_element_type=jnp.float32).astype(jnp.bfloat16)
-
-
-def attend(queries, keys_all, values_all, extra):
-    scores = jnp.einsum('bhk,bthk->bht', queries, keys_all, preferred_element_type=jnp.float32) + extra
-    probs_bf = jax.nn.softmax(scores, axis=-1).astype(jnp.bfloat16)
-    mixed_out = jnp.einsum('bht,bthk->bhk', probs_bf, values_all, preferred_element_type=jnp.float32)
-    return mixed_out.astype(jnp.bfloat16)
+SLOTS = 52
+GROUP = 8
+AR_CHUNKS = 4
+LANES = 128
+
+
+def cross_kernel(n_head, x_hbm, part_hbm, norm_ref, mask_ref, cq_hbm, ck_hbm, cv_hbm, co_hbm, wg_hbm, wu_hbm, wd_hbm,
+                 out_hbm,
+                 ring, pbuf, hbuf, res, xhalf, rx1, tx2, rx2, q_ref, mix_ref, mixbf, act,
+                 ring_sem, load_sem, s1_send, s1_recv, s2_send, s2_recv, s3_send, s3_recv, out_sem):
+    rows, d_model = hbuf.shape
+    half = rows // 2
+    depth = ring.shape[1]
+    inner = q_ref.shape[1]
+    d_ff = act.shape[1]
+    width = d_model // AR_CHUNKS
+
+    me = lax.axis_index("tp")
+    core = lax.rem(me, 2)
+    chip = me // 2
+    partner = {"tp": chip * 2 + (1 - core)}
+    across = {"tp": (1 - chip) * 2 + core}
+    mine = pl.ds(pl.multiple_of(core * half, half), half)
+    theirs = pl.ds(pl.multiple_of((1 - core) * half, half), half)
+    MESH = pl.DeviceIdType.MESH
+
+    n_q = cq_hbm.shape[1] // LANES
+    per_step = GROUP * inner // depth
+    n_step = rows // GROUP
+    first_kv = n_q
+    first_o = first_kv + 2 * per_step * n_step
+    o_blocks = depth // inner
+    n_o = co_hbm.shape[1] // LANES // o_blocks
+    first_gu = first_o + n_o
+    n_gu = d_ff // LANES
+    first_d = first_gu + 2 * n_gu
+    n_d = d_model // LANES
+    total = first_d + n_d
+
+    def slot_of(j):
+        return j % SLOTS if isinstance(j, int) else lax.rem(j, SLOTS)
+
+    def start(src, j, used=None):
+        dst = ring.at[slot_of(j)] if used is None else ring.at[slot_of(j), used]
+        pltpu.make_async_copy(src, dst, ring_sem.at[slot_of(j)]).start()
+
+    def cols(ref, i):
+        at = i * LANES
+        return ref.at[:, pl.ds(at if isinstance(at, int) else pl.multiple_of(at, LANES), LANES)]
+
+    def issue_q(j):
+        start(cols(cq_hbm, j), j)
+
+    def issue_kv(j):
+        n = j - first_kv
+        step, piece = n // (2 * per_step), n % (2 * per_step)
+        if isinstance(j, int):
+            src = ck_hbm if piece < per_step else cv_hbm
+            start(src.at[pl.ds((step * per_step + piece % per_step) * depth, depth)], j)
+
+    def issue_step(step, j0):
+        for piece in range(2 * per_step):
+            src = ck_hbm if piece < per_step else cv_hbm
+            at = (step * per_step + piece % per_step) * depth
+            start(src.at[pl.ds(pl.multiple_of(at, depth), depth)], j0 + piece)
+
+    def issue_o(j):
+        n = j - first_o
+        for r in range(o_blocks):
+            start(cols(co_hbm, n * o_blocks + r), j, pl.ds(r * inner, inner))
+
+    def issue_gu(pair, j0):
+        start(cols(wg_hbm, pair), j0)
+        start(cols(wu_hbm, pair), j0 + 1)
+
+    def issue_d(j):
+        start(cols(wd_hbm, j - first_d), j, pl.ds(0, d_ff))
+
+    def issue(j):
+        if j >= total:
+            return
+        if j < first_kv:
+            issue_q(j)
+        elif j < first_o:
+            issue_kv(j)
+        elif j < first_gu:
+            issue_o(j)
+        elif j < first_d:
+            n = j - first_gu
+            start(cols(wu_hbm if n % 2 else wg_hbm, n // 2), j)
+        else:
+            issue_d(j)
+
+    def landed(j, used=None):
+        dst = ring.at[slot_of(j)] if used is None else ring.at[slot_of(j), pl.ds(0, used)]
+        src = ck_hbm.at[pl.ds(0, depth if used is None else used)]
+        pltpu.make_async_copy(src, dst, ring_sem.at[slot_of(j)]).wait()
+
+    def part_load(j):
+        at = pl.ds(j * width, width)
+        return pltpu.make_async_copy(part_hbm.at[:, at], pbuf.at[:, at], load_sem.at[j])
+    x_load = pltpu.make_async_copy(x_hbm.at[mine], xhalf, load_sem.at[AR_CHUNKS])
+    for j in range(AR_CHUNKS):
+        part_load(j).start()
+    x_load.start()
+
+    barrier = pltpu.get_barrier_semaphore()
+    for other in (partner, across):
+        pl.semaphore_signal(barrier, inc=1, device_id=other, device_id_type=MESH)
+    pl.semaphore_wait(barrier, 2)
+
+    def to_partner(a, j):
+        at = pl.ds(j * width, width)
+        return pltpu.make_async_remote_copy(
+            src_ref=pbuf.at[theirs, at], dst_ref=rx1.at[a % 2, :, at], send_sem=s1_send.at[a % 2, j],
+            recv_sem=s1_recv.at[a % 2, j], device_id=partner, device_id_type=MESH)
+
+    def to_across(a, j):
+        at = pl.ds(j * width, width)
+        return pltpu.make_async_remote_copy(
+            src_ref=tx2.at[a % 2, :, at], dst_ref=rx2.at[a % 2, :, at], send_sem=s2_send.at[a % 2, j],
+            recv_sem=s2_recv.at[a % 2, j], device_id=across, device_id_type=MESH)
+
+    def blocks(fn, n=half // 16):
+        def body(i, carry):
+            fn(pl.multiple_of(i * 16, 16))
+            return carry
+        lax.fori_loop(0, n, body, 0)
+
+    def chip_sum(a, j):
+        at = pl.ds(j * width, width)
+        to_partner(a, j).wait_recv()
+
+        def add(r):
+            own = pbuf[pl.ds(pl.multiple_of(core * half + r, 16), 16), at].astype(F32)
+            tx2[a % 2, pl.ds(r, 16), at] = (own + rx1[a % 2, pl.ds(r, 16), at].astype(F32)).astype(BF16)
+        blocks(add)
+        to_across(a, j).start()
+
+    def full_sum(a, j):
+        at = pl.ds(j * width, width)
+        to_across(a, j).wait_recv()
+
+        def add(r):
+            both = tx2[a % 2, pl.ds(r, 16), at].astype(F32) + rx2[a % 2, pl.ds(r, 16), at].astype(F32)
+            res[pl.ds(r, 16), at] = res[pl.ds(r, 16), at] + both
+        blocks(add)
+
+    def sent(a):
+        for j in range(AR_CHUNKS):
+            to_partner(a, j).wait_send()
+            to_across(a, j).wait_send()
+
+    def rows_back(a, i):
+        at = pl.ds(pl.multiple_of(core * half + i * 16, 16), 16)
+        return pltpu.make_async_remote_copy(
+            src_ref=hbuf.at[at], dst_ref=hbuf.at[at], send_sem=s3_send.at[a % 2, i],
+            recv_sem=s3_recv.at[a % 2, i], device_id=partner, device_id_type=MESH)
+
+    def normalise(a):
+        norm = norm_ref[a + 1:a + 2, :]
+        for i in range(half // 16):
+            r = res[i * 16:(i + 1) * 16, :]
+            inv = lax.rsqrt(jnp.mean(r * r, axis=-1, keepdims=True) + 1e-6)
+            hbuf[pl.ds(pl.multiple_of(core * half + i * 16, 16), 16), :] = (r * inv * norm).astype(BF16)
+            rows_back(a, i).start()
+        for i in range(half // 16):
+            rows_back(a, i).wait()
+
+    for j in range(AR_CHUNKS):
+        part_load(j).wait()
+        to_partner(0, j).start()
+    for j in range(SLOTS):
+        issue(j)
+    x_load.wait()
+    blocks(lambda r: res.__setitem__((pl.ds(r, 16), slice(None)), xhalf[pl.ds(r, 16), :].astype(F32)))
+    for j in range(AR_CHUNKS):
+        chip_sum(0, j)
+    for j in range(AR_CHUNKS):
+        full_sum(0, j)
+    normalise(0)
+
+    def pair(j0, used=None):
+        a, b = ring.at[slot_of(j0)], ring.at[slot_of(j0 + 1)]
+        if used is None:
+            return jnp.concatenate([a[...], b[...]], axis=1)
+        return jnp.concatenate([a[0:used, :], b[0:used, :]], axis=1)
+
+    for i in range(n_q // 2):
+        landed(2 * i)
+        landed(2 * i + 1)
+        y = jnp.dot(hbuf[...], pair(2 * i), preferred_element_type=F32)
+        q_ref[:, 2 * i * LANES:(2 * i + 2) * LANES] = y.astype(BF16).astype(F32)
+        issue(2 * i + SLOTS)
+        issue(2 * i + 1 + SLOTS)
+
+    own_head = (lax.broadcasted_iota(jnp.int32, (n_head, inner), 1) // (inner // n_head)
+                == lax.broadcasted_iota(jnp.int32, (n_head, inner), 0))
+    in_slot = GROUP // per_step
+
+    def attend_step(g, carry):
+        j0 = first_kv + 2 * per_step * g
+        at = pl.ds(pl.multiple_of(g * GROUP, GROUP), GROUP)
+        q8 = q_ref[at, :]
+        m8 = mask_ref[at, :]
+
+        def spread(r):
+            return jnp.where(own_head, jnp.broadcast_to(q8[r:r + 1, :], (n_head, inner)), 0.0).astype(BF16)
+        landed(j0)
+        landed(j0 + 1)
+        scores = [None] * GROUP
+        for r in range(in_slot):
+            here = slice(r * inner, (r + 1) * inner)
+            keys = jnp.concatenate([ring.at[slot_of(j0)][here, :], ring.at[slot_of(j0 + 1)][here, :]], axis=1)
+            s = jnp.dot(jnp.concatenate([spread(r), spread(r + in_slot)], axis=0), keys, preferred_element_type=F32)
+            scores[r] = jnp.where(m8[r:r + 1, :] != 0, s[0:n_head, 0:LANES], NEG_FILL)
+            scores[r + in_slot] = jnp.where(m8[r + in_slot:r + in_slot + 1, :] != 0, s[n_head:, LANES:], NEG_FILL)
+        s = jnp.concatenate(scores, axis=0)
+        e = jnp.exp(s - jnp.max(s, axis=1, keepdims=True))
+        p = (e / jnp.sum(e, axis=1, keepdims=True)).astype(BF16)
+        landed(j0 + 2)
+        landed(j0 + 3)
+        none = jnp.zeros((n_head, LANES), BF16)
+        mixed = [None] * GROUP
+        for r in range(in_slot):
+            here = slice(r * inner, (r + 1) * inner)
+            values = jnp.concatenate([ring.at[slot_of(j0 + 2)][here, :], ring.at[slot_of(j0 + 3)][here, :]], axis=1)
+            pa = p[r * n_head:(r + 1) * n_head, :]
+            pb = p[(r + in_slot) * n_head:(r + in_slot + 1) * n_head, :]
+            lhs = jnp.concatenate([jnp.concatenate([pa, none], axis=1), jnp.concatenate([none, pb], axis=1)], axis=0)
+            y = lax.dot_general(lhs, values, (((1,), (1,)), ((), ())), preferred_element_type=F32)
+            mixed[r] = jnp.sum(jnp.where(own_head, y[0:n_head], 0.0), axis=0, keepdims=True)
+            mixed[r + in_slot] = jnp.sum(jnp.where(own_head, y[n_head:], 0.0), axis=0, keepdims=True)
+        mix_ref[at, :] = jnp.concatenate(mixed, axis=0)
+
+        n0 = j0 + SLOTS
+        last = (first_o - SLOTS - first_kv) // (2 * per_step)
+        last_o = (first_gu - SLOTS - first_kv) // (2 * per_step)
+        last_gu = (first_d - SLOTS - first_kv) // (2 * per_step)
+
+        @pl.when(g < last)
+        def _():
+            issue_step(g + SLOTS_STEPS, n0)
+
+        @pl.when((g >= last) & (g < last_o))
+        def _():
+            for piece in range(2 * per_step):
+                issue_o(n0 + piece)
+
+        @pl.when((g >= last_o) & (g < last_gu))
+        def _():
+            for piece in range(per_step):
+                issue_gu((g - last_o) * per_step + piece, n0 + 2 * piece)
+
+        @pl.when(g >= last_gu)
+        def _():
+            for piece in range(2 * per_step):
+                issue_d(n0 + piece)
+        return carry
+    SLOTS_STEPS = SLOTS // (2 * per_step)
+    lax.fori_loop(0, n_step, attend_step, 0)
+
+    sent(0)
+    mixbf[...] = mix_ref[...].astype(BF16)
+    o_cols = o_blocks * LANES
+    per_chunk = width // o_cols
+    for n in range(n_o):
+        j = first_o + n
+        landed(j)
+        w = jnp.concatenate([ring.at[slot_of(j)][r * inner:(r + 1) * inner, :] for r in range(o_blocks)], axis=1)
+        y = jnp.dot(mixbf[...], w, preferred_element_type=F32)
+        pbuf[:, n * o_cols:(n + 1) * o_cols] = y.astype(BF16)
+        issue(j + SLOTS)
+        if n % per_chunk == per_chunk - 1:
+            to_partner(1, n // per_chunk).start()
+            if n // per_chunk > 0:
+                chip_sum(1, n // per_chunk - 1)
+    chip_sum(1, AR_CHUNKS - 1)
+    for j in range(AR_CHUNKS):
+        full_sum(1, j)
+    normalise(1)
+
+    root = math.sqrt(2.0 / math.pi)
+
+    def gate_up(i, carry):
+        j0 = first_gu + 2 * i
+        landed(j0)
+        landed(j0 + 1)
+        y = jnp.dot(hbuf[...], pair(j0), preferred_element_type=F32)
+        u = y[:, 0:LANES]
+        gelu = 0.5 * u * (1.0 + jnp.tanh(root * (u + 0.044715 * (u * u * u))))
+        act[:, pl.ds(pl.multiple_of(i * LANES, LANES), LANES)] = (gelu * y[:, LANES:]).astype(BF16)
+
+        @pl.when(j0 + SLOTS < total)
+        def _():
+            issue_d(j0 + SLOTS)
+            issue_d(j0 + 1 + SLOTS)
+        return carry
+    lax.fori_loop(0, n_gu, gate_up, 0)
+    sent(1)
+
+    per_piece = width // (2 * LANES)
+
+    def out_back(j):
+        at = pl.ds(j * width, width)
+        return pltpu.make_async_remote_copy(
+            src_ref=hbuf.at[mine, at], dst_ref=hbuf.at[mine, at], send_sem=s3_send.at[0, j],
+            recv_sem=s3_recv.at[0, j], device_id=partner, device_id_type=MESH)
+
+    for c in range(AR_CHUNKS):
+        def down(i, carry):
+            j0 = first_d + 2 * (c * per_piece + i)
+            landed(j0, d_ff)
+            landed(j0 + 1, d_ff)
+            y = jnp.dot(act[...], pair(j0, d_ff), preferred_element_type=F32)
+            at = pl.multiple_of((c * per_piece + i) * 2 * LANES, 2 * LANES)
+            pbuf[:, pl.ds(at, 2 * LANES)] = y.astype(BF16)
+            return carry
+        lax.fori_loop(0, per_piece, down, 0)
+        to_partner(2, c).start()
+        if c > 0:
+            chip_sum(2, c - 1)
+    chip_sum(2, AR_CHUNKS - 1)
+
+    def out_copy(j):
+        at = pl.ds(j * width, width)
+        return pltpu.make_async_copy(hbuf.at[:, at], out_hbm.at[:, at], out_sem.at[j])
+
+    for j in range(AR_CHUNKS):
+        at = pl.ds(j * width, width)
+        to_across(2, j).wait_recv()
+
+        def add(r):
+            both = tx2[0, pl.ds(r, 16), at].astype(F32) + rx2[0, pl.ds(r, 16), at].astype(F32)
+            hbuf[pl.ds(pl.multiple_of(core * half + r, 16), 16), at] = (res[pl.ds(r, 16), at] + both).astype(BF16)
+        blocks(add)
+        out_back(j).start()
+    for j in range(AR_CHUNKS):
+        out_back(j).wait()
+        out_copy(j).start()
+    sent(2)
+    for j in range(AR_CHUNKS):
+        out_copy(j).wait()
+
+
+def rest_of_layer(x_in, part, norms, enc_mask, cross_k, cross_v, cross_q, cross_o, w_gate, w_up, w_down):
+    rows, d_model = x_in.shape
+    _, src_len, n_head, d_head = cross_k.shape
+    inner = n_head * d_head
+    d_ff = w_gate.shape[1]
+    half = rows // 2
+    flat = (rows * inner, src_len)
+    k_flat = cross_k.transpose(0, 2, 3, 1).reshape(flat)
+    v_flat = cross_v.transpose(0, 2, 3, 1).reshape(flat)
+    return pl.pallas_call(
+        functools.partial(cross_kernel, n_head),
+        out_shape=jax.ShapeDtypeStruct((rows, d_model), BF16),
+        in_specs=[ANY, ANY, VMEM, VMEM] + [ANY] * 7,
+        out_specs=ANY,
+        scratch_shapes=[
+            pltpu.VMEM((SLOTS, d_model, LANES), BF16),
+            pltpu.VMEM((rows, d_model), BF16),
+            pltpu.VMEM((rows, d_model), BF16),
+            pltpu.VMEM((half, d_model), F32),
+            pltpu.VMEM((half, d_model), BF16),
+            pltpu.VMEM((2, half, d_model), BF16),
+            pltpu.VMEM((2, half, d_model), BF16),
+            pltpu.VMEM((2, half, d_model), BF16),
+            pltpu.VMEM((rows, inner), F32),
+            pltpu.VMEM((rows, inner), F32),
+            pltpu.VMEM((rows, inner), BF16),
+            pltpu.VMEM((rows, d_ff), BF16),
+            pltpu.SemaphoreType.DMA((SLOTS,)),
+            pltpu.SemaphoreType.DMA((AR_CHUNKS + 1,)),
+            pltpu.SemaphoreType.DMA((2, AR_CHUNKS)),
+            pltpu.SemaphoreType.DMA((2, AR_CHUNKS)),
+            pltpu.SemaphoreType.DMA((2, AR_CHUNKS)),
+            pltpu.SemaphoreType.DMA((2, AR_CHUNKS)),
+            pltpu.SemaphoreType.DMA((2, AR_CHUNKS)),
+            pltpu.SemaphoreType.DMA((2, AR_CHUNKS)),
+            pltpu.SemaphoreType.DMA((AR_CHUNKS,)),
+        ],
+        compiler_params=pltpu.CompilerParams(vmem_limit_bytes=67_000_000, collective_id=0, has_side_effects=True),
+        name="rest_part",
+    )(x_in, part, norms, enc_mask, cross_q, k_flat, v_flat, cross_o, w_gate, w_up, w_down)
 
 
 def solution(mesh):
-    def tp_sum(partial_out):
-        return lax.psum(partial_out.astype(jnp.bfloat16), 'tp').astype(jnp.float32)
-
     def local_layer(x_in, tok_pos, self_k, self_v, cross_k, cross_v, enc_mask, rel_bias, w_q, w_k, w_v, w_o, cross_q, cross_o, w_gate, w_up, w_down, norm_self, norm_cross, norm_mlp):
-        row_count, t_len, head_count, head_dim = self_k.shape
-        head_shape = (row_count, head_count, head_dim)
-        flat_dim = head_count * head_dim
         norms = jnp.stack([norm_self, norm_cross, norm_mlp]).astype(F32)
         part, new_self_k, new_self_v = self_attention(x_in, norms, tok_pos, rel_bias, w_q, w_k, w_v, w_o, self_k, self_v)
-        residual = x_in.astype(jnp.float32) + tp_sum(part)
-        normed = rms_norm(residual, norm_cross)
-        cross_queries = project(normed, cross_q).reshape(head_shape)
-        cross_extra = jnp.where(enc_mask[:, None, :] != 0, 0.0, NEG_FILL)
-        mixed_cross = attend(cross_queries, cross_k, cross_v, cross_extra)
-        residual = residual + tp_sum(jnp.dot(mixed_cross.reshape(row_count, flat_dim), cross_o, preferred_element_type=jnp.float32))
-        normed = rms_norm(residual, norm_mlp)
-        gate_pre = jnp.dot(normed, w_gate, preferred_element_type=jnp.float32)
-        up_pre = jnp.dot(normed, w_up, preferred_element_type=jnp.float32)
-        hidden = (jax.nn.gelu(gate_pre, approximate=True) * up_pre).astype(jnp.bfloat16)
-        residual = residual + tp_sum(jnp.dot(hidden, w_down, preferred_element_type=jnp.float32))
-        return residual.astype(jnp.bfloat16), new_self_k, new_self_v
+        x_out = rest_of_layer(x_in, part, norms, enc_mask, cross_k, cross_v, cross_q, cross_o, w_gate, w_up, w_down)
+        return x_out, new_self_k, new_self_v
 
     cache_spec = P('dp', None, 'tp', None)
     split_cols = P(None, 'tp')

time: 244 us -> 136 us (0.56)
  waiting for transfers between devices: 95.8 us -> 0 us
  Pallas kernels: 39.5 us -> 130 us
  matrix products: 77.7 us -> 0 us
  between operations: 13.9 us -> 0.66 us
  other arithmetic: 10.2 us -> 0.69 us
    psum x3 -> x0, waiting for transfers between devices: 95.7 us -> none  [tp_sum(): return lax.psum(partial_out.astype(jnp.bfloat16), 'tp').astype(jnp.float32)]
    pallas_call x0 -> x1, Pallas kernels: none -> 90.6 us  [rest_of_layer(): pl.pallas_call(functools.partial(cross_kernel, n_head), out_shape=jax.Sha...]
    dot_general x6 -> x0, matrix products: 77.7 us -> none  [the longest x1 22.7 us: attend(): jnp.einsum('bht,bthk->bhk', probs_bf, values_all, preferred_element_type=...]
    reduce_sum x2 -> x0, other arithmetic: 3.92 us -> none  [rms_norm(): jnp.mean(values * values, axis=-1, keepdims=True) + 1e-06]
    convert_element_type x4 -> x0, other arithmetic: 3.73 us -> none  [the longest x1 3.17 us: local_layer(): return (residual.astype(jnp.bfloat16), new_self_k, new_self_v)]
  transfers between devices with their start and end apart: 3 -> 0, of which waited for: 3 -> 0; matrix products, arithmetic and copies ran while one was open for 0% -> 0% of each run, Pallas kernels for 0% -> 0%
where the time goes in v2:
time: 136 us
  Pallas kernels  130 us (96%)
  local copies, waits for them, and re-layouts  4.42 us (3%)
    pallas_call x1, Pallas kernels, rest_of_layer(): pl.pallas_call(functools.partial(cross_kernel, n_head), out_shape=jax.Sha...  90.6 us
    pallas_call x1, Pallas kernels, self_attention(): pl.pallas_call(body, out_shape=(jax.ShapeDtypeStruct((rows, w_o.shape[1])...  39.5 us

profile of v2, /device:TPU:0, one launch (start us, length us, event | category | flops | bytes accessed | tf_op | source)
XLA Modules:
  0.0 135.8 jit_solution(4968172203189945091)
XLA Ops:
  0.6 0.7 stack.12
  1.3 0.7 stack.13
  2.1 0.7 stack.14
  2.8 0.7 maximum_convert_fusion.refs_1_.norm_ref
  3.5 39.5 %self_part.1 = (bf16[128,4096]{1,0:T(8,128)(2,1)}, bf16[65536,128]{1,0:T(8,128)(2,1)}, bf16[65536,128]{1,0:T(8,128)(2,1)}) custom-call(bf16[128,4096]{1,0:T(8,128)(2,1)} %x_hbm.1, f32[3,4096]{1,0:T(4,128)} %maximum_convert_fusion.refs_1_.norm_ref, s32[1,128]{1,0:T(1,128)} %bitcast.25, f32[16,32]{1,0:T(8,128)} %bitcast.24, bf16[4096,1024]{1,0:T(8,128)(2,1)} %refs_4_.1, ...), custom_call_target="tpu_custom_call" | custom-call | flops 4400000000 | bytes 104000000 | tf_op jit(solution)/shard_map/self_part/pallas_call | solution.py:198
  42.9 90.6 %rest_part.1 = bf16[128,4096]{1,0:T(8,128)(2,1)} custom-call(bf16[128,4096]{1,0:T(8,128)(2,1)} %x_hbm.1, bf16[128,4096]{1,0:T(8,128)(2,1)} %get-tuple-element.6.part_hbm, f32[3,4096]{1,0:T(4,128)} %maximum_convert_fusion.refs_1_.norm_ref, s32[128,128]{1,0:T(8,128)} %mask_ref.1, bf16[4096,1024]{1,0:T(8,128)(2,1)} %cq_hbm.1, bf16[131072,128]{1,0:T(8,128)(2,1)} %bitcast.20, ...), custom_call_target="tpu_custom_call" | custom-call | tf_op jit(solution)/shard_map/rest_part/pallas_call | solution.py:584
  133.5 2.3 %copy.24 = bf16[128,4096]{1,0:T(8,128)(2,1)} copy(bf16[128,4096]{1,0:T(8,128)(2,1)} %rest_part.1) | data formatting | bytes 2097152

commit v3 on v1

--- a/solution.py
+++ b/solution.py
@@ -1,3 +1,4 @@
+import functools
 import math
 import jax
 import jax.numpy as jnp
@@ -16,10 +17,17 @@
 T_BLOCK = 8
 
 
-def self_kernel(x_hbm, norm_ref, pos_ref, rel_ref, wq_hbm, wk_hbm, wv_hbm, wo_hbm, k_hbm, v_hbm,
+def lay_row(dst, at, norm):
+    values = norm[...].astype(F32)
+    for i in range(values.shape[0]):
+        dst[at:at + 1, i * 128:(i + 1) * 128] = values[i:i + 1, :]
+
+
+def self_kernel(x_hbm, norm_hbm, pos_hbm, rel_hbm, wq_hbm, wk_hbm, wv_hbm, wo_hbm, k_hbm, v_hbm,
                 part_hbm, newk_hbm, newv_hbm,
                 xbuf, hbuf, wbuf, kvbuf, q_ref, kn_ref, hit_ref, score_ref, acc_ref,
-                x_sem, w_sem, kv_sem, out_sem, part_sem, window):
+                norm_ref, nrow, pos_ref, rel_ref,
+                x_sem, small_sem, w_sem, kv_sem, out_sem, part_sem, window):
     rows, d_model = xbuf.shape
     n_w = wbuf.shape[0]
     per_mat = n_w // 3
@@ -55,8 +63,15 @@
 
     x_copy = pltpu.make_async_copy(x_hbm, xbuf, x_sem)
     x_copy.start()
+    small = [pltpu.make_async_copy(src, dst, small_sem.at[i]) for i, (src, dst) in enumerate(
+        ((pos_hbm, pos_ref), (rel_hbm, rel_ref), (norm_hbm, norm_ref)))]
+    for copy in small:
+        copy.start()
     issue(window)
-
+    for copy in small:
+        copy.wait()
+
+    lay_row(nrow, 0, norm_ref)
     pos = pos_ref[...]
     pos16 = jnp.broadcast_to(pos, (16, rows))
 
@@ -78,7 +93,7 @@
 
     x_copy.wait()
     block = 16
-    norm = norm_ref[0:1, :]
+    norm = nrow[0:1, :]
 
     def norm_rows(i, carry):
         at = pl.ds(pl.multiple_of(i * block, block), block)
@@ -180,7 +195,7 @@
         copy.wait()
 
 
-def self_attention(x_in, norms, tok_pos, rel_bias, w_q, w_k, w_v, w_o, self_k, self_v):
+def self_attention(x_in, norm_self, tok_pos, rel_bias, w_q, w_k, w_v, w_o, self_k, self_v):
     rows, t_len, n_head, d_head = self_k.shape
     d_model = x_in.shape[1]
     inner = n_head * d_head
@@ -192,13 +207,13 @@
     n_wo = w_o.shape[1] // COLS // (d_model // inner)
 
     def body(*refs):
-        self_kernel(*refs, window=6)
+        self_kernel(*refs, window=12)
 
     part, new_k, new_v = pl.pallas_call(
         body,
         out_shape=(jax.ShapeDtypeStruct((rows, w_o.shape[1]), BF16),
                    jax.ShapeDtypeStruct(flat, BF16), jax.ShapeDtypeStruct(flat, BF16)),
-        in_specs=[ANY, VMEM, VMEM, VMEM] + [ANY] * 6,
+        in_specs=[ANY] * 10,
         out_specs=(ANY, ANY, ANY),
         scratch_shapes=[
             pltpu.VMEM((rows, d_model), BF16),
@@ -210,7 +225,12 @@
             pltpu.VMEM((t_len, 16, rows), BF16),
             pltpu.VMEM((n_head, t_len, rows), F32),
             pltpu.VMEM((inner, rows), F32),
+            pltpu.VMEM((d_model // 128, 128), BF16),
+            pltpu.VMEM((1, d_model), F32),
+            pltpu.VMEM((1, rows), jnp.int32),
+            pltpu.VMEM(rel_bias.shape[::-1], F32),
             pltpu.SemaphoreType.DMA,
+            pltpu.SemaphoreType.DMA((3,)),
             pltpu.SemaphoreType.DMA((n_w,)),
             pltpu.SemaphoreType.DMA((2 * n_chunk,)),
             pltpu.SemaphoreType.DMA((2 * n_chunk,)),
@@ -219,51 +239,424 @@
         compiler_params=pltpu.CompilerParams(vmem_limit_bytes=66_900_000),
         cost_estimate=pl.CostEstimate(flops=4_400_000_000, bytes_accessed=104_000_000, transcendentals=131_072),
         name="self_part",
-    )(x_in, norms, tok_pos.reshape(1, rows), rel_bias.T, w_q, w_k, w_v, w_o, k_flat, v_flat)
+    )(x_in, norm_self.reshape(d_model // 128, 128), tok_pos.reshape(1, rows), rel_bias.T, w_q, w_k, w_v, w_o, k_flat, v_flat)
 
     def unflat(cache):
         return cache.reshape(t_len, n_head, d_head, rows).transpose(3, 0, 1, 2)
     return part, unflat(new_k), unflat(new_v)
 
 
-def rms_norm(values, norm_scale):
-    inv_rms = lax.rsqrt(jnp.mean(values * values, axis=-1, keepdims=True) + 1e-6)
-    return (values * inv_rms * norm_scale.astype(jnp.float32)).astype(jnp.bfloat16)
-
-
-def project(normed, weight):
-    return jnp.dot(normed, weight, preferred_element_type=jnp.float32).astype(jnp.bfloat16)
-
-
-def attend(queries, keys_all, values_all, extra):
-    scores = jnp.einsum('bhk,bthk->bht', queries, keys_all, preferred_element_type=jnp.float32) + extra
-    probs_bf = jax.nn.softmax(scores, axis=-1).astype(jnp.bfloat16)
-    mixed_out = jnp.einsum('bht,bthk->bhk', probs_bf, values_all, preferred_element_type=jnp.float32)
-    return mixed_out.astype(jnp.bfloat16)
+SLOTS = 52
+FIXED = 8
+RING = SLOTS - 2 * FIXED
+GROUP = 8
+AR_CHUNKS = 4
+LANES = 128
+
+
+def cross_kernel(n_head, x_hbm, part_hbm, ncross_hbm, nmlp_hbm, mask_hbm, cq_hbm, ck_hbm, cv_hbm, co_hbm, wg_hbm, wu_hbm, wd_hbm,
+                 out_hbm,
+                 ring, pbuf, hbuf, res, xhalf, rx1, tx2, rx2, q_ref, mix_ref, act, norm_in, nrow, mask_ref,
+                 ring_sem, load_sem, small_sem, s1_send, s1_recv, s2_send, s2_recv, s3_send, s3_recv, out_sem):
+    rows, d_model = hbuf.shape
+    half = rows // 2
+    part = half // 2
+    depth = ring.shape[1]
+    inner = q_ref.shape[1]
+    d_ff = act.shape[1]
+    width = d_model // AR_CHUNKS
+    MESH = pl.DeviceIdType.MESH
+
+    me = lax.axis_index("tp")
+    core = lax.rem(me, 2)
+    chip = me // 2
+    partner = {"tp": chip * 2 + (1 - core)}
+    across = {"tp": (1 - chip) * 2 + core}
+
+    def mine(at, n):
+        return pl.ds(pl.multiple_of(core * half + at, 16), n)
+
+    def theirs(at, n):
+        return pl.ds(pl.multiple_of((1 - core) * half + at, 16), n)
+
+    def piece(j):
+        return pl.ds(j * width, width)
+
+    per_step = GROUP * inner // depth
+    n_step = rows // GROUP
+    n_kv = 2 * per_step * n_step
+    n_gu = d_ff // LANES
+    n_d = d_model // LANES
+    o_blocks = depth // inner
+    fixed_d = 2 * FIXED
+
+    def copy_in(src, slot, used=None):
+        dst = ring.at[slot] if used is None else ring.at[slot, used]
+        pltpu.make_async_copy(src, dst, ring_sem.at[slot]).start()
+
+    def landed(slot, used=depth):
+        pltpu.make_async_copy(ck_hbm.at[pl.ds(0, used)], ring.at[slot, pl.ds(0, used)], ring_sem.at[slot]).wait()
+
+    def cols(ref, i):
+        return ref.at[:, pl.ds(i * LANES if isinstance(i, int) else pl.multiple_of(i * LANES, LANES), LANES)]
+
+    def ring_slot(n):
+        return 2 * FIXED + n % RING
+
+    def group_of(step):
+        per_half, u = n_step // 2, step % (n_step // 2)
+        return (step // per_half) * (part // GROUP) + u + (u // (part // GROUP)) * (part // GROUP)
+
+    def issue_step(step):
+        for k in range(2 * per_step):
+            src = ck_hbm if k < per_step else cv_hbm
+            at = (group_of(step) * per_step + k % per_step) * depth
+            at = at if isinstance(at, int) else pl.multiple_of(at, depth)
+            copy_in(src.at[pl.ds(at, depth)], ring_slot(step * 2 * per_step + k))
+
+    def issue_gu(i):
+        copy_in(cols(wg_hbm, i), ring_slot(n_kv + 2 * i))
+        copy_in(cols(wu_hbm, i), ring_slot(n_kv + 2 * i + 1))
+
+    def d_slot(i):
+        if isinstance(i, int) and i < fixed_d:
+            return i
+        return ring_slot(n_kv + 2 * n_gu + i - fixed_d)
+
+    def issue_d(i):
+        copy_in(cols(wd_hbm, i), d_slot(i), pl.ds(0, d_ff))
+
+    def to_partner(a, h, j, at, n):
+        return pltpu.make_async_remote_copy(
+            src_ref=pbuf.at[theirs(at, n), piece(j)], dst_ref=rx1.at[a % 2, pl.ds(at, n), piece(j)],
+            send_sem=s1_send.at[a % 2, h, j], recv_sem=s1_recv.at[a % 2, h, j], device_id=partner, device_id_type=MESH)
+
+    def to_across(a, h, j, at, n):
+        return pltpu.make_async_remote_copy(
+            src_ref=tx2.at[a % 2, pl.ds(at, n), piece(j)], dst_ref=rx2.at[a % 2, pl.ds(at, n), piece(j)],
+            send_sem=s2_send.at[a % 2, h, j], recv_sem=s2_recv.at[a % 2, h, j], device_id=across, device_id_type=MESH)
+
+    def blocks(at, n, fn):
+        def body(i, carry):
+            fn(pl.multiple_of(at + i * 16, 16))
+            return carry
+        lax.fori_loop(0, n // 16, body, 0)
+
+    def chip_sum(a, h, j, at, n):
+        to_partner(a, h, j, at, n).wait_recv()
+
+        def add(r):
+            own = pbuf[mine(r, 16), piece(j)].astype(F32)
+            tx2[a % 2, pl.ds(r, 16), piece(j)] = (own + rx1[a % 2, pl.ds(r, 16), piece(j)].astype(F32)).astype(BF16)
+        blocks(at, n, add)
+        to_across(a, h, j, at, n).start()
+
+    def full_sum(a, h, j, at, n):
+        to_across(a, h, j, at, n).wait_recv()
+
+        def add(r):
+            both = tx2[a % 2, pl.ds(r, 16), piece(j)].astype(F32) + rx2[a % 2, pl.ds(r, 16), piece(j)].astype(F32)
+            res[pl.ds(r, 16), piece(j)] = res[pl.ds(r, 16), piece(j)] + both
+        blocks(at, n, add)
+
+    def sent(a, h, at, n):
+        for j in range(AR_CHUNKS):
+            to_partner(a, h, j, at, n).wait_send()
+            to_across(a, h, j, at, n).wait_send()
+
+    def rows_back(a, h, i):
+        at = mine(h * part + i * 16, 16)
+        return pltpu.make_async_remote_copy(
+            src_ref=hbuf.at[at], dst_ref=hbuf.at[at], send_sem=s3_send.at[a % 2, h, i],
+            recv_sem=s3_recv.at[a % 2, h, i], device_id=partner, device_id_type=MESH)
+
+    def normalise(a, h):
+        norm = nrow[a:a + 1, :]
+        for i in range(part // 16):
+            r = res[h * part + i * 16:h * part + (i + 1) * 16, :]
+            inv = lax.rsqrt(jnp.mean(r * r, axis=-1, keepdims=True) + 1e-6)
+            hbuf[mine(h * part + i * 16, 16), :] = (r * inv * norm).astype(BF16)
+            rows_back(a, h, i).start()
+
+    def all_rows(a, h):
+        for i in range(part // 16):
+            rows_back(a, h, i).wait()
+
+    pieces = range(AR_CHUNKS)
+    halves = range(2)
+    first = [pltpu.make_async_copy(part_hbm.at[:, piece(j)], pbuf.at[:, piece(j)], load_sem.at[j]) for j in pieces]
+    for copy in first:
+        copy.start()
+    small = [pltpu.make_async_copy(src, dst, small_sem.at[i]) for i, (src, dst) in enumerate(
+        ((x_hbm.at[mine(0, half)], xhalf), (ncross_hbm, norm_in.at[0]), (nmlp_hbm, norm_in.at[1]), (mask_hbm, mask_ref)))]
+    for copy in small:
+        copy.start()
+    barrier = pltpu.get_barrier_semaphore()
+    for other in (partner, across):
+        pl.semaphore_signal(barrier, inc=1, device_id=other, device_id_type=MESH)
+    pl.semaphore_wait(barrier, 2)
+
+    for j in pieces:
+        first[j].wait()
+        to_partner(0, 0, j, 0, part).start()
+    for j in pieces:
+        to_partner(0, 1, j, part, part).start()
+    for i in range(FIXED):
+        copy_in(cols(cq_hbm, i), i)
+    for step in range(RING // (2 * per_step)):
+        issue_step(step)
+    for i in range(FIXED):
+        for r in range(o_blocks):
+            copy_in(cols(co_hbm, i * o_blocks + r), FIXED + i, pl.ds(r * inner, inner))
+    for h in halves:
+        for j in pieces:
+            chip_sum(0, h, j, h * part, part)
+    for copy in small:
+        copy.wait()
+    lay_row(nrow, 0, norm_in.at[0])
+    lay_row(nrow, 1, norm_in.at[1])
+    blocks(0, half, lambda r: res.__setitem__((pl.ds(r, 16), slice(None)), xhalf[pl.ds(r, 16), :].astype(F32)))
+
+    def beside(a, b, used=depth):
+        return jnp.concatenate([ring[a, 0:used, :], ring[b, 0:used, :]], axis=1)
+
+    def both_cores(ref, h):
+        return jnp.concatenate([ref[h * part:(h + 1) * part, :], ref[half + h * part:half + (h + 1) * part, :]], axis=0)
+
+    def project_q(h):
+        lhs = both_cores(hbuf, h)
+        for i in range(FIXED // 2):
+            if h == 0:
+                landed(2 * i)
+                landed(2 * i + 1)
+            y = jnp.dot(lhs, beside(2 * i, 2 * i + 1), preferred_element_type=F32).astype(BF16).astype(F32)
+            here = slice(2 * i * LANES, (2 * i + 2) * LANES)
+            q_ref[h * part:(h + 1) * part, here] = y[0:part]
+            q_ref[half + h * part:half + (h + 1) * part, here] = y[part:]
+
+    own_head = (lax.broadcasted_iota(jnp.int32, (n_head, inner), 1) // (inner // n_head)
+                == lax.broadcasted_iota(jnp.int32, (n_head, inner), 0))
+    in_slot = GROUP // per_step
+
+    def attend_step(step, carry):
+        at = pl.ds(pl.multiple_of(group_of(step) * GROUP, GROUP), GROUP)
+        ka, kb, va, vb = [ring_slot(step * 2 * per_step + k) for k in range(4)]
+        q8 = q_ref[at, :]
+        m8 = mask_ref[at, :]
+
+        def spread(r):
+            return jnp.where(own_head, jnp.broadcast_to(q8[r:r + 1, :], (n_head, inner)), 0.0).astype(BF16)
+
+        def rows_of(a, b, r):
+            here = pl.ds(r * inner, inner)
+            return jnp.concatenate([ring[a, here, :], ring[b, here, :]], axis=1)
+        landed(ka)
+        landed(kb)
+        scores = [None] * GROUP
+        for r in range(in_slot):
+            s = jnp.dot(jnp.concatenate([spread(r), spread(r + in_slot)], axis=0), rows_of(ka, kb, r), preferred_element_type=F32)
+            scores[r] = jnp.where(m8[r:r + 1, :] != 0, s[0:n_head, 0:LANES], NEG_FILL)
+            scores[r + in_slot] = jnp.where(m8[r + in_slot:r + in_slot + 1, :] != 0, s[n_head:, LANES:], NEG_FILL)
+        s = jnp.concatenate(scores, axis=0)
+        e = jnp.exp(s - jnp.max(s, axis=1, keepdims=True))
+        p = (e / jnp.sum(e, axis=1, keepdims=True)).astype(BF16)
+        landed(va)
+        landed(vb)
+        none = jnp.zeros((n_head, LANES), BF16)
+        mixed = [None] * GROUP
+        for r in range(in_slot):
+            pa = p[r * n_head:(r + 1) * n_head, :]
+            pb = p[(r + in_slot) * n_head:(r + in_slot + 1) * n_head, :]
+            lhs = jnp.concatenate([jnp.concatenate([pa, none], axis=1), jnp.concatenate([none, pb], axis=1)], axis=0)
+            y = lax.dot_general(lhs, rows_of(va, vb, r), (((1,), (1,)), ((), ())), preferred_element_type=F32)
+            mixed[r] = jnp.sum(jnp.where(own_head, y[0:n_head], 0.0), axis=0, keepdims=True)
+            mixed[r + in_slot] = jnp.sum(jnp.where(own_head, y[n_head:], 0.0), axis=0, keepdims=True)
+        mix_ref[at, :] = jnp.concatenate(mixed, axis=0)
+
+        ahead = RING // (2 * per_step)
+
+        @pl.when(step + ahead < n_step)
+        def _():
+            issue_step(step + ahead)
+
+        @pl.when(step + ahead >= n_step)
+        def _():
+            for k in range(per_step):
+                issue_gu((step + ahead - n_step) * per_step + k)
+        return carry
+
+    o_cols = o_blocks * LANES
+    per_piece_o = width // o_cols
+
+    def project_o(h, after):
+        lhs = both_cores(mix_ref, h).astype(BF16)
+        for n in range(FIXED):
+            if h == 0:
+                landed(FIXED + n)
+            w = jnp.concatenate([ring[FIXED + n, r * inner:(r + 1) * inner, :] for r in range(o_blocks)], axis=1)
+            y = jnp.dot(lhs, w, preferred_element_type=F32).astype(BF16)
+            here = slice(n * o_cols, (n + 1) * o_cols)
+            pbuf[h * part:(h + 1) * part, here] = y[0:part]
+            pbuf[half + h * part:half + (h + 1) * part, here] = y[part:]
+            if n % per_piece_o == per_piece_o - 1:
+                j = n // per_piece_o
+                to_partner(1, h, j, h * part, part).start()
+                if after and j > 0:
+                    chip_sum(1, h, j - 1, h * part, part)
+        if after:
+            chip_sum(1, h, AR_CHUNKS - 1, h * part, part)
+
+    for j in pieces:
+        full_sum(0, 0, j, 0, part)
+    normalise(0, 0)
+    all_rows(0, 0)
+    project_q(0)
+    lax.fori_loop(0, n_step // 2, attend_step, 0)
+    sent(0, 0, 0, part)
+    project_o(0, False)
+    for j in pieces:
+        full_sum(0, 1, j, part, part)
+    normalise(0, 1)
+    for j in pieces:
+        chip_sum(1, 0, j, 0, part)
+    all_rows(0, 1)
+    project_q(1)
+    lax.fori_loop(n_step // 2, n_step, attend_step, 0)
+    sent(0, 1, part, part)
+    project_o(1, True)
+    for i in range(fixed_d):
+        issue_d(i)
+    for j in pieces:
+        full_sum(1, 0, j, 0, part)
+    normalise(1, 0)
+    for j in pieces:
+        full_sum(1, 1, j, part, part)
+    normalise(1, 1)
+    for h in halves:
+        all_rows(1, h)
+        sent(1, h, h * part, part)
+
+    root = math.sqrt(2.0 / math.pi)
+    gu_ahead = (n_kv + 2 * n_gu - (n_kv + RING)) // 2
+
+    def gate_up(i, carry):
+        a, b = ring_slot(n_kv + 2 * i), ring_slot(n_kv + 2 * i + 1)
+        landed(a)
+        landed(b)
+        y = jnp.dot(hbuf[...], beside(a, b), preferred_element_type=F32)
+        u = y[:, 0:LANES]
+        gelu = 0.5 * u * (1.0 + jnp.tanh(root * (u + 0.044715 * (u * u * u))))
+        act[:, pl.ds(pl.multiple_of(i * LANES, LANES), LANES)] = (gelu * y[:, LANES:]).astype(BF16)
+
+        @pl.when(i < gu_ahead)
+        def _():
+            issue_gu(i + RING // 2)
+
+        @pl.when((i >= gu_ahead) & (i < gu_ahead + (n_d - fixed_d) // 2))
+        def _():
+            issue_d(fixed_d + 2 * (i - gu_ahead))
+            issue_d(fixed_d + 2 * (i - gu_ahead) + 1)
+        return carry
+    lax.fori_loop(0, n_gu, gate_up, 0)
+
+    per_piece = width // (2 * LANES)
+
+    def out_back(j):
+        return pltpu.make_async_remote_copy(
+            src_ref=hbuf.at[mine(0, half), piece(j)], dst_ref=hbuf.at[mine(0, half), piece(j)], send_sem=s3_send.at[0, 0, j],
+            recv_sem=s3_recv.at[0, 0, j], device_id=partner, device_id_type=MESH)
+
+    for c in pieces:
+        def down(i, carry):
+            n = c * per_piece + i
+            if (c + 1) * per_piece * 2 <= fixed_d:
+                a, b = 2 * n, 2 * n + 1
+            else:
+                a = ring_slot(n_kv + 2 * n_gu + 2 * n - fixed_d)
+                b = ring_slot(n_kv + 2 * n_gu + 2 * n + 1 - fixed_d)
+            landed(a, d_ff)
+            landed(b, d_ff)
+            y = jnp.dot(act[...], beside(a, b, d_ff), preferred_element_type=F32)
+            pbuf[:, pl.ds(pl.multiple_of(n * 2 * LANES, 2 * LANES), 2 * LANES)] = y.astype(BF16)
+            return carry
+        lax.fori_loop(0, per_piece, down, 0)
+        to_partner(2, 0, c, 0, half).start()
+        if c > 0:
+            chip_sum(2, 0, c - 1, 0, half)
+    chip_sum(2, 0, AR_CHUNKS - 1, 0, half)
+
+    def out_copy(j):
+        return pltpu.make_async_copy(hbuf.at[:, piece(j)], out_hbm.at[:, piece(j)], out_sem.at[j])
+
+    for j in pieces:
+        to_across(2, 0, j, 0, half).wait_recv()
+
+        def add(r):
+            both = tx2[0, pl.ds(r, 16), piece(j)].astype(F32) + rx2[0, pl.ds(r, 16), piece(j)].astype(F32)
+            hbuf[mine(r, 16), piece(j)] = (res[pl.ds(r, 16), piece(j)] + both).astype(BF16)
+        blocks(0, half, add)
+        out_back(j).start()
+        if j > 0:
+            out_back(j - 1).wait()
+            out_copy(j - 1).start()
+    out_back(AR_CHUNKS - 1).wait()
+    out_copy(AR_CHUNKS - 1).start()
+    sent(2, 0, 0, half)
+    for j in pieces:
+        out_copy(j).wait()
+
+
+def rest_of_layer(x_in, part, norm_cross, norm_mlp, enc_mask, cross_k, cross_v, cross_q, cross_o, w_gate, w_up, w_down):
+    rows, d_model = x_in.shape
+    _, src_len, n_head, d_head = cross_k.shape
+    inner = n_head * d_head
+    d_ff = w_gate.shape[1]
+    half = rows // 2
+    flat = (rows * inner, src_len)
+    k_flat = cross_k.transpose(0, 2, 3, 1).reshape(flat)
+    v_flat = cross_v.transpose(0, 2, 3, 1).reshape(flat)
+    square = (d_model // 128, 128)
+    return pl.pallas_call(
+        functools.partial(cross_kernel, n_head),
+        out_shape=jax.ShapeDtypeStruct((rows, d_model), BF16),
+        in_specs=[ANY] * 12,
+        out_specs=ANY,
+        scratch_shapes=[
+            pltpu.VMEM((SLOTS, d_model, LANES), BF16),
+            pltpu.VMEM((rows, d_model), BF16),
+            pltpu.VMEM((rows, d_model), BF16),
+            pltpu.VMEM((half, d_model), F32),
+            pltpu.VMEM((half, d_model), BF16),
+            pltpu.VMEM((2, half, d_model), BF16),
+            pltpu.VMEM((2, half, d_model), BF16),
+            pltpu.VMEM((2, half, d_model), BF16),
+            pltpu.VMEM((rows, inner), F32),
+            pltpu.VMEM((rows, inner), F32),
+            pltpu.VMEM((rows, d_ff), BF16),
+            pltpu.VMEM((2,) + square, BF16),
+            pltpu.VMEM((2, d_model), F32),
+            pltpu.VMEM((rows, src_len), jnp.int32),
+            pltpu.SemaphoreType.DMA((SLOTS,)),
+            pltpu.SemaphoreType.DMA((AR_CHUNKS,)),
+            pltpu.SemaphoreType.DMA((4,)),
+            pltpu.SemaphoreType.DMA((2, 2, AR_CHUNKS)),
+            pltpu.SemaphoreType.DMA((2, 2, AR_CHUNKS)),
+            pltpu.SemaphoreType.DMA((2, 2, AR_CHUNKS)),
+            pltpu.SemaphoreType.DMA((2, 2, AR_CHUNKS)),
+            pltpu.SemaphoreType.DMA((2, 2, AR_CHUNKS)),
+            pltpu.SemaphoreType.DMA((2, 2, AR_CHUNKS)),
+            pltpu.SemaphoreType.DMA((AR_CHUNKS,)),
+        ],
+        compiler_params=pltpu.CompilerParams(vmem_limit_bytes=67_000_000, collective_id=0, has_side_effects=True),
+        name="rest_part",
+    )(x_in, part, norm_cross.reshape(square), norm_mlp.reshape(square), enc_mask, cross_q, k_flat, v_flat, cross_o, w_gate, w_up, w_down)
 
 
 def solution(mesh):
-    def tp_sum(partial_out):
-        return lax.psum(partial_out.astype(jnp.bfloat16), 'tp').astype(jnp.float32)
-
     def local_layer(x_in, tok_pos, self_k, self_v, cross_k, cross_v, enc_mask, rel_bias, w_q, w_k, w_v, w_o, cross_q, cross_o, w_gate, w_up, w_down, norm_self, norm_cross, norm_mlp):
-        row_count, t_len, head_count, head_dim = self_k.shape
-        head_shape = (row_count, head_count, head_dim)
-        flat_dim = head_count * head_dim
-        norms = jnp.stack([norm_self, norm_cross, norm_mlp]).astype(F32)
-        part, new_self_k, new_self_v = self_attention(x_in, norms, tok_pos, rel_bias, w_q, w_k, w_v, w_o, self_k, self_v)
-        residual = x_in.astype(jnp.float32) + tp_sum(part)
-        normed = rms_norm(residual, norm_cross)
-        cross_queries = project(normed, cross_q).reshape(head_shape)
-        cross_extra = jnp.where(enc_mask[:, None, :] != 0, 0.0, NEG_FILL)
-        mixed_cross = attend(cross_queries, cross_k, cross_v, cross_extra)
-        residual = residual + tp_sum(jnp.dot(mixed_cross.reshape(row_count, flat_dim), cross_o, preferred_element_type=jnp.float32))
-        normed = rms_norm(residual, norm_mlp)
-        gate_pre = jnp.dot(normed, w_gate, preferred_element_type=jnp.float32)
-        up_pre = jnp.dot(normed, w_up, preferred_element_type=jnp.float32)
-        hidden = (jax.nn.gelu(gate_pre, approximate=True) * up_pre).astype(jnp.bfloat16)
-        residual = residual + tp_sum(jnp.dot(hidden, w_down, preferred_element_type=jnp.float32))
-        return residual.astype(jnp.bfloat16), new_self_k, new_self_v
+        part, new_self_k, new_self_v = self_attention(x_in, norm_self, tok_pos, rel_bias, w_q, w_k, w_v, w_o, self_k, self_v)
+        x_out = rest_of_layer(x_in, part, norm_cross, norm_mlp, enc_mask, cross_k, cross_v, cross_q, cross_o, w_gate, w_up, w_down)
+        return x_out, new_self_k, new_self_v
 
     cache_spec = P('dp', None, 'tp', None)
     split_cols = P(None, 'tp')

time: 244 us -> 127 us (0.52)
  waiting for transfers between devices: 95.8 us -> 0 us
  Pallas kernels: 39.5 us -> 124 us
  matrix products: 77.7 us -> 0 us
  between operations: 13.9 us -> 0.65 us
  other arithmetic: 10.2 us -> 0 us
  local copies, waits for them, and re-layouts: 5.59 us -> 2.29 us
    psum x3 -> x0, waiting for transfers between devices: 95.7 us -> none  [tp_sum(): return lax.psum(partial_out.astype(jnp.bfloat16), 'tp').astype(jnp.float32)]
    pallas_call x0 -> x1, Pallas kernels: none -> 83.3 us  [rest_of_layer(): pl.pallas_call(functools.partial(cross_kernel, n_head), out_shape=jax.Sha...]
    dot_general x6 -> x0, matrix products: 77.7 us -> none  [the longest x1 22.7 us: attend(): jnp.einsum('bht,bthk->bhk', probs_bf, values_all, preferred_element_type=...]
    convert_element_type x5 -> x0, other arithmetic: 4.41 us -> none  [the longest x1 3.17 us: local_layer(): return (residual.astype(jnp.bfloat16), new_self_k, new_self_v)]
    reduce_sum x2 -> x0, other arithmetic: 3.92 us -> none  [rms_norm(): jnp.mean(values * values, axis=-1, keepdims=True) + 1e-06]
  transfers between devices with their start and end apart: 3 -> 0, of which waited for: 3 -> 0; matrix products, arithmetic and copies ran while one was open for 0% -> 0% of each run, Pallas kernels for 0% -> 0%
where the time goes in v3:
time: 127 us
  Pallas kernels  124 us (98%)
  local copies, waits for them, and re-layouts  2.29 us (2%)
    pallas_call x1, Pallas kernels, rest_of_layer(): pl.pallas_call(functools.partial(cross_kernel, n_head), out_shape=jax.Sha...  83.3 us
    pallas_call x1, Pallas kernels, self_attention(): pl.pallas_call(body, out_shape=(jax.ShapeDtypeStruct((rows, w_o.shape[1])...  40.6 us

profile of v3, /device:TPU:0, one launch (start us, length us, event | category | flops | bytes accessed | tf_op | source)
XLA Modules:
  0.0 126.8 jit_solution(11430735943058457264)
XLA Ops:
  0.6 40.6 %self_part.1 = (bf16[128,4096]{1,0:T(8,128)(2,1)}, bf16[65536,128]{1,0:T(8,128)(2,1)}, bf16[65536,128]{1,0:T(8,128)(2,1)}) custom-call(bf16[128,4096]{1,0:T(8,128)(2,1)} %x_hbm.1, bf16[32,128]{1,0:T(8,128)(2,1)} %bitcast.27, s32[1,128]{1,0:T(1,128)} %bitcast.31, f32[16,32]{1,0:T(8,128)} %bitcast.28, bf16[4096,1024]{1,0:T(8,128)(2,1)} %refs_4_.1, ...), custom_call_target="tpu_custom_call" | custom-call | flops 4400000000 | bytes 104000000 | tf_op jit(solution)/shard_map/self_part/pallas_call | solution.py:212
  41.2 83.3 %rest_part.1 = bf16[128,4096]{1,0:T(8,128)(2,1)} custom-call(bf16[128,4096]{1,0:T(8,128)(2,1)} %x_hbm.1, bf16[128,4096]{1,0:T(8,128)(2,1)} %get-tuple-element.6.part_hbm, bf16[32,128]{1,0:T(8,128)(2,1)} %bitcast.29, bf16[32,128]{1,0:T(8,128)(2,1)} %bitcast.30, s32[128,128]{1,0:T(8,128)} %mask_hbm.1, bf16[4096,1024]{1,0:T(8,128)(2,1)} %cq_hbm.1, ...), custom_call_target="tpu_custom_call" | custom-call | tf_op jit(solution)/shard_map/rest_part/pallas_call | solution.py:619
  124.5 2.3 %copy.24 = bf16[128,4096]{1,0:T(8,128)(2,1)} copy(bf16[128,4096]{1,0:T(8,128)(2,1)} %rest_part.1) | data formatting | bytes 2097152

commit v4 on v3

--- a/solution.py
+++ b/solution.py
@@ -25,7 +25,7 @@
 
 def self_kernel(x_hbm, norm_hbm, pos_hbm, rel_hbm, wq_hbm, wk_hbm, wv_hbm, wo_hbm, k_hbm, v_hbm,
                 part_hbm, newk_hbm, newv_hbm,
-                xbuf, hbuf, wbuf, kvbuf, q_ref, kn_ref, hit_ref, score_ref, acc_ref,
+                xbuf, hbuf, wbuf, kvbuf, sum_ref, q_ref, kn_ref, hit_ref, score_ref, acc_ref,
                 norm_ref, nrow, pos_ref, rel_ref,
                 x_sem, small_sem, w_sem, kv_sem, out_sem, part_sem, window):
     rows, d_model = xbuf.shape
@@ -37,20 +37,19 @@
     d_head = inner // n_head
     chunk_rows = kvbuf.shape[1]
     sub = d_head // 16
-    wo_per_slot = wbuf.shape[1] // inner
-    n_wo = wo_hbm.shape[1] // COLS // wo_per_slot
+    k_rows = wbuf.shape[1]
+    n_wo = wo_hbm.shape[1] // inner
 
     def w_copy(c):
         src = (wq_hbm, wk_hbm, wv_hbm)[c // per_mat]
-        return pltpu.make_async_copy(src.at[:, pl.ds((c % per_mat) * COLS, COLS)], wbuf.at[c], w_sem.at[c])
+        return pltpu.make_async_copy(src.at[pl.ds((c % per_mat) * k_rows, k_rows)], wbuf.at[c], w_sem.at[c])
 
     def kv_copy(i):
         src = k_hbm if i < n_chunk else v_hbm
         return pltpu.make_async_copy(src.at[pl.ds((i % n_chunk) * chunk_rows, chunk_rows)], kvbuf.at[i], kv_sem.at[i])
 
     def wo_copies(i):
-        return [pltpu.make_async_copy(wo_hbm.at[:, pl.ds((i * wo_per_slot + r) * COLS, COLS)],
-                                      wbuf.at[i, pl.ds(r * inner, inner)], w_sem.at[i]) for r in range(wo_per_slot)]
+        return [pltpu.make_async_copy(wo_hbm.at[:, pl.ds(i * inner, inner)], wbuf.at[i], w_sem.at[i])]
 
     loads = [[w_copy(c)] for c in range(n_w)] + [[kv_copy(i)] for i in range(2 * n_chunk)] + [wo_copies(i) for i in range(n_wo)]
     issued = [0]
@@ -106,12 +105,20 @@
     for c in range(n_w):
         w_copy(c).wait()
         issue(c + 1 + window)
-        y = jnp.dot(hbuf[...], wbuf[c], preferred_element_type=F32).astype(BF16).astype(F32).T
-        at = (c % per_mat) * COLS
-        if c < per_mat:
-            q_ref[at:at + COLS, :] = y
-        else:
-            kn_ref[c // per_mat - 1, at:at + COLS, :] = y.astype(BF16)
+        k = c % per_mat
+        for n in range(inner // COLS):
+            here = slice(n * COLS, (n + 1) * COLS)
+            y = jnp.dot(hbuf[:, k * k_rows:(k + 1) * k_rows], wbuf[c, :, here], preferred_element_type=F32)
+            if k > 0:
+                y = y + sum_ref[:, here]
+            if k < per_mat - 1:
+                sum_ref[:, here] = y
+                continue
+            y = y.astype(BF16).astype(F32).T
+            if c < per_mat:
+                q_ref[here, :] = y
+            else:
+                kn_ref[c // per_mat - 1, here, :] = y.astype(BF16)
 
     def chunk_out(i):
         dst = newk_hbm if i < n_chunk else newv_hbm
@@ -137,7 +144,7 @@
             score_ref[h, j * T_BLOCK:(j + 1) * T_BLOCK, :] = jnp.concatenate(rows_out, axis=0)
             return carry
         lax.fori_loop(0, n_head, k_head, 0)
-        chunk_out(j).start()
+        chunk_out(j).start(priority=1)
 
     t_iota = lax.broadcasted_iota(jnp.int32, (t_len, rows), 0)
     causal = t_iota <= pos
@@ -173,20 +180,20 @@
             acc_ref[pl.ds(at, d_head), :] = acc
             return carry
         lax.fori_loop(0, n_head, v_head, 0)
-        chunk_out(n_chunk + j).start()
+        chunk_out(n_chunk + j).start(priority=1)
 
     issue(len(loads))
     hbuf[:, 0:inner] = acc_ref[...].T.astype(BF16)
-    width = wo_per_slot * COLS
     part_copies = []
     for i in range(n_wo):
         for copy in wo_copies(i):
             copy.wait()
-        for r in range(wo_per_slot):
-            at = (i * wo_per_slot + r) * COLS
-            y = jnp.dot(hbuf[:, 0:inner], wbuf[i, r * inner:(r + 1) * inner, :], preferred_element_type=F32)
+        for r in range(inner // COLS):
+            at = i * inner + r * COLS
+            y = jnp.dot(hbuf[:, 0:inner], wbuf[i, :, r * COLS:(r + 1) * COLS], preferred_element_type=F32)
             xbuf[:, at:at + COLS] = y.astype(BF16)
-        copy = pltpu.make_async_copy(xbuf.at[:, pl.ds(i * width, width)], part_hbm.at[:, pl.ds(i * width, width)], part_sem.at[i])
+        here = pl.ds(i * inner, inner)
+        copy = pltpu.make_async_copy(xbuf.at[:, here], part_hbm.at[:, here], part_sem.at[i])
         copy.start()
         part_copies.append(copy)
     for i in range(2 * n_chunk):
@@ -202,12 +209,12 @@
     flat = (t_len * inner, rows)
     k_flat = self_k.transpose(1, 2, 3, 0).reshape(flat)
     v_flat = self_v.transpose(1, 2, 3, 0).reshape(flat)
-    n_w = 3 * (inner // COLS)
+    n_w = 3 * (d_model // inner)
     n_chunk = t_len // T_BLOCK
-    n_wo = w_o.shape[1] // COLS // (d_model // inner)
+    n_wo = w_o.shape[1] // inner
 
     def body(*refs):
-        self_kernel(*refs, window=12)
+        self_kernel(*refs, window=8)
 
     part, new_k, new_v = pl.pallas_call(
         body,
@@ -218,8 +225,9 @@
         scratch_shapes=[
             pltpu.VMEM((rows, d_model), BF16),
             pltpu.VMEM((rows, d_model), BF16),
-            pltpu.VMEM((n_w, d_model, COLS), BF16),
+            pltpu.VMEM((n_w, inner, inner), BF16),
             pltpu.VMEM((2 * n_chunk, T_BLOCK * inner, rows), BF16),
+            pltpu.VMEM((rows, inner), F32),
             pltpu.VMEM((inner, rows), F32),
             pltpu.VMEM((2, inner, rows), BF16),
             pltpu.VMEM((t_len, 16, rows), BF16),

time: 127 us -> 122 us (0.961)
  Pallas kernels: 124 us -> 119 us
    pallas_call x1, Pallas kernels: 40.6 us -> 35.8 us  [self_attention(): pl.pallas_call(body, out_shape=(jax.ShapeDtypeStruct((rows, w_o.shape[1])...]
where the time goes in v4:
time: 122 us
  Pallas kernels  119 us (98%)
  local copies, waits for them, and re-layouts  2.29 us (2%)
    pallas_call x1, Pallas kernels, rest_of_layer(): pl.pallas_call(functools.partial(cross_kernel, n_head), out_shape=jax.Sha...  83.2 us
    pallas_call x1, Pallas kernels, self_attention(): pl.pallas_call(body, out_shape=(jax.ShapeDtypeStruct((rows, w_o.shape[1])...  35.8 us

profile of v4, /device:TPU:0, one launch (start us, length us, event | category | flops | bytes accessed | tf_op | source)
XLA Modules:
  0.0 121.9 jit_solution(15146832499224322734)
XLA Ops:
  0.6 35.8 %self_part.1 = (bf16[128,4096]{1,0:T(8,128)(2,1)}, bf16[65536,128]{1,0:T(8,128)(2,1)}, bf16[65536,128]{1,0:T(8,128)(2,1)}) custom-call(bf16[128,4096]{1,0:T(8,128)(2,1)} %x_hbm.1, bf16[32,128]{1,0:T(8,128)(2,1)} %bitcast.27, s32[1,128]{1,0:T(1,128)} %bitcast.31, f32[16,32]{1,0:T(8,128)} %bitcast.28, bf16[4096,1024]{1,0:T(8,128)(2,1)} %refs_4_.1, ...), custom_call_target="tpu_custom_call" | custom-call | flops 4400000000 | bytes 104000000 | tf_op jit(solution)/shard_map/self_part/pallas_call | solution.py:219
  36.4 83.2 %rest_part.1 = bf16[128,4096]{1,0:T(8,128)(2,1)} custom-call(bf16[128,4096]{1,0:T(8,128)(2,1)} %x_hbm.1, bf16[128,4096]{1,0:T(8,128)(2,1)} %get-tuple-element.6.part_hbm, bf16[32,128]{1,0:T(8,128)(2,1)} %bitcast.29, bf16[32,128]{1,0:T(8,128)(2,1)} %bitcast.30, s32[128,128]{1,0:T(8,128)} %mask_hbm.1, bf16[4096,1024]{1,0:T(8,128)(2,1)} %cq_hbm.1, ...), custom_call_target="tpu_custom_call" | custom-call | tf_op jit(solution)/shard_map/rest_part/pallas_call | solution.py:627
  119.7 2.3 %copy.24 = bf16[128,4096]{1,0:T(8,128)(2,1)} copy(bf16[128,4096]{1,0:T(8,128)(2,1)} %rest_part.1) | data formatting | bytes 2097152

commit v5 on v4

--- a/solution.py
+++ b/solution.py
@@ -254,9 +254,8 @@
     return part, unflat(new_k), unflat(new_v)
 
 
-SLOTS = 52
-FIXED = 8
-RING = SLOTS - 2 * FIXED
+RING = 20
+WIDE = 1024
 GROUP = 8
 AR_CHUNKS = 4
 LANES = 128
@@ -264,8 +263,8 @@
 
 def cross_kernel(n_head, x_hbm, part_hbm, ncross_hbm, nmlp_hbm, mask_hbm, cq_hbm, ck_hbm, cv_hbm, co_hbm, wg_hbm, wu_hbm, wd_hbm,
                  out_hbm,
-                 ring, pbuf, hbuf, res, xhalf, rx1, tx2, rx2, q_ref, mix_ref, act, norm_in, nrow, mask_ref,
-                 ring_sem, load_sem, small_sem, s1_send, s1_recv, s2_send, s2_recv, s3_send, s3_recv, out_sem):
+                 ring, pw, gw, pbuf, hbuf, res, xhalf, rx1, tx2, rx2, q_ref, mix_ref, act, norm_in, nrow, mask_ref,
+                 ring_sem, p_sem, g_sem, load_sem, small_sem, s1_send, s1_recv, s2_send, s2_recv, s3_send, s3_recv, out_sem):
     rows, d_model = hbuf.shape
     half = rows // 2
     part = half // 2
@@ -292,11 +291,11 @@
 
     per_step = GROUP * inner // depth
     n_step = rows // GROUP
-    n_kv = 2 * per_step * n_step
-    n_gu = d_ff // LANES
-    n_d = d_model // LANES
-    o_blocks = depth // inner
-    fixed_d = 2 * FIXED
+    ahead = RING // (2 * per_step)
+    n_sq = pw.shape[0] // 2
+    g_rows, g_cols = gw.shape[1:]
+    g_cut = d_model // g_rows
+    n_pair = gw.shape[0] // (2 * g_cut)
 
     def copy_in(src, slot, used=None):
         dst = ring.at[slot] if used is None else ring.at[slot, used]
@@ -305,11 +304,8 @@
     def landed(slot, used=depth):
         pltpu.make_async_copy(ck_hbm.at[pl.ds(0, used)], ring.at[slot, pl.ds(0, used)], ring_sem.at[slot]).wait()
 
-    def cols(ref, i):
-        return ref.at[:, pl.ds(i * LANES if isinstance(i, int) else pl.multiple_of(i * LANES, LANES), LANES)]
-
     def ring_slot(n):
-        return 2 * FIXED + n % RING
+        return n % RING
 
     def group_of(step):
         per_half, u = n_step // 2, step % (n_step // 2)
@@ -322,17 +318,33 @@
             at = at if isinstance(at, int) else pl.multiple_of(at, depth)
             copy_in(src.at[pl.ds(at, depth)], ring_slot(step * 2 * per_step + k))
 
-    def issue_gu(i):
-        copy_in(cols(wg_hbm, i), ring_slot(n_kv + 2 * i))
-        copy_in(cols(wu_hbm, i), ring_slot(n_kv + 2 * i + 1))
-
-    def d_slot(i):
-        if isinstance(i, int) and i < fixed_d:
-            return i
-        return ring_slot(n_kv + 2 * n_gu + i - fixed_d)
+    def q_copy(k):
+        return pltpu.make_async_copy(cq_hbm.at[pl.ds(k * WIDE, WIDE)], pw.at[k], p_sem.at[k])
+
+    def o_copy(i):
+        return pltpu.make_async_copy(co_hbm.at[:, pl.ds(i * WIDE, WIDE)], pw.at[n_sq + i], p_sem.at[n_sq + i])
+
+    def gu_square(i):
+        src = wg_hbm if i < n_sq else wu_hbm
+        return pltpu.make_async_copy(src.at[pl.ds((i % n_sq) * WIDE, WIDE), pl.ds(0, WIDE)], pw.at[i], p_sem.at[i])
+
+    def gu_tall(pair, i):
+        src = wg_hbm if i < g_cut else wu_hbm
+        slot = (pair % n_pair) * 2 * g_cut + i
+        return pltpu.make_async_copy(src.at[pl.ds((i % g_cut) * g_rows, g_rows), pl.ds(WIDE + pair * g_cols, g_cols)],
+                                     gw.at[slot], g_sem.at[slot])
+
+    d_cut = -(-d_ff // WIDE)
+    d_narrow = 2 * WIDE // LANES
+
+    def d_square(c, i):
+        slot = (c - 2) * d_cut + i
+        n = min(WIDE, d_ff - i * WIDE)
+        return pltpu.make_async_copy(wd_hbm.at[pl.ds(i * WIDE, n), pl.ds(c * WIDE, WIDE)],
+                                     pw.at[slot, pl.ds(0, n)], p_sem.at[slot])
 
     def issue_d(i):
-        copy_in(cols(wd_hbm, i), d_slot(i), pl.ds(0, d_ff))
+        copy_in(wd_hbm.at[:, pl.ds(i * LANES, LANES)], i, pl.ds(0, d_ff))
 
     def to_partner(a, h, j, at, n):
         return pltpu.make_async_remote_copy(
@@ -409,13 +421,14 @@
         to_partner(0, 0, j, 0, part).start()
     for j in pieces:
         to_partner(0, 1, j, part, part).start()
-    for i in range(FIXED):
-        copy_in(cols(cq_hbm, i), i)
-    for step in range(RING // (2 * per_step)):
+    for k in range(n_sq):
+        q_copy(k).start()
+    for step in range(ahead):
         issue_step(step)
-    for i in range(FIXED):
-        for r in range(o_blocks):
-            copy_in(cols(co_hbm, i * o_blocks + r), FIXED + i, pl.ds(r * inner, inner))
+    for i in range(n_sq):
+        o_copy(i).start()
+    for i in range(2 * g_cut):
+        gu_tall(0, i).start()
     for h in halves:
         for j in pieces:
             chip_sum(0, h, j, h * part, part)
@@ -428,19 +441,25 @@
     def beside(a, b, used=depth):
         return jnp.concatenate([ring[a, 0:used, :], ring[b, 0:used, :]], axis=1)
 
-    def both_cores(ref, h):
-        return jnp.concatenate([ref[h * part:(h + 1) * part, :], ref[half + h * part:half + (h + 1) * part, :]], axis=0)
+    def both_cores(ref, h, at=slice(None)):
+        return jnp.concatenate([ref[h * part:(h + 1) * part, at], ref[half + h * part:half + (h + 1) * part, at]], axis=0)
 
     def project_q(h):
-        lhs = both_cores(hbuf, h)
-        for i in range(FIXED // 2):
-            if h == 0:
-                landed(2 * i)
-                landed(2 * i + 1)
-            y = jnp.dot(lhs, beside(2 * i, 2 * i + 1), preferred_element_type=F32).astype(BF16).astype(F32)
-            here = slice(2 * i * LANES, (2 * i + 2) * LANES)
+        if h == 0:
+            for k in range(n_sq):
+                q_copy(k).wait()
+
+        def block(n, carry):
+            here = pl.ds(pl.multiple_of(n * COLS, COLS), COLS)
+            y = None
+            for k in range(n_sq):
+                z = jnp.dot(both_cores(hbuf, h, slice(k * WIDE, (k + 1) * WIDE)), pw[k, :, here], preferred_element_type=F32)
+                y = z if y is None else y + z
+            y = y.astype(BF16).astype(F32)
             q_ref[h * part:(h + 1) * part, here] = y[0:part]
             q_ref[half + h * part:half + (h + 1) * part, here] = y[part:]
+            return carry
+        lax.fori_loop(0, inner // COLS, block, 0)
 
     own_head = (lax.broadcasted_iota(jnp.int32, (n_head, inner), 1) // (inner // n_head)
                 == lax.broadcasted_iota(jnp.int32, (n_head, inner), 0))
@@ -481,36 +500,24 @@
             mixed[r + in_slot] = jnp.sum(jnp.where(own_head, y[n_head:], 0.0), axis=0, keepdims=True)
         mix_ref[at, :] = jnp.concatenate(mixed, axis=0)
 
-        ahead = RING // (2 * per_step)
-
         @pl.when(step + ahead < n_step)
         def _():
             issue_step(step + ahead)
-
-        @pl.when(step + ahead >= n_step)
-        def _():
-            for k in range(per_step):
-                issue_gu((step + ahead - n_step) * per_step + k)
         return carry
-
-    o_cols = o_blocks * LANES
-    per_piece_o = width // o_cols
 
     def project_o(h, after):
         lhs = both_cores(mix_ref, h).astype(BF16)
-        for n in range(FIXED):
+        for j in pieces:
             if h == 0:
-                landed(FIXED + n)
-            w = jnp.concatenate([ring[FIXED + n, r * inner:(r + 1) * inner, :] for r in range(o_blocks)], axis=1)
-            y = jnp.dot(lhs, w, preferred_element_type=F32).astype(BF16)
-            here = slice(n * o_cols, (n + 1) * o_cols)
-            pbuf[h * part:(h + 1) * part, here] = y[0:part]
-            pbuf[half + h * part:half + (h + 1) * part, here] = y[part:]
-            if n % per_piece_o == per_piece_o - 1:
-                j = n // per_piece_o
-                to_partner(1, h, j, h * part, part).start()
-                if after and j > 0:
-                    chip_sum(1, h, j - 1, h * part, part)
+                o_copy(j).wait()
+            for n in range(WIDE // COLS):
+                y = jnp.dot(lhs, pw[n_sq + j, :, n * COLS:(n + 1) * COLS], preferred_element_type=F32).astype(BF16)
+                here = slice(j * WIDE + n * COLS, j * WIDE + (n + 1) * COLS)
+                pbuf[h * part:(h + 1) * part, here] = y[0:part]
+                pbuf[half + h * part:half + (h + 1) * part, here] = y[part:]
+            to_partner(1, h, j, h * part, part).start()
+            if after and j > 0:
+                chip_sum(1, h, j - 1, h * part, part)
         if after:
             chip_sum(1, h, AR_CHUNKS - 1, h * part, part)
 
@@ -520,6 +527,9 @@
     all_rows(0, 0)
     project_q(0)
     lax.fori_loop(0, n_step // 2, attend_step, 0)
+    for pair in range(1, n_pair):
+        for i in range(2 * g_cut):
+            gu_tall(pair, i).start()
     sent(0, 0, 0, part)
     project_o(0, False)
     for j in pieces:
@@ -529,10 +539,14 @@
         chip_sum(1, 0, j, 0, part)
     all_rows(0, 1)
     project_q(1)
+    for i in range(n_sq):
+        gu_square(i).start()
     lax.fori_loop(n_step // 2, n_step, attend_step, 0)
     sent(0, 1, part, part)
     project_o(1, True)
-    for i in range(fixed_d):
+    for i in range(n_sq):
+        gu_square(n_sq + i).start()
+    for i in range(d_narrow):
         issue_d(i)
     for j in pieces:
         full_sum(1, 0, j, 0, part)
@@ -545,29 +559,54 @@
         sent(1, h, h * part, part)
 
     root = math.sqrt(2.0 / math.pi)
-    gu_ahead = (n_kv + 2 * n_gu - (n_kv + RING)) // 2
-
-    def gate_up(i, carry):
-        a, b = ring_slot(n_kv + 2 * i), ring_slot(n_kv + 2 * i + 1)
-        landed(a)
-        landed(b)
-        y = jnp.dot(hbuf[...], beside(a, b), preferred_element_type=F32)
-        u = y[:, 0:LANES]
+    def mlp_block(at, gate, up):
+        u, v = None, None
+        for k in range(len(gate)):
+            n = d_model // len(gate)
+            lhs = hbuf[:, k * n:(k + 1) * n]
+            y = jnp.dot(lhs, gate[k], preferred_element_type=F32)
+            z = jnp.dot(lhs, up[k], preferred_element_type=F32)
+            u, v = (y, z) if u is None else (u + y, v + z)
         gelu = 0.5 * u * (1.0 + jnp.tanh(root * (u + 0.044715 * (u * u * u))))
-        act[:, pl.ds(pl.multiple_of(i * LANES, LANES), LANES)] = (gelu * y[:, LANES:]).astype(BF16)
-
-        @pl.when(i < gu_ahead)
-        def _():
-            issue_gu(i + RING // 2)
-
-        @pl.when((i >= gu_ahead) & (i < gu_ahead + (n_d - fixed_d) // 2))
-        def _():
-            issue_d(fixed_d + 2 * (i - gu_ahead))
-            issue_d(fixed_d + 2 * (i - gu_ahead) + 1)
-        return carry
-    lax.fori_loop(0, n_gu, gate_up, 0)
-
-    per_piece = width // (2 * LANES)
+        act[:, pl.ds(at, COLS)] = (gelu * v).astype(BF16)
+
+    def mlp_tall(pair):
+        for i in range(2 * g_cut):
+            gu_tall(pair, i).wait()
+        base = (pair % n_pair) * 2 * g_cut
+
+        def block(n, carry):
+            here = pl.ds(pl.multiple_of(n * COLS, COLS), COLS)
+            mlp_block(pl.multiple_of(WIDE + pair * g_cols + n * COLS, COLS), [gw[base + i, :, here] for i in range(g_cut)],
+                      [gw[base + g_cut + i, :, here] for i in range(g_cut)])
+            return carry
+        lax.fori_loop(0, g_cols // COLS, block, 0)
+
+    def mlp_square():
+        for i in range(2 * n_sq):
+            gu_square(i).wait()
+
+        def block(n, carry):
+            here = pl.ds(pl.multiple_of(n * COLS, COLS), COLS)
+            mlp_block(pl.multiple_of(n * COLS, COLS), [pw[i, :, here] for i in range(n_sq)],
+                      [pw[n_sq + i, :, here] for i in range(n_sq)])
+            return carry
+        lax.fori_loop(0, WIDE // COLS, block, 0)
+
+    n_tall = (d_ff - WIDE) // g_cols
+    for pair in range(n_pair):
+        mlp_tall(pair)
+        if pair + n_pair < n_tall:
+            for i in range(2 * g_cut):
+                gu_tall(pair + n_pair, i).start()
+    mlp_square()
+    for c in (2, 3):
+        for i in range(d_cut):
+            d_square(c, i).start()
+    for pair in range(n_pair, n_tall):
+        mlp_tall(pair)
+
+    per_piece = width // COLS
 
     def out_back(j):
         return pltpu.make_async_remote_copy(
@@ -575,17 +614,24 @@
             recv_sem=s3_recv.at[0, 0, j], device_id=partner, device_id_type=MESH)
 
     for c in pieces:
+        if c >= 2:
+            for i in range(d_cut):
+                d_square(c, i).wait()
+
         def down(i, carry):
             n = c * per_piece + i
-            if (c + 1) * per_piece * 2 <= fixed_d:
-                a, b = 2 * n, 2 * n + 1
+            if c < 2:
+                landed(2 * n, d_ff)
+                landed(2 * n + 1, d_ff)
+                y = jnp.dot(act[...], beside(2 * n, 2 * n + 1, d_ff), preferred_element_type=F32)
             else:
-                a = ring_slot(n_kv + 2 * n_gu + 2 * n - fixed_d)
-                b = ring_slot(n_kv + 2 * n_gu + 2 * n + 1 - fixed_d)
-            landed(a, d_ff)
-            landed(b, d_ff)
-            y = jnp.dot(act[...], beside(a, b, d_ff), preferred_element_type=F32)
-            pbuf[:, pl.ds(pl.multiple_of(n * 2 * LANES, 2 * LANES), 2 * LANES)] = y.astype(BF16)
+                y = None
+                for k in range(d_cut):
+                    at, rest = k * WIDE, min(WIDE, d_ff - k * WIDE)
+                    w = pw[(c - 2) * d_cut + k, 0:rest, pl.ds(pl.multiple_of(i * COLS, COLS), COLS)]
+                    z = jnp.dot(act[:, at:at + rest], w, preferred_element_type=F32)
+                    y = z if y is None else y + z
+            pbuf[:, pl.ds(pl.multiple_of(n * COLS, COLS), COLS)] = y.astype(BF16)
             return carry
         lax.fori_loop(0, per_piece, down, 0)
         to_partner(2, 0, c, 0, half).start()
@@ -630,7 +676,9 @@
         in_specs=[ANY] * 12,
         out_specs=ANY,
         scratch_shapes=[
-            pltpu.VMEM((SLOTS, d_model, LANES), BF16),
+            pltpu.VMEM((RING, d_model, LANES), BF16),
+            pltpu.VMEM((8, WIDE, WIDE), BF16),
+            pltpu.VMEM((8, d_model // 2, 512), BF16),
             pltpu.VMEM((rows, d_model), BF16),
             pltpu.VMEM((rows, d_model), BF16),
             pltpu.VMEM((half, d_model), F32),
@@ -644,7 +692,9 @@
             pltpu.VMEM((2,) + square, BF16),
             pltpu.VMEM((2, d_model), F32),
             pltpu.VMEM((rows, src_len), jnp.int32),
-            pltpu.SemaphoreType.DMA((SLOTS,)),
+            pltpu.SemaphoreType.DMA((RING,)),
+            pltpu.SemaphoreType.DMA((8,)),
+            pltpu.SemaphoreType.DMA((8,)),
             pltpu.SemaphoreType.DMA((AR_CHUNKS,)),
             pltpu.SemaphoreType.DMA((4,)),
             pltpu.SemaphoreType.DMA((2, 2, AR_CHUNKS)),

time: 122 us -> 120 us (0.984)
  Pallas kernels: 119 us -> 117 us
    pallas_call x1, Pallas kernels: 83.2 us -> 80.8 us  [rest_of_layer(): pl.pallas_call(functools.partial(cross_kernel, n_head), out_shape=jax.Sha...]
where the time goes in v5:
time: 120 us
  Pallas kernels  117 us (98%)
  local copies, waits for them, and re-layouts  2.29 us (2%)
    pallas_call x1, Pallas kernels, rest_of_layer(): pl.pallas_call(functools.partial(cross_kernel, n_head), out_shape=jax.Sha...  80.8 us
    pallas_call x1, Pallas kernels, self_attention(): pl.pallas_call(body, out_shape=(jax.ShapeDtypeStruct((rows, w_o.shape[1])...  35.8 us

profile of v5, /device:TPU:0, one launch (start us, length us, event | category | flops | bytes accessed | tf_op | source)
XLA Modules:
  0.0 119.5 jit_solution(15320556391315648299)
XLA Ops:
  0.6 35.8 %self_part.1 = (bf16[128,4096]{1,0:T(8,128)(2,1)}, bf16[65536,128]{1,0:T(8,128)(2,1)}, bf16[65536,128]{1,0:T(8,128)(2,1)}) custom-call(bf16[128,4096]{1,0:T(8,128)(2,1)} %x_hbm.1, bf16[32,128]{1,0:T(8,128)(2,1)} %bitcast.27, s32[1,128]{1,0:T(1,128)} %bitcast.31, f32[16,32]{1,0:T(8,128)} %bitcast.28, bf16[4096,1024]{1,0:T(8,128)(2,1)} %refs_4_.1, ...), custom_call_target="tpu_custom_call" | custom-call | flops 4400000000 | bytes 104000000 | tf_op jit(solution)/shard_map/self_part/pallas_call | solution.py:219
  36.4 80.8 %rest_part.1 = bf16[128,4096]{1,0:T(8,128)(2,1)} custom-call(bf16[128,4096]{1,0:T(8,128)(2,1)} %x_hbm.1, bf16[128,4096]{1,0:T(8,128)(2,1)} %get-tuple-element.6.part_hbm, bf16[32,128]{1,0:T(8,128)(2,1)} %bitcast.29, bf16[32,128]{1,0:T(8,128)(2,1)} %bitcast.30, s32[128,128]{1,0:T(8,128)} %mask_hbm.1, bf16[4096,1024]{1,0:T(8,128)(2,1)} %cq_hbm.1, ...), custom_call_target="tpu_custom_call" | custom-call | tf_op jit(solution)/shard_map/rest_part/pallas_call | solution.py:673
  117.2 2.3 %copy.24 = bf16[128,4096]{1,0:T(8,128)(2,1)} copy(bf16[128,4096]{1,0:T(8,128)(2,1)} %rest_part.1) | data formatting | bytes 2097152

commit v6 on v5

--- a/solution.py
+++ b/solution.py
@@ -214,7 +214,7 @@
     n_wo = w_o.shape[1] // inner
 
     def body(*refs):
-        self_kernel(*refs, window=8)
+        self_kernel(*refs, window=14)
 
     part, new_k, new_v = pl.pallas_call(
         body,
@@ -527,9 +527,6 @@
     all_rows(0, 0)
     project_q(0)
     lax.fori_loop(0, n_step // 2, attend_step, 0)
-    for pair in range(1, n_pair):
-        for i in range(2 * g_cut):
-            gu_tall(pair, i).start()
     sent(0, 0, 0, part)
     project_o(0, False)
     for j in pieces:
@@ -539,9 +536,12 @@
         chip_sum(1, 0, j, 0, part)
     all_rows(0, 1)
     project_q(1)
+    lax.fori_loop(n_step // 2, n_step, attend_step, 0)
+    for pair in range(1, n_pair):
+        for i in range(2 * g_cut):
+            gu_tall(pair, i).start()
     for i in range(n_sq):
         gu_square(i).start()
-    lax.fori_loop(n_step // 2, n_step, attend_step, 0)
     sent(0, 1, part, part)
     project_o(1, True)
     for i in range(n_sq):
@@ -606,58 +606,86 @@
     for pair in range(n_pair, n_tall):
         mlp_tall(pair)
 
-    per_piece = width // COLS
-
-    def out_back(j):
+    n_last = 2 * AR_CHUNKS
+    w_last = d_model // n_last
+    per_piece = w_last // COLS
+
+    def last_piece(j):
+        return pl.ds(j * w_last, w_last)
+
+    def last_to_partner(j):
         return pltpu.make_async_remote_copy(
-            src_ref=hbuf.at[mine(0, half), piece(j)], dst_ref=hbuf.at[mine(0, half), piece(j)], send_sem=s3_send.at[0, 0, j],
-            recv_sem=s3_recv.at[0, 0, j], device_id=partner, device_id_type=MESH)
-
-    for c in pieces:
-        if c >= 2:
+            src_ref=pbuf.at[theirs(0, half), last_piece(j)], dst_ref=rx1.at[0, :, last_piece(j)],
+            send_sem=s1_send.at[0, j // AR_CHUNKS, j % AR_CHUNKS], recv_sem=s1_recv.at[0, j // AR_CHUNKS, j % AR_CHUNKS],
+            device_id=partner, device_id_type=MESH)
+
+    def last_to_across(j):
+        return pltpu.make_async_remote_copy(
+            src_ref=tx2.at[0, :, last_piece(j)], dst_ref=rx2.at[0, :, last_piece(j)],
+            send_sem=s2_send.at[0, j // AR_CHUNKS, j % AR_CHUNKS], recv_sem=s2_recv.at[0, j // AR_CHUNKS, j % AR_CHUNKS],
+            device_id=across, device_id_type=MESH)
+
+    def last_back(j):
+        return pltpu.make_async_remote_copy(
+            src_ref=hbuf.at[mine(0, half), last_piece(j)], dst_ref=out_hbm.at[mine(0, half), last_piece(j)],
+            send_sem=s3_send.at[0, j // AR_CHUNKS, j % AR_CHUNKS], recv_sem=s3_recv.at[0, j // AR_CHUNKS, j % AR_CHUNKS],
+            device_id=partner, device_id_type=MESH)
+
+    def last_own(j):
+        return pltpu.make_async_copy(hbuf.at[mine(0, half), last_piece(j)], out_hbm.at[mine(0, half), last_piece(j)], out_sem.at[j])
+
+    def last_chip_sum(j):
+        last_to_partner(j).wait_recv()
+
+        def add(r):
+            own = pbuf[mine(r, 16), last_piece(j)].astype(F32)
+            tx2[0, pl.ds(r, 16), last_piece(j)] = (own + rx1[0, pl.ds(r, 16), last_piece(j)].astype(F32)).astype(BF16)
+        blocks(0, half, add)
+        last_to_across(j).start()
+
+    for c in range(n_last):
+        at = c * w_last
+        block_c, in_block = at // WIDE, at % WIDE
+        if block_c >= 2 and in_block == 0:
             for i in range(d_cut):
-                d_square(c, i).wait()
+                d_square(block_c, i).wait()
 
         def down(i, carry):
             n = c * per_piece + i
-            if c < 2:
+            if block_c < 2:
                 landed(2 * n, d_ff)
                 landed(2 * n + 1, d_ff)
                 y = jnp.dot(act[...], beside(2 * n, 2 * n + 1, d_ff), preferred_element_type=F32)
             else:
                 y = None
                 for k in range(d_cut):
-                    at, rest = k * WIDE, min(WIDE, d_ff - k * WIDE)
-                    w = pw[(c - 2) * d_cut + k, 0:rest, pl.ds(pl.multiple_of(i * COLS, COLS), COLS)]
-                    z = jnp.dot(act[:, at:at + rest], w, preferred_element_type=F32)
+                    row, rest = k * WIDE, min(WIDE, d_ff - k * WIDE)
+                    w = pw[(block_c - 2) * d_cut + k, 0:rest, pl.ds(pl.multiple_of(in_block + i * COLS, COLS), COLS)]
+                    z = jnp.dot(act[:, row:row + rest], w, preferred_element_type=F32)
                     y = z if y is None else y + z
             pbuf[:, pl.ds(pl.multiple_of(n * COLS, COLS), COLS)] = y.astype(BF16)
             return carry
         lax.fori_loop(0, per_piece, down, 0)
-        to_partner(2, 0, c, 0, half).start()
-        if c > 0:
-            chip_sum(2, 0, c - 1, 0, half)
-    chip_sum(2, 0, AR_CHUNKS - 1, 0, half)
-
-    def out_copy(j):
-        return pltpu.make_async_copy(hbuf.at[:, piece(j)], out_hbm.at[:, piece(j)], out_sem.at[j])
-
-    for j in pieces:
-        to_across(2, 0, j, 0, half).wait_recv()
+        last_to_partner(c).start()
+        if c > 1:
+            last_chip_sum(c - 2)
+    last_chip_sum(n_last - 2)
+    last_chip_sum(n_last - 1)
+
+    for j in range(n_last):
+        last_to_across(j).wait_recv()
 
         def add(r):
-            both = tx2[0, pl.ds(r, 16), piece(j)].astype(F32) + rx2[0, pl.ds(r, 16), piece(j)].astype(F32)
-            hbuf[mine(r, 16), piece(j)] = (res[pl.ds(r, 16), piece(j)] + both).astype(BF16)
+            both = tx2[0, pl.ds(r, 16), last_piece(j)].astype(F32) + rx2[0, pl.ds(r, 16), last_piece(j)].astype(F32)
+            hbuf[mine(r, 16), last_piece(j)] = (res[pl.ds(r, 16), last_piece(j)] + both).astype(BF16)
         blocks(0, half, add)
-        out_back(j).start()
-        if j > 0:
-            out_back(j - 1).wait()
-            out_copy(j - 1).start()
-    out_back(AR_CHUNKS - 1).wait()
-    out_copy(AR_CHUNKS - 1).start()
-    sent(2, 0, 0, half)
-    for j in pieces:
-        out_copy(j).wait()
+        last_back(j).start()
+        last_own(j).start()
+    for j in range(n_last):
+        last_to_partner(j).wait_send()
+        last_to_across(j).wait_send()
+        last_back(j).wait()
+        last_own(j).wait()
 
 
 def rest_of_layer(x_in, part, norm_cross, norm_mlp, enc_mask, cross_k, cross_v, cross_q, cross_o, w_gate, w_up, w_down):
@@ -703,7 +731,7 @@
             pltpu.SemaphoreType.DMA((2, 2, AR_CHUNKS)),
             pltpu.SemaphoreType.DMA((2, 2, AR_CHUNKS)),
             pltpu.SemaphoreType.DMA((2, 2, AR_CHUNKS)),
-            pltpu.SemaphoreType.DMA((AR_CHUNKS,)),
+            pltpu.SemaphoreType.DMA((2 * AR_CHUNKS,)),
         ],
         compiler_params=pltpu.CompilerParams(vmem_limit_bytes=67_000_000, collective_id=0, has_side_effects=True),
         name="rest_part",

time: 120 us -> 119 us (level)
    pallas_call x1, Pallas kernels: 80.8 us -> 79.4 us  [rest_of_layer(): pl.pallas_call(functools.partial(cross_kernel, n_head), out_shape=jax.Sha...]
where the time goes in v6:
time: 119 us
  Pallas kernels  116 us (97%)
  local copies, waits for them, and re-layouts  2.29 us (2%)
    pallas_call x1, Pallas kernels, rest_of_layer(): pl.pallas_call(functools.partial(cross_kernel, n_head), out_shape=jax.Sha...  79.4 us
    pallas_call x1, Pallas kernels, self_attention(): pl.pallas_call(body, out_shape=(jax.ShapeDtypeStruct((rows, w_o.shape[1])...  36.5 us

profile of v6, /device:TPU:0, one launch (start us, length us, event | category | flops | bytes accessed | tf_op | source)
XLA Modules:
  0.0 118.8 jit_solution(6000405990625736888)
XLA Ops:
  0.6 36.5 %self_part.1 = (bf16[128,4096]{1,0:T(8,128)(2,1)}, bf16[65536,128]{1,0:T(8,128)(2,1)}, bf16[65536,128]{1,0:T(8,128)(2,1)}) custom-call(bf16[128,4096]{1,0:T(8,128)(2,1)} %x_hbm.1, bf16[32,128]{1,0:T(8,128)(2,1)} %bitcast.27, s32[1,128]{1,0:T(1,128)} %bitcast.31, f32[16,32]{1,0:T(8,128)} %bitcast.28, bf16[4096,1024]{1,0:T(8,128)(2,1)} %refs_4_.1, ...), custom_call_target="tpu_custom_call" | custom-call | flops 4400000000 | bytes 104000000 | tf_op jit(solution)/shard_map/self_part/pallas_call | solution.py:219
  37.2 79.4 %rest_part.1 = bf16[128,4096]{1,0:T(8,128)(2,1)} custom-call(bf16[128,4096]{1,0:T(8,128)(2,1)} %x_hbm.1, bf16[128,4096]{1,0:T(8,128)(2,1)} %get-tuple-element.6.part_hbm, bf16[32,128]{1,0:T(8,128)(2,1)} %bitcast.29, bf16[32,128]{1,0:T(8,128)(2,1)} %bitcast.30, s32[128,128]{1,0:T(8,128)} %mask_hbm.1, bf16[4096,1024]{1,0:T(8,128)(2,1)} %cq_hbm.1, ...), custom_call_target="tpu_custom_call" | custom-call | tf_op jit(solution)/shard_map/rest_part/pallas_call | solution.py:701
  116.6 2.3 %copy.24 = bf16[128,4096]{1,0:T(8,128)(2,1)} copy(bf16[128,4096]{1,0:T(8,128)(2,1)} %rest_part.1) | data formatting | bytes 2097152

commit v7 on v6

--- a/solution.py
+++ b/solution.py
@@ -15,6 +15,21 @@
 VMEM = pl.BlockSpec(memory_space=pltpu.VMEM)
 COLS = 256
 T_BLOCK = 8
+
+
+def multiple_of(at, n):
+    return at if isinstance(at, int) else pl.multiple_of(at, n)
+
+
+def twice(n, body):
+    def pair(i, carry):
+        body(2 * i, carry)
+        body(2 * i + 1, carry)
+        return carry
+    if n == 2:
+        pair(0, 0)
+    else:
+        lax.fori_loop(0, n // 2, pair, 0)
 
 
 def lay_row(dst, at, norm):
@@ -95,7 +110,7 @@
     norm = nrow[0:1, :]
 
     def norm_rows(i, carry):
-        at = pl.ds(pl.multiple_of(i * block, block), block)
+        at = pl.ds(multiple_of(i * block, block), block)
         r = xbuf[at, :].astype(F32)
         inv = lax.rsqrt(jnp.mean(r * r, axis=-1, keepdims=True) + 1e-6)
         hbuf[at, :] = (r * inv * norm).astype(BF16)
@@ -129,12 +144,12 @@
         issue(n_w + j + 1 + window)
 
         def k_head(h, carry):
-            at = pl.multiple_of(h * d_head, d_head)
+            at = multiple_of(h * d_head, d_head)
             q = q_ref[pl.ds(at, d_head), :]
             kn = kn_ref[0, pl.ds(at, d_head), :].reshape(sub, 16, rows)
             rows_out = []
             for tt in range(T_BLOCK):
-                here = pl.ds(pl.multiple_of(tt * inner + at, d_head), d_head)
+                here = pl.ds(multiple_of(tt * inner + at, d_head), d_head)
                 old = kvbuf[j, here, :].reshape(sub, 16, rows)
                 hit = hit_ref[j * T_BLOCK + tt] != 0
                 new = jnp.where(hit[None], kn, old)
@@ -143,7 +158,7 @@
                 rows_out.append(jnp.sum(prod, axis=0, keepdims=True))
             score_ref[h, j * T_BLOCK:(j + 1) * T_BLOCK, :] = jnp.concatenate(rows_out, axis=0)
             return carry
-        lax.fori_loop(0, n_head, k_head, 0)
+        twice(n_head, k_head)
         chunk_out(j).start(priority=1)
 
     t_iota = lax.broadcasted_iota(jnp.int32, (t_len, rows), 0)
@@ -166,12 +181,12 @@
         issue(n_w + n_chunk + j + 1 + window)
 
         def v_head(h, carry):
-            at = pl.multiple_of(h * d_head, d_head)
+            at = multiple_of(h * d_head, d_head)
             vn = kn_ref[1, pl.ds(at, d_head), :].reshape(sub, 16, rows)
             p = score_ref[h, j * T_BLOCK:(j + 1) * T_BLOCK, :]
             acc = acc_ref[pl.ds(at, d_head), :]
             for tt in range(T_BLOCK):
-                here = pl.ds(pl.multiple_of(tt * inner + at, d_head), d_head)
+                here = pl.ds(multiple_of(tt * inner + at, d_head), d_head)
                 old = kvbuf[n_chunk + j, here, :].reshape(sub, 16, rows)
                 hit = hit_ref[j * T_BLOCK + tt] != 0
                 new = jnp.where(hit[None], vn, old)
@@ -179,7 +194,7 @@
                 acc = acc + new.reshape(d_head, rows).astype(F32) * p[tt:tt + 1, :]
             acc_ref[pl.ds(at, d_head), :] = acc
             return carry
-        lax.fori_loop(0, n_head, v_head, 0)
+        twice(n_head, v_head)
         chunk_out(n_chunk + j).start(priority=1)
 
     issue(len(loads))
@@ -214,7 +229,7 @@
     n_wo = w_o.shape[1] // inner
 
     def body(*refs):
-        self_kernel(*refs, window=14)
+        self_kernel(*refs, window=8)
 
     part, new_k, new_v = pl.pallas_call(
         body,
@@ -263,7 +278,7 @@
 
 def cross_kernel(n_head, x_hbm, part_hbm, ncross_hbm, nmlp_hbm, mask_hbm, cq_hbm, ck_hbm, cv_hbm, co_hbm, wg_hbm, wu_hbm, wd_hbm,
                  out_hbm,
-                 ring, pw, gw, pbuf, hbuf, res, xhalf, rx1, tx2, rx2, q_ref, mix_ref, act, norm_in, nrow, mask_ref,
+                 ring, pw, gw, pbuf, hbuf, res, xhalf, rx1, tx2, rx2, q_ref, mix_ref, p_ref, act, norm_in, nrow, mask_ref,
                  ring_sem, p_sem, g_sem, load_sem, small_sem, s1_send, s1_recv, s2_send, s2_recv, s3_send, s3_recv, out_sem):
     rows, d_model = hbuf.shape
     half = rows // 2
@@ -281,10 +296,10 @@
     across = {"tp": (1 - chip) * 2 + core}
 
     def mine(at, n):
-        return pl.ds(pl.multiple_of(core * half + at, 16), n)
+        return pl.ds(multiple_of(core * half + at, 16), n)
 
     def theirs(at, n):
-        return pl.ds(pl.multiple_of((1 - core) * half + at, 16), n)
+        return pl.ds(multiple_of((1 - core) * half + at, 16), n)
 
     def piece(j):
         return pl.ds(j * width, width)
@@ -304,19 +319,18 @@
     def landed(slot, used=depth):
         pltpu.make_async_copy(ck_hbm.at[pl.ds(0, used)], ring.at[slot, pl.ds(0, used)], ring_sem.at[slot]).wait()
 
-    def ring_slot(n):
-        return n % RING
-
     def group_of(step):
         per_half, u = n_step // 2, step % (n_step // 2)
         return (step // per_half) * (part // GROUP) + u + (u // (part // GROUP)) * (part // GROUP)
 
-    def issue_step(step):
-        for k in range(2 * per_step):
-            src = ck_hbm if k < per_step else cv_hbm
-            at = (group_of(step) * per_step + k % per_step) * depth
-            at = at if isinstance(at, int) else pl.multiple_of(at, depth)
-            copy_in(src.at[pl.ds(at, depth)], ring_slot(step * 2 * per_step + k))
+    def kv_slot(step, value):
+        return (ahead * value + step % ahead) * per_step
+
+    def issue_kv(step, value):
+        src = cv_hbm if value else ck_hbm
+        for i in range(per_step):
+            at = multiple_of((group_of(step) * per_step + i) * depth, depth)
+            copy_in(src.at[pl.ds(at, depth)], kv_slot(step, value) + i)
 
     def q_copy(k):
         return pltpu.make_async_copy(cq_hbm.at[pl.ds(k * WIDE, WIDE)], pw.at[k], p_sem.at[k])
@@ -358,7 +372,7 @@
 
     def blocks(at, n, fn):
         def body(i, carry):
-            fn(pl.multiple_of(at + i * 16, 16))
+            fn(multiple_of(at + i * 16, 16))
             return carry
         lax.fori_loop(0, n // 16, body, 0)
 
@@ -424,7 +438,8 @@
     for k in range(n_sq):
         q_copy(k).start()
     for step in range(ahead):
-        issue_step(step)
+        issue_kv(step, 0)
+        issue_kv(step, 1)
     for i in range(n_sq):
         o_copy(i).start()
     for i in range(2 * g_cut):
@@ -450,7 +465,7 @@
                 q_copy(k).wait()
 
         def block(n, carry):
-            here = pl.ds(pl.multiple_of(n * COLS, COLS), COLS)
+            here = pl.ds(multiple_of(n * COLS, COLS), COLS)
             y = None
             for k in range(n_sq):
                 z = jnp.dot(both_cores(hbuf, h, slice(k * WIDE, (k + 1) * WIDE)), pw[k, :, here], preferred_element_type=F32)
@@ -459,51 +474,83 @@
             q_ref[h * part:(h + 1) * part, here] = y[0:part]
             q_ref[half + h * part:half + (h + 1) * part, here] = y[part:]
             return carry
-        lax.fori_loop(0, inner // COLS, block, 0)
+        twice(inner // COLS, block)
 
     own_head = (lax.broadcasted_iota(jnp.int32, (n_head, inner), 1) // (inner // n_head)
                 == lax.broadcasted_iota(jnp.int32, (n_head, inner), 0))
     in_slot = GROUP // per_step
 
-    def attend_step(step, carry):
-        at = pl.ds(pl.multiple_of(group_of(step) * GROUP, GROUP), GROUP)
-        ka, kb, va, vb = [ring_slot(step * 2 * per_step + k) for k in range(4)]
-        q8 = q_ref[at, :]
-        m8 = mask_ref[at, :]
+    def rows_of(slot, r):
+        here = pl.ds(r * inner, inner)
+        return jnp.concatenate([ring[slot, here, :], ring[slot + 1, here, :]], axis=1)
+
+    def group_rows(step):
+        return pl.ds(multiple_of(group_of(step) * GROUP, GROUP), GROUP)
+
+    def score_dots(step):
+        q8 = q_ref[group_rows(step), :]
 
         def spread(r):
             return jnp.where(own_head, jnp.broadcast_to(q8[r:r + 1, :], (n_head, inner)), 0.0).astype(BF16)
-
-        def rows_of(a, b, r):
-            here = pl.ds(r * inner, inner)
-            return jnp.concatenate([ring[a, here, :], ring[b, here, :]], axis=1)
-        landed(ka)
-        landed(kb)
-        scores = [None] * GROUP
-        for r in range(in_slot):
-            s = jnp.dot(jnp.concatenate([spread(r), spread(r + in_slot)], axis=0), rows_of(ka, kb, r), preferred_element_type=F32)
-            scores[r] = jnp.where(m8[r:r + 1, :] != 0, s[0:n_head, 0:LANES], NEG_FILL)
-            scores[r + in_slot] = jnp.where(m8[r + in_slot:r + in_slot + 1, :] != 0, s[n_head:, LANES:], NEG_FILL)
-        s = jnp.concatenate(scores, axis=0)
+        return [jnp.dot(jnp.concatenate([spread(r), spread(r + in_slot)], axis=0), rows_of(kv_slot(step, 0), r),
+                        preferred_element_type=F32) for r in range(in_slot)]
+
+    def probabilities(step, dots):
+        m8 = mask_ref[group_rows(step), :]
+        scores = [s[0:n_head, 0:LANES] for s in dots] + [s[n_head:, LANES:] for s in dots]
+        s = jnp.concatenate([jnp.where(m8[r:r + 1, :] != 0, scores[r], NEG_FILL) for r in range(GROUP)], axis=0)
         e = jnp.exp(s - jnp.max(s, axis=1, keepdims=True))
-        p = (e / jnp.sum(e, axis=1, keepdims=True)).astype(BF16)
-        landed(va)
-        landed(vb)
+        p_ref[...] = (e / jnp.sum(e, axis=1, keepdims=True)).astype(BF16)
+
+    def value_dots(step, p):
         none = jnp.zeros((n_head, LANES), BF16)
-        mixed = [None] * GROUP
+        out = []
         for r in range(in_slot):
             pa = p[r * n_head:(r + 1) * n_head, :]
             pb = p[(r + in_slot) * n_head:(r + in_slot + 1) * n_head, :]
             lhs = jnp.concatenate([jnp.concatenate([pa, none], axis=1), jnp.concatenate([none, pb], axis=1)], axis=0)
-            y = lax.dot_general(lhs, rows_of(va, vb, r), (((1,), (1,)), ((), ())), preferred_element_type=F32)
-            mixed[r] = jnp.sum(jnp.where(own_head, y[0:n_head], 0.0), axis=0, keepdims=True)
-            mixed[r + in_slot] = jnp.sum(jnp.where(own_head, y[n_head:], 0.0), axis=0, keepdims=True)
-        mix_ref[at, :] = jnp.concatenate(mixed, axis=0)
-
-        @pl.when(step + ahead < n_step)
+            out.append(lax.dot_general(lhs, rows_of(kv_slot(step, 1), r), (((1,), (1,)), ((), ())), preferred_element_type=F32))
+        return out
+
+    def store_mixed(step, dots):
+        mixed = [y[0:n_head] for y in dots] + [y[n_head:] for y in dots]
+        mix_ref[group_rows(step), :] = jnp.concatenate(
+            [jnp.sum(jnp.where(own_head, y, 0.0), axis=0, keepdims=True) for y in mixed], axis=0)
+
+    def wait_kv(step, value):
+        for i in range(per_step):
+            landed(kv_slot(step, value) + i)
+
+    def refill(step, value):
+        if isinstance(step, int):
+            if step < n_step:
+                issue_kv(step, value)
+            return
+
+        @pl.when(step < n_step)
         def _():
-            issue_step(step + ahead)
-        return carry
+            issue_kv(step, value)
+
+    def attend(lo, hi):
+        wait_kv(lo, 0)
+        probabilities(lo, score_dots(lo))
+        refill(lo + ahead, 0)
+
+        def body(step, carry):
+            wait_kv(step + 1, 0)
+            wait_kv(step, 1)
+            p = p_ref[...]
+            dots = score_dots(step + 1)
+            values = value_dots(step, p)
+            probabilities(step + 1, dots)
+            store_mixed(step, values)
+            refill(step + 1 + ahead, 0)
+            refill(step + ahead, 1)
+            return carry
+        lax.fori_loop(lo, hi - 1, body, 0)
+        wait_kv(hi - 1, 1)
+        store_mixed(hi - 1, value_dots(hi - 1, p_ref[...]))
+        refill(hi - 1 + ahead, 1)
 
     def project_o(h, after):
         lhs = both_cores(mix_ref, h).astype(BF16)
@@ -526,7 +573,7 @@
     normalise(0, 0)
     all_rows(0, 0)
     project_q(0)
-    lax.fori_loop(0, n_step // 2, attend_step, 0)
+    attend(0, n_step // 2)
     sent(0, 0, 0, part)
     project_o(0, False)
     for j in pieces:
@@ -536,7 +583,7 @@
         chip_sum(1, 0, j, 0, part)
     all_rows(0, 1)
     project_q(1)
-    lax.fori_loop(n_step // 2, n_step, attend_step, 0)
+    attend(n_step // 2, n_step)
     for pair in range(1, n_pair):
         for i in range(2 * g_cut):
             gu_tall(pair, i).start()
@@ -576,22 +623,22 @@
         base = (pair % n_pair) * 2 * g_cut
 
         def block(n, carry):
-            here = pl.ds(pl.multiple_of(n * COLS, COLS), COLS)
-            mlp_block(pl.multiple_of(WIDE + pair * g_cols + n * COLS, COLS), [gw[base + i, :, here] for i in range(g_cut)],
+            here = pl.ds(multiple_of(n * COLS, COLS), COLS)
+            mlp_block(multiple_of(WIDE + pair * g_cols + n * COLS, COLS), [gw[base + i, :, here] for i in range(g_cut)],
                       [gw[base + g_cut + i, :, here] for i in range(g_cut)])
             return carry
-        lax.fori_loop(0, g_cols // COLS, block, 0)
+        twice(g_cols // COLS, block)
 
     def mlp_square():
         for i in range(2 * n_sq):
             gu_square(i).wait()
 
         def block(n, carry):
-            here = pl.ds(pl.multiple_of(n * COLS, COLS), COLS)
-            mlp_block(pl.multiple_of(n * COLS, COLS), [pw[i, :, here] for i in range(n_sq)],
+            here = pl.ds(multiple_of(n * COLS, COLS), COLS)
+            mlp_block(multiple_of(n * COLS, COLS), [pw[i, :, here] for i in range(n_sq)],
                       [pw[n_sq + i, :, here] for i in range(n_sq)])
             return carry
-        lax.fori_loop(0, WIDE // COLS, block, 0)
+        twice(WIDE // COLS, block)
 
     n_tall = (d_ff - WIDE) // g_cols
     for pair in range(n_pair):
@@ -660,12 +707,12 @@
                 y = None
                 for k in range(d_cut):
                     row, rest = k * WIDE, min(WIDE, d_ff - k * WIDE)
-                    w = pw[(block_c - 2) * d_cut + k, 0:rest, pl.ds(pl.multiple_of(in_block + i * COLS, COLS), COLS)]
+                    w = pw[(block_c - 2) * d_cut + k, 0:rest, pl.ds(multiple_of(in_block + i * COLS, COLS), COLS)]
                     z = jnp.dot(act[:, row:row + rest], w, preferred_element_type=F32)
                     y = z if y is None else y + z
-            pbuf[:, pl.ds(pl.multiple_of(n * COLS, COLS), COLS)] = y.astype(BF16)
+            pbuf[:, pl.ds(multiple_of(n * COLS, COLS), COLS)] = y.astype(BF16)
             return carry
-        lax.fori_loop(0, per_piece, down, 0)
+        twice(per_piece, down)
         last_to_partner(c).start()
         if c > 1:
             last_chip_sum(c - 2)
@@ -716,6 +763,7 @@
             pltpu.VMEM((2, half, d_model), BF16),
             pltpu.VMEM((rows, inner), F32),
             pltpu.VMEM((rows, inner), F32),
+            pltpu.VMEM((GROUP * n_head, src_len), BF16),
             pltpu.VMEM((rows, d_ff), BF16),
             pltpu.VMEM((2,) + square, BF16),
             pltpu.VMEM((2, d_model), F32),

time: 119 us -> 114 us (0.958)
  Pallas kernels: 116 us -> 111 us
    pallas_call x1, Pallas kernels: 79.4 us -> 74.9 us  [rest_of_layer(): pl.pallas_call(functools.partial(cross_kernel, n_head), out_shape=jax.Sha...]
where the time goes in v7:
time: 114 us
  Pallas kernels  111 us (97%)
  local copies, waits for them, and re-layouts  2.29 us (2%)
    pallas_call x1, Pallas kernels, rest_of_layer(): pl.pallas_call(functools.partial(cross_kernel, n_head), out_shape=jax.Sha...  74.9 us
    pallas_call x1, Pallas kernels, self_attention(): pl.pallas_call(body, out_shape=(jax.ShapeDtypeStruct((rows, w_o.shape[1])...  35.9 us
    unnamed x1, local copies, waits for them, and re-layouts  2.29 us

profile of v7, /device:TPU:0, one launch (start us, length us, event | category | flops | bytes accessed | tf_op | source)
XLA Modules:
  0.0 113.7 jit_solution(8420760503726135575)
XLA Ops:
  0.6 35.9 %self_part.1 = (bf16[128,4096]{1,0:T(8,128)(2,1)}, bf16[65536,128]{1,0:T(8,128)(2,1)}, bf16[65536,128]{1,0:T(8,128)(2,1)}) custom-call(bf16[128,4096]{1,0:T(8,128)(2,1)} %x_hbm.1, bf16[32,128]{1,0:T(8,128)(2,1)} %bitcast.27, s32[1,128]{1,0:T(1,128)} %bitcast.31, f32[16,32]{1,0:T(8,128)} %bitcast.28, bf16[4096,1024]{1,0:T(8,128)(2,1)} %refs_4_.1, ...), custom_call_target="tpu_custom_call" | custom-call | flops 4400000000 | bytes 104000000 | tf_op jit(solution)/shard_map/self_part/pallas_call | solution.py:234
  36.6 74.9 %rest_part.1 = bf16[128,4096]{1,0:T(8,128)(2,1)} custom-call(bf16[128,4096]{1,0:T(8,128)(2,1)} %x_hbm.1, bf16[128,4096]{1,0:T(8,128)(2,1)} %get-tuple-element.6.part_hbm, bf16[32,128]{1,0:T(8,128)(2,1)} %bitcast.29, bf16[32,128]{1,0:T(8,128)(2,1)} %bitcast.30, s32[128,128]{1,0:T(8,128)} %mask_hbm.1, bf16[4096,1024]{1,0:T(8,128)(2,1)} %cq_hbm.1, ...), custom_call_target="tpu_custom_call" | custom-call | tf_op jit(solution)/shard_map/rest_part/pallas_call | solution.py:748
  111.4 2.3 %copy.24 = bf16[128,4096]{1,0:T(8,128)(2,1)} copy(bf16[128,4096]{1,0:T(8,128)(2,1)} %rest_part.1) | data formatting | bytes 2097152

commit v8 on v7

--- a/solution.py
+++ b/solution.py
@@ -38,8 +38,8 @@
         dst[at:at + 1, i * 128:(i + 1) * 128] = values[i:i + 1, :]
 
 
-def self_kernel(x_hbm, norm_hbm, pos_hbm, rel_hbm, wq_hbm, wk_hbm, wv_hbm, wo_hbm, k_hbm, v_hbm,
-                part_hbm, newk_hbm, newv_hbm,
+def self_kernel(x_hbm, norm_hbm, pos_hbm, rel_hbm, wq_hbm, wk_hbm, wv_hbm, k_hbm, v_hbm,
+                mixed_hbm, newk_hbm, newv_hbm,
                 xbuf, hbuf, wbuf, kvbuf, sum_ref, q_ref, kn_ref, hit_ref, score_ref, acc_ref,
                 norm_ref, nrow, pos_ref, rel_ref,
                 x_sem, small_sem, w_sem, kv_sem, out_sem, part_sem, window):
@@ -53,7 +53,6 @@
     chunk_rows = kvbuf.shape[1]
     sub = d_head // 16
     k_rows = wbuf.shape[1]
-    n_wo = wo_hbm.shape[1] // inner
 
     def w_copy(c):
         src = (wq_hbm, wk_hbm, wv_hbm)[c // per_mat]
@@ -63,10 +62,7 @@
         src = k_hbm if i < n_chunk else v_hbm
         return pltpu.make_async_copy(src.at[pl.ds((i % n_chunk) * chunk_rows, chunk_rows)], kvbuf.at[i], kv_sem.at[i])
 
-    def wo_copies(i):
-        return [pltpu.make_async_copy(wo_hbm.at[:, pl.ds(i * inner, inner)], wbuf.at[i], w_sem.at[i])]
-
-    loads = [[w_copy(c)] for c in range(n_w)] + [[kv_copy(i)] for i in range(2 * n_chunk)] + [wo_copies(i) for i in range(n_wo)]
+    loads = [[w_copy(c)] for c in range(n_w)] + [[kv_copy(i)] for i in range(2 * n_chunk)]
     issued = [0]
 
     def issue(upto):
@@ -199,25 +195,14 @@
 
     issue(len(loads))
     hbuf[:, 0:inner] = acc_ref[...].T.astype(BF16)
-    part_copies = []
-    for i in range(n_wo):
-        for copy in wo_copies(i):
-            copy.wait()
-        for r in range(inner // COLS):
-            at = i * inner + r * COLS
-            y = jnp.dot(hbuf[:, 0:inner], wbuf[i, :, r * COLS:(r + 1) * COLS], preferred_element_type=F32)
-            xbuf[:, at:at + COLS] = y.astype(BF16)
-        here = pl.ds(i * inner, inner)
-        copy = pltpu.make_async_copy(xbuf.at[:, here], part_hbm.at[:, here], part_sem.at[i])
-        copy.start()
-        part_copies.append(copy)
+    mixed_copy = pltpu.make_async_copy(hbuf.at[:, pl.ds(0, inner)], mixed_hbm, part_sem)
+    mixed_copy.start()
     for i in range(2 * n_chunk):
         chunk_out(i).wait()
-    for copy in part_copies:
-        copy.wait()
-
-
-def self_attention(x_in, norm_self, tok_pos, rel_bias, w_q, w_k, w_v, w_o, self_k, self_v):
+    mixed_copy.wait()
+
+
+def self_attention(x_in, norm_self, tok_pos, rel_bias, w_q, w_k, w_v, self_k, self_v):
     rows, t_len, n_head, d_head = self_k.shape
     d_model = x_in.shape[1]
     inner = n_head * d_head
@@ -226,16 +211,15 @@
     v_flat = self_v.transpose(1, 2, 3, 0).reshape(flat)
     n_w = 3 * (d_model // inner)
     n_chunk = t_len // T_BLOCK
-    n_wo = w_o.shape[1] // inner
 
     def body(*refs):
         self_kernel(*refs, window=8)
 
-    part, new_k, new_v = pl.pallas_call(
+    mixed, new_k, new_v = pl.pallas_call(
         body,
-        out_shape=(jax.ShapeDtypeStruct((rows, w_o.shape[1]), BF16),
+        out_shape=(jax.ShapeDtypeStruct((rows, inner), BF16),
                    jax.ShapeDtypeStruct(flat, BF16), jax.ShapeDtypeStruct(flat, BF16)),
-        in_specs=[ANY] * 10,
+        in_specs=[ANY] * 9,
         out_specs=(ANY, ANY, ANY),
         scratch_shapes=[
             pltpu.VMEM((rows, d_model), BF16),
@@ -257,16 +241,16 @@
             pltpu.SemaphoreType.DMA((n_w,)),
             pltpu.SemaphoreType.DMA((2 * n_chunk,)),
             pltpu.SemaphoreType.DMA((2 * n_chunk,)),
-            pltpu.SemaphoreType.DMA((n_wo,)),
+            pltpu.SemaphoreType.DMA,
         ],
         compiler_params=pltpu.CompilerParams(vmem_limit_bytes=66_900_000),
-        cost_estimate=pl.CostEstimate(flops=4_400_000_000, bytes_accessed=104_000_000, transcendentals=131_072),
+        cost_estimate=pl.CostEstimate(flops=3_300_000_000, bytes_accessed=95_000_000, transcendentals=131_072),
         name="self_part",
-    )(x_in, norm_self.reshape(d_model // 128, 128), tok_pos.reshape(1, rows), rel_bias.T, w_q, w_k, w_v, w_o, k_flat, v_flat)
+    )(x_in, norm_self.reshape(d_model // 128, 128), tok_pos.reshape(1, rows), rel_bias.T, w_q, w_k, w_v, k_flat, v_flat)
 
     def unflat(cache):
         return cache.reshape(t_len, n_head, d_head, rows).transpose(3, 0, 1, 2)
-    return part, unflat(new_k), unflat(new_v)
+    return mixed, unflat(new_k), unflat(new_v)
 
 
 RING = 20
@@ -276,9 +260,9 @@
 LANES = 128
 
 
-def cross_kernel(n_head, x_hbm, part_hbm, ncross_hbm, nmlp_hbm, mask_hbm, cq_hbm, ck_hbm, cv_hbm, co_hbm, wg_hbm, wu_hbm, wd_hbm,
+def cross_kernel(n_head, x_hbm, mixed_hbm, wo_hbm, ncross_hbm, nmlp_hbm, mask_hbm, cq_hbm, ck_hbm, cv_hbm, co_hbm, wg_hbm, wu_hbm, wd_hbm,
                  out_hbm,
-                 ring, pw, gw, pbuf, hbuf, res, xhalf, rx1, tx2, rx2, q_ref, mix_ref, p_ref, act, norm_in, nrow, mask_ref,
+                 ring, pw, gw, mixbf, pbuf, hbuf, res, xhalf, rx1, tx2, rx2, q_ref, mix_ref, p_ref, act, norm_in, nrow, mask_ref,
                  ring_sem, p_sem, g_sem, load_sem, small_sem, s1_send, s1_recv, s2_send, s2_recv, s3_send, s3_recv, out_sem):
     rows, d_model = hbuf.shape
     half = rows // 2
@@ -418,9 +402,16 @@
 
     pieces = range(AR_CHUNKS)
     halves = range(2)
-    first = [pltpu.make_async_copy(part_hbm.at[:, piece(j)], pbuf.at[:, piece(j)], load_sem.at[j]) for j in pieces]
-    for copy in first:
-        copy.start()
+    n_wo = d_model // g_cols
+    mixed_copy = pltpu.make_async_copy(mixed_hbm, mixbf, load_sem.at[n_wo])
+    mixed_copy.start()
+
+    def wo_copy(i):
+        per_slot = g_rows // inner
+        return pltpu.make_async_copy(wo_hbm.at[:, pl.ds(i * g_cols, g_cols)],
+                                     gw.at[i // per_slot, pl.ds(i % per_slot * inner, inner)], load_sem.at[i])
+    for i in range(n_wo):
+        wo_copy(i).start()
     small = [pltpu.make_async_copy(src, dst, small_sem.at[i]) for i, (src, dst) in enumerate(
         ((x_hbm.at[mine(0, half)], xhalf), (ncross_hbm, norm_in.at[0]), (nmlp_hbm, norm_in.at[1]), (mask_hbm, mask_ref)))]
     for copy in small:
@@ -430,11 +421,6 @@
         pl.semaphore_signal(barrier, inc=1, device_id=other, device_id_type=MESH)
     pl.semaphore_wait(barrier, 2)
 
-    for j in pieces:
-        first[j].wait()
-        to_partner(0, 0, j, 0, part).start()
-    for j in pieces:
-        to_partner(0, 1, j, part, part).start()
     for k in range(n_sq):
         q_copy(k).start()
     for step in range(ahead):
@@ -442,11 +428,26 @@
         issue_kv(step, 1)
     for i in range(n_sq):
         o_copy(i).start()
+    mixed_copy.wait()
+    for i in range(n_wo):
+        wo_copy(i).wait()
+        per_slot = g_rows // inner
+        for n in range(g_cols // COLS):
+            w = gw[i // per_slot, i % per_slot * inner:(i % per_slot + 1) * inner, n * COLS:(n + 1) * COLS]
+            y = jnp.dot(mixbf[...], w, preferred_element_type=F32)
+            pbuf[:, i * g_cols + n * COLS:i * g_cols + (n + 1) * COLS] = y.astype(BF16)
+        if (i + 1) * g_cols % width == 0:
+            j = (i + 1) * g_cols // width - 1
+            to_partner(0, 0, j, 0, part).start()
+            if j > 0:
+                chip_sum(0, 0, j - 1, 0, part)
+    for j in pieces:
+        to_partner(0, 1, j, part, part).start()
     for i in range(2 * g_cut):
         gu_tall(0, i).start()
-    for h in halves:
-        for j in pieces:
-            chip_sum(0, h, j, h * part, part)
+    chip_sum(0, 0, AR_CHUNKS - 1, 0, part)
+    for j in pieces:
+        chip_sum(0, 1, j, part, part)
     for copy in small:
         copy.wait()
     lay_row(nrow, 0, norm_in.at[0])
@@ -531,7 +532,7 @@
         def _():
             issue_kv(step, value)
 
-    def attend(lo, hi):
+    def attend(lo, hi, at=None, hook=None):
         wait_kv(lo, 0)
         probabilities(lo, score_dots(lo))
         refill(lo + ahead, 0)
@@ -544,6 +545,8 @@
             values = value_dots(step, p)
             probabilities(step + 1, dots)
             store_mixed(step, values)
+            if hook is not None:
+                pl.when(step == at)(hook)
             refill(step + 1 + ahead, 0)
             refill(step + ahead, 1)
             return carry
@@ -573,16 +576,18 @@
     normalise(0, 0)
     all_rows(0, 0)
     project_q(0)
-    attend(0, n_step // 2)
+
+    def second_half():
+        for j in pieces:
+            full_sum(0, 1, j, part, part)
+        normalise(0, 1)
+    attend(0, n_step // 2, n_step // 2 - 3, second_half)
     sent(0, 0, 0, part)
     project_o(0, False)
-    for j in pieces:
-        full_sum(0, 1, j, part, part)
-    normalise(0, 1)
+    all_rows(0, 1)
+    project_q(1)
     for j in pieces:
         chip_sum(1, 0, j, 0, part)
-    all_rows(0, 1)
-    project_q(1)
     attend(n_step // 2, n_step)
     for pair in range(1, n_pair):
         for i in range(2 * g_cut):
@@ -735,7 +740,7 @@
         last_own(j).wait()
 
 
-def rest_of_layer(x_in, part, norm_cross, norm_mlp, enc_mask, cross_k, cross_v, cross_q, cross_o, w_gate, w_up, w_down):
+def rest_of_layer(x_in, mixed, w_o, norm_cross, norm_mlp, enc_mask, cross_k, cross_v, cross_q, cross_o, w_gate, w_up, w_down):
     rows, d_model = x_in.shape
     _, src_len, n_head, d_head = cross_k.shape
     inner = n_head * d_head
@@ -748,12 +753,13 @@
     return pl.pallas_call(
         functools.partial(cross_kernel, n_head),
         out_shape=jax.ShapeDtypeStruct((rows, d_model), BF16),
-        in_specs=[ANY] * 12,
+        in_specs=[ANY] * 13,
         out_specs=ANY,
         scratch_shapes=[
             pltpu.VMEM((RING, d_model, LANES), BF16),
             pltpu.VMEM((8, WIDE, WIDE), BF16),
             pltpu.VMEM((8, d_model // 2, 512), BF16),
+            pltpu.VMEM((rows, inner), BF16),
             pltpu.VMEM((rows, d_model), BF16),
             pltpu.VMEM((rows, d_model), BF16),
             pltpu.VMEM((half, d_model), F32),
@@ -771,7 +777,7 @@
             pltpu.SemaphoreType.DMA((RING,)),
             pltpu.SemaphoreType.DMA((8,)),
             pltpu.SemaphoreType.DMA((8,)),
-            pltpu.SemaphoreType.DMA((AR_CHUNKS,)),
+            pltpu.SemaphoreType.DMA((d_model // 512 + 1,)),
             pltpu.SemaphoreType.DMA((4,)),
             pltpu.SemaphoreType.DMA((2, 2, AR_CHUNKS)),
             pltpu.SemaphoreType.DMA((2, 2, AR_CHUNKS)),
@@ -783,13 +789,13 @@
         ],
         compiler_params=pltpu.CompilerParams(vmem_limit_bytes=67_000_000, collective_id=0, has_side_effects=True),
         name="rest_part",
-    )(x_in, part, norm_cross.reshape(square), norm_mlp.reshape(square), enc_mask, cross_q, k_flat, v_flat, cross_o, w_gate, w_up, w_down)
+    )(x_in, mixed, w_o, norm_cross.reshape(square), norm_mlp.reshape(square), enc_mask, cross_q, k_flat, v_flat, cross_o, w_gate, w_up, w_down)
 
 
 def solution(mesh):
     def local_layer(x_in, tok_pos, self_k, self_v, cross_k, cross_v, enc_mask, rel_bias, w_q, w_k, w_v, w_o, cross_q, cross_o, w_gate, w_up, w_down, norm_self, norm_cross, norm_mlp):
-        part, new_self_k, new_self_v = self_attention(x_in, norm_self, tok_pos, rel_bias, w_q, w_k, w_v, w_o, self_k, self_v)
-        x_out = rest_of_layer(x_in, part, norm_cross, norm_mlp, enc_mask, cross_k, cross_v, cross_q, cross_o, w_gate, w_up, w_down)
+        mixed, new_self_k, new_self_v = self_attention(x_in, norm_self, tok_pos, rel_bias, w_q, w_k, w_v, self_k, self_v)
+        x_out = rest_of_layer(x_in, mixed, w_o, norm_cross, norm_mlp, enc_mask, cross_k, cross_v, cross_q, cross_o, w_gate, w_up, w_down)
         return x_out, new_self_k, new_self_v
 
     cache_spec = P('dp', None, 'tp', None)

time: 114 us -> 111 us (0.974)
  Pallas kernels: 111 us -> 108 us
    pallas_call x1, Pallas kernels: 35.9 us -> 32.4 us  [self_attention(): pl.pallas_call(body, out_shape=(jax.ShapeDtypeStruct((rows, inner), BF16)...]
where the time goes in v8:
time: 111 us; the launch traced here: 110 us
  Pallas kernels  108 us (97%)
  local copies, waits for them, and re-layouts  2.29 us (2%)
    pallas_call x1, Pallas kernels, rest_of_layer(): pl.pallas_call(functools.partial(cross_kernel, n_head), out_shape=jax.Sha...  75.1 us
    pallas_call x1, Pallas kernels, self_attention(): pl.pallas_call(body, out_shape=(jax.ShapeDtypeStruct((rows, inner), BF16)...  32.4 us
    unnamed x1, local copies, waits for them, and re-layouts  2.29 us

profile of v8, /device:TPU:0, one launch (start us, length us, event | category | flops | bytes accessed | tf_op | source)
XLA Modules:
  0.0 110.4 jit_solution(8834281400532693606)
XLA Ops:
  0.6 32.4 %self_part.1 = (bf16[128,1024]{1,0:T(8,128)(2,1)}, bf16[65536,128]{1,0:T(8,128)(2,1)}, bf16[65536,128]{1,0:T(8,128)(2,1)}) custom-call(bf16[128,4096]{1,0:T(8,128)(2,1)} %x_hbm.1, bf16[32,128]{1,0:T(8,128)(2,1)} %bitcast.27, s32[1,128]{1,0:T(1,128)} %bitcast.31, f32[16,32]{1,0:T(8,128)} %bitcast.28, bf16[4096,1024]{1,0:T(8,128)(2,1)} %refs_4_.1, ...), custom_call_target="tpu_custom_call" | custom-call | flops 3300000000 | bytes 95000000 | tf_op jit(solution)/shard_map/self_part/pallas_call | solution.py:218
  33.0 75.1 %rest_part.1 = bf16[128,4096]{1,0:T(8,128)(2,1)} custom-call(bf16[128,4096]{1,0:T(8,128)(2,1)} %x_hbm.1, bf16[128,1024]{1,0:T(8,128)(2,1)} %get-tuple-element.6.mixed_hbm, bf16[1024,4096]{1,0:T(8,128)(2,1)} %wo_hbm.1, bf16[32,128]{1,0:T(8,128)(2,1)} %bitcast.29, bf16[32,128]{1,0:T(8,128)(2,1)} %bitcast.30, s32[128,128]{1,0:T(8,128)} %mask_hbm.1, ...), custom_call_target="tpu_custom_call" | custom-call | tf_op jit(solution)/shard_map/rest_part/pallas_call | solution.py:753
  108.2 2.3 %copy.24 = bf16[128,4096]{1,0:T(8,128)(2,1)} copy(bf16[128,4096]{1,0:T(8,128)(2,1)} %rest_part.1) | data formatting | bytes 2097152

commit v9 on v8

--- a/solution.py
+++ b/solution.py
@@ -213,7 +213,7 @@
     n_chunk = t_len // T_BLOCK
 
     def body(*refs):
-        self_kernel(*refs, window=8)
+        self_kernel(*refs, window=5)
 
     mixed, new_k, new_v = pl.pallas_call(
         body,
@@ -267,6 +267,7 @@
     rows, d_model = hbuf.shape
     half = rows // 2
     part = half // 2
+    quarter = part // 2
     depth = ring.shape[1]
     inner = q_ref.shape[1]
     d_ff = act.shape[1]
@@ -304,8 +305,9 @@
         pltpu.make_async_copy(ck_hbm.at[pl.ds(0, used)], ring.at[slot, pl.ds(0, used)], ring_sem.at[slot]).wait()
 
     def group_of(step):
-        per_half, u = n_step // 2, step % (n_step // 2)
-        return (step // per_half) * (part // GROUP) + u + (u // (part // GROUP)) * (part // GROUP)
+        per_quarter = quarter // GROUP
+        w = step % (2 * per_quarter)
+        return step // (2 * per_quarter) * per_quarter + w // per_quarter * (half // GROUP) + w % per_quarter
 
     def kv_slot(step, value):
         return (ahead * value + step % ahead) * per_step
@@ -382,23 +384,23 @@
             to_partner(a, h, j, at, n).wait_send()
             to_across(a, h, j, at, n).wait_send()
 
-    def rows_back(a, h, i):
-        at = mine(h * part + i * 16, 16)
+    def rows_back(a, h, i, at):
+        at = mine(at + i * 16, 16)
         return pltpu.make_async_remote_copy(
             src_ref=hbuf.at[at], dst_ref=hbuf.at[at], send_sem=s3_send.at[a % 2, h, i],
             recv_sem=s3_recv.at[a % 2, h, i], device_id=partner, device_id_type=MESH)
 
-    def normalise(a, h):
+    def normalise(a, h, at, n):
         norm = nrow[a:a + 1, :]
-        for i in range(part // 16):
-            r = res[h * part + i * 16:h * part + (i + 1) * 16, :]
+        for i in range(n // 16):
+            r = res[at + i * 16:at + (i + 1) * 16, :]
             inv = lax.rsqrt(jnp.mean(r * r, axis=-1, keepdims=True) + 1e-6)
-            hbuf[mine(h * part + i * 16, 16), :] = (r * inv * norm).astype(BF16)
-            rows_back(a, h, i).start()
-
-    def all_rows(a, h):
-        for i in range(part // 16):
-            rows_back(a, h, i).wait()
+            hbuf[mine(at + i * 16, 16), :] = (r * inv * norm).astype(BF16)
+            rows_back(a, h, i, at).start()
+
+    def all_rows(a, h, at, n):
+        for i in range(n // 16):
+            rows_back(a, h, i, at).wait()
 
     pieces = range(AR_CHUNKS)
     halves = range(2)
@@ -457,8 +459,8 @@
     def beside(a, b, used=depth):
         return jnp.concatenate([ring[a, 0:used, :], ring[b, 0:used, :]], axis=1)
 
-    def both_cores(ref, h, at=slice(None)):
-        return jnp.concatenate([ref[h * part:(h + 1) * part, at], ref[half + h * part:half + (h + 1) * part, at]], axis=0)
+    def both_cores(ref, at, n, here=slice(None)):
+        return jnp.concatenate([ref[at:at + n, here], ref[half + at:half + at + n, here]], axis=0)
 
     def project_q(h):
         if h == 0:
@@ -469,7 +471,7 @@
             here = pl.ds(multiple_of(n * COLS, COLS), COLS)
             y = None
             for k in range(n_sq):
-                z = jnp.dot(both_cores(hbuf, h, slice(k * WIDE, (k + 1) * WIDE)), pw[k, :, here], preferred_element_type=F32)
+                z = jnp.dot(both_cores(hbuf, h * part, part, slice(k * WIDE, (k + 1) * WIDE)), pw[k, :, here], preferred_element_type=F32)
                 y = z if y is None else y + z
             y = y.astype(BF16).astype(F32)
             q_ref[h * part:(h + 1) * part, here] = y[0:part]
@@ -532,7 +534,7 @@
         def _():
             issue_kv(step, value)
 
-    def attend(lo, hi, at=None, hook=None):
+    def attend(lo, hi, hooks):
         wait_kv(lo, 0)
         probabilities(lo, score_dots(lo))
         refill(lo + ahead, 0)
@@ -545,7 +547,7 @@
             values = value_dots(step, p)
             probabilities(step + 1, dots)
             store_mixed(step, values)
-            if hook is not None:
+            for at, hook in hooks.items():
                 pl.when(step == at)(hook)
             refill(step + 1 + ahead, 0)
             refill(step + ahead, 1)
@@ -555,60 +557,62 @@
         store_mixed(hi - 1, value_dots(hi - 1, p_ref[...]))
         refill(hi - 1 + ahead, 1)
 
-    def project_o(h, after):
-        lhs = both_cores(mix_ref, h).astype(BF16)
+    def project_o(h, at, n, after):
+        lhs = both_cores(mix_ref, at, n).astype(BF16)
         for j in pieces:
             if h == 0:
                 o_copy(j).wait()
-            for n in range(WIDE // COLS):
-                y = jnp.dot(lhs, pw[n_sq + j, :, n * COLS:(n + 1) * COLS], preferred_element_type=F32).astype(BF16)
-                here = slice(j * WIDE + n * COLS, j * WIDE + (n + 1) * COLS)
-                pbuf[h * part:(h + 1) * part, here] = y[0:part]
-                pbuf[half + h * part:half + (h + 1) * part, here] = y[part:]
-            to_partner(1, h, j, h * part, part).start()
+            for i in range(WIDE // COLS):
+                y = jnp.dot(lhs, pw[n_sq + j, :, i * COLS:(i + 1) * COLS], preferred_element_type=F32).astype(BF16)
+                here = slice(j * WIDE + i * COLS, j * WIDE + (i + 1) * COLS)
+                pbuf[at:at + n, here] = y[0:n]
+                pbuf[half + at:half + at + n, here] = y[n:]
+            to_partner(1, h, j, at, n).start()
             if after and j > 0:
-                chip_sum(1, h, j - 1, h * part, part)
+                chip_sum(1, h, j - 1, at, n)
         if after:
-            chip_sum(1, h, AR_CHUNKS - 1, h * part, part)
-
-    for j in pieces:
-        full_sum(0, 0, j, 0, part)
-    normalise(0, 0)
-    all_rows(0, 0)
+            chip_sum(1, h, AR_CHUNKS - 1, at, n)
+
+    def finish(a, h, at, n):
+        for j in pieces:
+            full_sum(a, h, j, at, n)
+        normalise(a, h, at, n)
+
+    finish(0, 0, 0, part)
+    all_rows(0, 0, 0, part)
     project_q(0)
-
-    def second_half():
-        for j in pieces:
-            full_sum(0, 1, j, part, part)
-        normalise(0, 1)
-    attend(0, n_step // 2, n_step // 2 - 3, second_half)
+    attend(0, n_step // 2, {n_step // 2 - 3: lambda: finish(0, 1, part, part)})
     sent(0, 0, 0, part)
-    project_o(0, False)
-    all_rows(0, 1)
+    project_o(0, 0, part, False)
+    all_rows(0, 1, part, part)
     project_q(1)
     for j in pieces:
         chip_sum(1, 0, j, 0, part)
-    attend(n_step // 2, n_step)
+
+    def third_quarter():
+        sent(0, 1, part, part)
+        project_o(1, part, quarter, False)
+
+    def third_quarter_sum():
+        for j in pieces:
+            chip_sum(1, 1, j, part, quarter)
+    attend(n_step // 2, n_step, {3 * n_step // 4 - 1: third_quarter, 3 * n_step // 4: third_quarter_sum})
     for pair in range(1, n_pair):
         for i in range(2 * g_cut):
             gu_tall(pair, i).start()
     for i in range(n_sq):
         gu_square(i).start()
-    sent(0, 1, part, part)
-    project_o(1, True)
+    project_o(2, part + quarter, quarter, True)
     for i in range(n_sq):
         gu_square(n_sq + i).start()
     for i in range(d_narrow):
         issue_d(i)
-    for j in pieces:
-        full_sum(1, 0, j, 0, part)
-    normalise(1, 0)
-    for j in pieces:
-        full_sum(1, 1, j, part, part)
-    normalise(1, 1)
-    for h in halves:
-        all_rows(1, h)
-        sent(1, h, h * part, part)
+    shares = ((0, 0, part), (1, part, quarter), (2, part + quarter, quarter))
+    for share in shares:
+        finish(1, *share)
+    for share in shares:
+        all_rows(1, *share)
+        sent(1, *share)
 
     root = math.sqrt(2.0 / math.pi)
     def mlp_block(at, gate, up):
@@ -779,12 +783,12 @@
             pltpu.SemaphoreType.DMA((8,)),
             pltpu.SemaphoreType.DMA((d_model // 512 + 1,)),
             pltpu.SemaphoreType.DMA((4,)),
-            pltpu.SemaphoreType.DMA((2, 2, AR_CHUNKS)),
-            pltpu.SemaphoreType.DMA((2, 2, AR_CHUNKS)),
-            pltpu.SemaphoreType.DMA((2, 2, AR_CHUNKS)),
-            pltpu.SemaphoreType.DMA((2, 2, AR_CHUNKS)),
-            pltpu.SemaphoreType.DMA((2, 2, AR_CHUNKS)),
-            pltpu.SemaphoreType.DMA((2, 2, AR_CHUNKS)),
+            pltpu.SemaphoreType.DMA((2, 3, AR_CHUNKS)),
+            pltpu.SemaphoreType.DMA((2, 3, AR_CHUNKS)),
+            pltpu.SemaphoreType.DMA((2, 3, AR_CHUNKS)),
+            pltpu.SemaphoreType.DMA((2, 3, AR_CHUNKS)),
+            pltpu.SemaphoreType.DMA((2, 3, AR_CHUNKS)),
+            pltpu.SemaphoreType.DMA((2, 3, AR_CHUNKS)),
             pltpu.SemaphoreType.DMA((2 * AR_CHUNKS,)),
         ],
         compiler_params=pltpu.CompilerParams(vmem_limit_bytes=67_000_000, collective_id=0, has_side_effects=True),

time: 111 us -> 110 us (level)
  no operation moved by 1% of the time
where the time goes in v9:
time: 110 us
  Pallas kernels  107 us (97%)
  local copies, waits for them, and re-layouts  2.29 us (2%)
    pallas_call x1, Pallas kernels, rest_of_layer(): pl.pallas_call(functools.partial(cross_kernel, n_head), out_shape=jax.Sha...  75.2 us
    pallas_call x1, Pallas kernels, self_attention(): pl.pallas_call(body, out_shape=(jax.ShapeDtypeStruct((rows, inner), BF16)...  31.8 us
    unnamed x1, local copies, waits for them, and re-layouts  2.29 us

profile of v9, /device:TPU:0, one launch (start us, length us, event | category | flops | bytes accessed | tf_op | source)
XLA Modules:
  0.0 110.0 jit_solution(13241358434795508778)
XLA Ops:
  0.6 31.8 %self_part.1 = (bf16[128,1024]{1,0:T(8,128)(2,1)}, bf16[65536,128]{1,0:T(8,128)(2,1)}, bf16[65536,128]{1,0:T(8,128)(2,1)}) custom-call(bf16[128,4096]{1,0:T(8,128)(2,1)} %x_hbm.1, bf16[32,128]{1,0:T(8,128)(2,1)} %bitcast.27, s32[1,128]{1,0:T(1,128)} %bitcast.31, f32[16,32]{1,0:T(8,128)} %bitcast.28, bf16[4096,1024]{1,0:T(8,128)(2,1)} %refs_4_.1, ...), custom_call_target="tpu_custom_call" | custom-call | flops 3300000000 | bytes 95000000 | tf_op jit(solution)/shard_map/self_part/pallas_call | solution.py:218
  32.5 75.2 %rest_part.1 = bf16[128,4096]{1,0:T(8,128)(2,1)} custom-call(bf16[128,4096]{1,0:T(8,128)(2,1)} %x_hbm.1, bf16[128,1024]{1,0:T(8,128)(2,1)} %get-tuple-element.6.mixed_hbm, bf16[1024,4096]{1,0:T(8,128)(2,1)} %wo_hbm.1, bf16[32,128]{1,0:T(8,128)(2,1)} %bitcast.29, bf16[32,128]{1,0:T(8,128)(2,1)} %bitcast.30, s32[128,128]{1,0:T(8,128)} %mask_hbm.1, ...), custom_call_target="tpu_custom_call" | custom-call | tf_op jit(solution)/shard_map/rest_part/pallas_call | solution.py:757
  107.7 2.3 %copy.24 = bf16[128,4096]{1,0:T(8,128)(2,1)} copy(bf16[128,4096]{1,0:T(8,128)(2,1)} %rest_part.1) | data formatting | bytes 2097152

commit v10 on v8

--- a/solution.py
+++ b/solution.py
@@ -213,7 +213,7 @@
     n_chunk = t_len // T_BLOCK
 
     def body(*refs):
-        self_kernel(*refs, window=8)
+        self_kernel(*refs, window=4)
 
     mixed, new_k, new_v = pl.pallas_call(
         body,
@@ -443,8 +443,6 @@
                 chip_sum(0, 0, j - 1, 0, part)
     for j in pieces:
         to_partner(0, 1, j, part, part).start()
-    for i in range(2 * g_cut):
-        gu_tall(0, i).start()
     chip_sum(0, 0, AR_CHUNKS - 1, 0, part)
     for j in pieces:
         chip_sum(0, 1, j, part, part)
@@ -589,7 +587,7 @@
     for j in pieces:
         chip_sum(1, 0, j, 0, part)
     attend(n_step // 2, n_step)
-    for pair in range(1, n_pair):
+    for pair in range(n_pair):
         for i in range(2 * g_cut):
             gu_tall(pair, i).start()
     for i in range(n_sq):

time: 111 us -> 112 us (level)
    pallas_call x1, Pallas kernels: 32.4 us -> 33.6 us  [self_attention(): pl.pallas_call(body, out_shape=(jax.ShapeDtypeStruct((rows, inner), BF16)...]
where the time goes in v10:
time: 112 us
  Pallas kernels  109 us (97%)
  local copies, waits for them, and re-layouts  2.29 us (2%)
    pallas_call x1, Pallas kernels, rest_of_layer(): pl.pallas_call(functools.partial(cross_kernel, n_head), out_shape=jax.Sha...  75.2 us
    pallas_call x1, Pallas kernels, self_attention(): pl.pallas_call(body, out_shape=(jax.ShapeDtypeStruct((rows, inner), BF16)...  33.6 us
    unnamed x1, local copies, waits for them, and re-layouts  2.29 us

profile of v10, /device:TPU:0, one launch (start us, length us, event | category | flops | bytes accessed | tf_op | source)
XLA Modules:
  0.0 111.7 jit_solution(212642177881029746)
XLA Ops:
  0.6 33.6 %self_part.1 = (bf16[128,1024]{1,0:T(8,128)(2,1)}, bf16[65536,128]{1,0:T(8,128)(2,1)}, bf16[65536,128]{1,0:T(8,128)(2,1)}) custom-call(bf16[128,4096]{1,0:T(8,128)(2,1)} %x_hbm.1, bf16[32,128]{1,0:T(8,128)(2,1)} %bitcast.27, s32[1,128]{1,0:T(1,128)} %bitcast.31, f32[16,32]{1,0:T(8,128)} %bitcast.28, bf16[4096,1024]{1,0:T(8,128)(2,1)} %refs_4_.1, ...), custom_call_target="tpu_custom_call" | custom-call | flops 3300000000 | bytes 95000000 | tf_op jit(solution)/shard_map/self_part/pallas_call | solution.py:218
  34.2 75.2 %rest_part.1 = bf16[128,4096]{1,0:T(8,128)(2,1)} custom-call(bf16[128,4096]{1,0:T(8,128)(2,1)} %x_hbm.1, bf16[128,1024]{1,0:T(8,128)(2,1)} %get-tuple-element.6.mixed_hbm, bf16[1024,4096]{1,0:T(8,128)(2,1)} %wo_hbm.1, bf16[32,128]{1,0:T(8,128)(2,1)} %bitcast.29, bf16[32,128]{1,0:T(8,128)(2,1)} %bitcast.30, s32[128,128]{1,0:T(8,128)} %mask_hbm.1, ...), custom_call_target="tpu_custom_call" | custom-call | tf_op jit(solution)/shard_map/rest_part/pallas_call | solution.py:751
  109.4 2.3 %copy.24 = bf16[128,4096]{1,0:T(8,128)(2,1)} copy(bf16[128,4096]{1,0:T(8,128)(2,1)} %rest_part.1) | data formatting | bytes 2097152

commit v11 on v8

--- a/solution.py
+++ b/solution.py
@@ -213,7 +213,7 @@
     n_chunk = t_len // T_BLOCK
 
     def body(*refs):
-        self_kernel(*refs, window=8)
+        self_kernel(*refs, window=5)
 
     mixed, new_k, new_v = pl.pallas_call(
         body,
@@ -588,12 +588,14 @@
     project_q(1)
     for j in pieces:
         chip_sum(1, 0, j, 0, part)
-    attend(n_step // 2, n_step)
-    for pair in range(1, n_pair):
-        for i in range(2 * g_cut):
-            gu_tall(pair, i).start()
-    for i in range(n_sq):
-        gu_square(i).start()
+
+    def start_mlp():
+        for pair in range(1, n_pair):
+            for i in range(2 * g_cut):
+                gu_tall(pair, i).start()
+        for i in range(n_sq):
+            gu_square(i).start()
+    attend(n_step // 2, n_step, n_step - ahead, start_mlp)
     sent(0, 1, part, part)
     project_o(1, True)
     for i in range(n_sq):

time: 111 us -> 110 us (level)
  no operation moved by 1% of the time
where the time goes in v11:
time: 110 us
  Pallas kernels  107 us (97%)
  local copies, waits for them, and re-layouts  2.29 us (2%)
    pallas_call x1, Pallas kernels, rest_of_layer(): pl.pallas_call(functools.partial(cross_kernel, n_head), out_shape=jax.Sha...  75.1 us
    pallas_call x1, Pallas kernels, self_attention(): pl.pallas_call(body, out_shape=(jax.ShapeDtypeStruct((rows, inner), BF16)...  31.8 us
    unnamed x1, local copies, waits for them, and re-layouts  2.29 us

profile of v11, /device:TPU:0, one launch (start us, length us, event | category | flops | bytes accessed | tf_op | source)
XLA Modules:
  0.0 109.9 jit_solution(619850484309113485)
XLA Ops:
  0.6 31.8 %self_part.1 = (bf16[128,1024]{1,0:T(8,128)(2,1)}, bf16[65536,128]{1,0:T(8,128)(2,1)}, bf16[65536,128]{1,0:T(8,128)(2,1)}) custom-call(bf16[128,4096]{1,0:T(8,128)(2,1)} %x_hbm.1, bf16[32,128]{1,0:T(8,128)(2,1)} %bitcast.27, s32[1,128]{1,0:T(1,128)} %bitcast.31, f32[16,32]{1,0:T(8,128)} %bitcast.28, bf16[4096,1024]{1,0:T(8,128)(2,1)} %refs_4_.1, ...), custom_call_target="tpu_custom_call" | custom-call | flops 3300000000 | bytes 95000000 | tf_op jit(solution)/shard_map/self_part/pallas_call | solution.py:218
  32.5 75.1 %rest_part.1 = bf16[128,4096]{1,0:T(8,128)(2,1)} custom-call(bf16[128,4096]{1,0:T(8,128)(2,1)} %x_hbm.1, bf16[128,1024]{1,0:T(8,128)(2,1)} %get-tuple-element.6.mixed_hbm, bf16[1024,4096]{1,0:T(8,128)(2,1)} %wo_hbm.1, bf16[32,128]{1,0:T(8,128)(2,1)} %bitcast.29, bf16[32,128]{1,0:T(8,128)(2,1)} %bitcast.30, s32[128,128]{1,0:T(8,128)} %mask_hbm.1, ...), custom_call_target="tpu_custom_call" | custom-call | tf_op jit(solution)/shard_map/rest_part/pallas_call | solution.py:755
  107.6 2.3 %copy.24 = bf16[128,4096]{1,0:T(8,128)(2,1)} copy(bf16[128,4096]{1,0:T(8,128)(2,1)} %rest_part.1) | data formatting | bytes 2097152
